TPU v7x, 32 devices: a whole 2x2x4 slice. The times are simulated.
32 devices in a mesh: ia: 4 (over y, x), ja: 4 (over z), ka: 2 (over core).
Axes of the slice: x: 2, y: 2, z: 4, core: 2. Of those that a mesh axis runs over, the one named last changes fastest.
Arguments:
- tensor: bfloat16 [1024, 512, 256], P('ia', 'ja', 'ka'), may hold values from -6 to 6
- factor_b: bfloat16 [512, 256], P('ja', 'ka'), may hold values from -16 to 16
- factor_c: bfloat16 [256, 256], P('ka', 'ja'), may hold values from -16 to 16
Outputs:
- factor_a: float32 [1024, 256], P(('ia', 'ja', 'ka'))
All inputs are finite; a program needn't handle non-finite values.
Results may differ from a plain program's by a relative error of at most 0.0003.
Values may be sent and summed in bfloat16 or wider, within the bound.
No kernel may reach another device: no remote copies, remote signals or barrier semaphores. Data moves between devices by JAX's collectives and lax.ppermute only.
A program may use at most 64 MiB of HBM per device.

v0:
```python
import math

import jax
import jax.numpy as jnp
from jax import lax
from jax.sharding import PartitionSpec as P

ridge_weight = 0.1


def contract(block, b_wide, c_wide):
    rows, width_j, width_k = block.shape
    inner = jnp.dot(
        block.reshape(rows * width_j, width_k), c_wide, preferred_element_type=jnp.float32
    )
    inner = inner.reshape(rows, width_j, -1)
    return jnp.sum(inner * b_wide.astype(jnp.float32)[None], axis=1)


def partial_rows(tensor, b_wide, c_wide, row_count):
    step_rows = math.gcd(row_count, 16)
    pieces = tensor.reshape(row_count // step_rows, step_rows, tensor.shape[1], tensor.shape[2])
    result = lax.map(lambda piece: contract(piece, b_wide, c_wide), pieces)
    return result.reshape(row_count, b_wide.shape[1])


def body(tensor, factor_b, factor_c):
    b_wide = lax.all_gather(factor_b, "ka", axis=1, tiled=True)
    c_wide = lax.all_gather(factor_c, "ja", axis=1, tiled=True)
    rank = b_wide.shape[1]
    gram_b = lax.psum(jnp.dot(b_wide.T, b_wide, preferred_element_type=jnp.float32), "ja")
    gram_c = lax.psum(jnp.dot(c_wide.T, c_wide, preferred_element_type=jnp.float32), "ka")
    normal_matrix = gram_b * gram_c + ridge_weight * jnp.eye(rank, dtype=jnp.float32)
    block_rows = tensor.shape[0]
    owned = block_rows // (lax.axis_size("ja") * lax.axis_size("ka"))
    mine = lax.psum_scatter(
        partial_rows(tensor, b_wide, c_wide, owned * lax.axis_size(("ja", "ka"))),
        ("ja", "ka"),
        scatter_dimension=0,
        tiled=True,
    )
    lower = jnp.linalg.cholesky(normal_matrix)
    solved = jax.scipy.linalg.cho_solve((lower, True), mine.T)
    return solved.T


def solution(mesh):
    placed = (P("ia", "ja", "ka"), P("ja", "ka"), P("ka", "ja"))
    return jax.shard_map(
        body, mesh=mesh, in_specs=placed, out_specs=P(("ia", "ja", "ka"), None), check_vma=False
    )
```

profile of v0, /device:TPU:0, one launch (start us, length us, event | category | flops | bytes accessed | tf_op | source)
XLA Modules:
  0.0 142.1 jit_solution(7812872350361288820)
XLA Ops:
  7.4 2.2 %all_gather.6 = bf16[128,256]{1,0:T(8,128)(2,1)S(1)} all-gather(bf16[128,128]{1,0:T(8,128)(2,1)} %param.6), channel_id=1, replica_groups=mesh['ia'=4,'ja'=4,'ka'=2] {'ka'}, dimensions={1}, use_global_device_ids=true | all-gather | bytes 98304 | tf_op jit(solution)/shard_map/all_gather | solution.py:28
  10.6 15.2 %all_gather.7 = bf16[128,256]{0,1:T(8,128)(2,1)S(1)} all-gather(bf16[128,64]{0,1:T(8,128)(2,1)} %param.7), channel_id=1, replica_groups=mesh['ia'=4,'ja'=4,'ka'=2] {'ja'}, dimensions={1}, use_global_device_ids=true | all-gather | bytes 81920 | tf_op jit(solution)/shard_map/all_gather | solution.py:29
  26.9 33.7 %while.11 = (s32[]{:T(128)}, f32[16,16,256]{2,1,0:T(8,128)}, bf16[16,16,128,128]{3,2,1,0:T(8,128)(2,1)}, bf16[128,256]{1,0:T(8,128)(2,1)S(1)}, bf16[128,256]{1,0:T(8,128)(2,1)S(1)}, /*index=5*/s32[]{:T(128)}) while((s32[]{:T(128)}, f32[16,16,256]{2,1,0:T(8,128)}, bf16[16,16,128,128]{3,2,1,0:T(8,128)(2,1)}, bf16[128,256]{1,0:T(8,128)(2,1)S(1)}, ...), condition=%wide.region_8.9_spmd, body=%wide.region_6.8_spmd.sunk | while | flops 135294976 | bytes 967749 | solution.py:23
  26.9 1.5 %multiply_reduce_fusion.2 = f32[16,256]{1,0:T(8,128)S(1)} fusion(f32[128,256]{1,0:T(8,128)S(1)} %convert_element_type.9, bf16[16,16,128,128]{3,2,1,0:T(8,128)(2,1)} %get-tuple-element.167, s32[]{:T(128)} %get-tuple-element.159, bf16[128,256]{1,0:T(8,128)(2,1)S(1)} %get-tuple-element.168), kind=kOutput, calls=%fused_computation.clone.1 | convolution fusion | flops 135262208 | bytes 737792 | tf_op jit(solution)/shard_map/while/body/eval_jaxpr/dot_general | solution.py:13
  29.0 1.5 %multiply_reduce_fusion.2 = f32[16,256]{1,0:T(8,128)S(1)} fusion(f32[128,256]{1,0:T(8,128)S(1)} %convert_element_type.9, bf16[16,16,128,128]{3,2,1,0:T(8,128)(2,1)} %get-tuple-element.167, s32[]{:T(128)} %get-tuple-element.159, bf16[128,256]{1,0:T(8,128)(2,1)S(1)} %get-tuple-element.168), kind=kOutput, calls=%fused_computation.clone.1 | convolution fusion | flops 135262208 | bytes 737792 | tf_op jit(solution)/shard_map/while/body/eval_jaxpr/dot_general | solution.py:13
  31.1 1.5 %multiply_reduce_fusion.2 = f32[16,256]{1,0:T(8,128)S(1)} fusion(f32[128,256]{1,0:T(8,128)S(1)} %convert_element_type.9, bf16[16,16,128,128]{3,2,1,0:T(8,128)(2,1)} %get-tuple-element.167, s32[]{:T(128)} %get-tuple-element.159, bf16[128,256]{1,0:T(8,128)(2,1)S(1)} %get-tuple-element.168), kind=kOutput, calls=%fused_computation.clone.1 | convolution fusion | flops 135262208 | bytes 737792 | tf_op jit(solution)/shard_map/while/body/eval_jaxpr/dot_general | solution.py:13
  33.2 1.5 %multiply_reduce_fusion.2 = f32[16,256]{1,0:T(8,128)S(1)} fusion(f32[128,256]{1,0:T(8,128)S(1)} %convert_element_type.9, bf16[16,16,128,128]{3,2,1,0:T(8,128)(2,1)} %get-tuple-element.167, s32[]{:T(128)} %get-tuple-element.159, bf16[128,256]{1,0:T(8,128)(2,1)S(1)} %get-tuple-element.168), kind=kOutput, calls=%fused_computation.clone.1 | convolution fusion | flops 135262208 | bytes 737792 | tf_op jit(solution)/shard_map/while/body/eval_jaxpr/dot_general | solution.py:13
  35.3 1.5 %multiply_reduce_fusion.2 = f32[16,256]{1,0:T(8,128)S(1)} fusion(f32[128,256]{1,0:T(8,128)S(1)} %convert_element_type.9, bf16[16,16,128,128]{3,2,1,0:T(8,128)(2,1)} %get-tuple-element.167, s32[]{:T(128)} %get-tuple-element.159, bf16[128,256]{1,0:T(8,128)(2,1)S(1)} %get-tuple-element.168), kind=kOutput, calls=%fused_computation.clone.1 | convolution fusion | flops 135262208 | bytes 737792 | tf_op jit(solution)/shard_map/while/body/eval_jaxpr/dot_general | solution.py:13
  37.4 1.5 %multiply_reduce_fusion.2 = f32[16,256]{1,0:T(8,128)S(1)} fusion(f32[128,256]{1,0:T(8,128)S(1)} %convert_element_type.9, bf16[16,16,128,128]{3,2,1,0:T(8,128)(2,1)} %get-tuple-element.167, s32[]{:T(128)} %get-tuple-element.159, bf16[128,256]{1,0:T(8,128)(2,1)S(1)} %get-tuple-element.168), kind=kOutput, calls=%fused_computation.clone.1 | convolution fusion | flops 135262208 | bytes 737792 | tf_op jit(solution)/shard_map/while/body/eval_jaxpr/dot_general | solution.py:13
  39.5 1.5 %multiply_reduce_fusion.2 = f32[16,256]{1,0:T(8,128)S(1)} fusion(f32[128,256]{1,0:T(8,128)S(1)} %convert_element_type.9, bf16[16,16,128,128]{3,2,1,0:T(8,128)(2,1)} %get-tuple-element.167, s32[]{:T(128)} %get-tuple-element.159, bf16[128,256]{1,0:T(8,128)(2,1)S(1)} %get-tuple-element.168), kind=kOutput, calls=%fused_computation.clone.1 | convolution fusion | flops 135262208 | bytes 737792 | tf_op jit(solution)/shard_map/while/body/eval_jaxpr/dot_general | solution.py:13
  41.6 1.5 %multiply_reduce_fusion.2 = f32[16,256]{1,0:T(8,128)S(1)} fusion(f32[128,256]{1,0:T(8,128)S(1)} %convert_element_type.9, bf16[16,16,128,128]{3,2,1,0:T(8,128)(2,1)} %get-tuple-element.167, s32[]{:T(128)} %get-tuple-element.159, bf16[128,256]{1,0:T(8,128)(2,1)S(1)} %get-tuple-element.168), kind=kOutput, calls=%fused_computation.clone.1 | convolution fusion | flops 135262208 | bytes 737792 | tf_op jit(solution)/shard_map/while/body/eval_jaxpr/dot_general | solution.py:13
  43.7 1.5 %multiply_reduce_fusion.2 = f32[16,256]{1,0:T(8,128)S(1)} fusion(f32[128,256]{1,0:T(8,128)S(1)} %convert_element_type.9, bf16[16,16,128,128]{3,2,1,0:T(8,128)(2,1)} %get-tuple-element.167, s32[]{:T(128)} %get-tuple-element.159, bf16[128,256]{1,0:T(8,128)(2,1)S(1)} %get-tuple-element.168), kind=kOutput, calls=%fused_computation.clone.1 | convolution fusion | flops 135262208 | bytes 737792 | tf_op jit(solution)/shard_map/while/body/eval_jaxpr/dot_general | solution.py:13
  45.8 1.5 %multiply_reduce_fusion.2 = f32[16,256]{1,0:T(8,128)S(1)} fusion(f32[128,256]{1,0:T(8,128)S(1)} %convert_element_type.9, bf16[16,16,128,128]{3,2,1,0:T(8,128)(2,1)} %get-tuple-element.167, s32[]{:T(128)} %get-tuple-element.159, bf16[128,256]{1,0:T(8,128)(2,1)S(1)} %get-tuple-element.168), kind=kOutput, calls=%fused_computation.clone.1 | convolution fusion | flops 135262208 | bytes 737792 | tf_op jit(solution)/shard_map/while/body/eval_jaxpr/dot_general | solution.py:13
  47.9 1.5 %multiply_reduce_fusion.2 = f32[16,256]{1,0:T(8,128)S(1)} fusion(f32[128,256]{1,0:T(8,128)S(1)} %convert_element_type.9, bf16[16,16,128,128]{3,2,1,0:T(8,128)(2,1)} %get-tuple-element.167, s32[]{:T(128)} %get-tuple-element.159, bf16[128,256]{1,0:T(8,128)(2,1)S(1)} %get-tuple-element.168), kind=kOutput, calls=%fused_computation.clone.1 | convolution fusion | flops 135262208 | bytes 737792 | tf_op jit(solution)/shard_map/while/body/eval_jaxpr/dot_general | solution.py:13
  50.0 1.5 %multiply_reduce_fusion.2 = f32[16,256]{1,0:T(8,128)S(1)} fusion(f32[128,256]{1,0:T(8,128)S(1)} %convert_element_type.9, bf16[16,16,128,128]{3,2,1,0:T(8,128)(2,1)} %get-tuple-element.167, s32[]{:T(128)} %get-tuple-element.159, bf16[128,256]{1,0:T(8,128)(2,1)S(1)} %get-tuple-element.168), kind=kOutput, calls=%fused_computation.clone.1 | convolution fusion | flops 135262208 | bytes 737792 | tf_op jit(solution)/shard_map/while/body/eval_jaxpr/dot_general | solution.py:13
  52.1 1.5 %multiply_reduce_fusion.2 = f32[16,256]{1,0:T(8,128)S(1)} fusion(f32[128,256]{1,0:T(8,128)S(1)} %convert_element_type.9, bf16[16,16,128,128]{3,2,1,0:T(8,128)(2,1)} %get-tuple-element.167, s32[]{:T(128)} %get-tuple-element.159, bf16[128,256]{1,0:T(8,128)(2,1)S(1)} %get-tuple-element.168), kind=kOutput, calls=%fused_computation.clone.1 | convolution fusion | flops 135262208 | bytes 737792 | tf_op jit(solution)/shard_map/while/body/eval_jaxpr/dot_general | solution.py:13
  56.3 1.5 %multiply_reduce_fusion.2 = f32[16,256]{1,0:T(8,128)S(1)} fusion(f32[128,256]{1,0:T(8,128)S(1)} %convert_element_type.9, bf16[16,16,128,128]{3,2,1,0:T(8,128)(2,1)} %get-tuple-element.167, s32[]{:T(128)} %get-tuple-element.159, bf16[128,256]{1,0:T(8,128)(2,1)S(1)} %get-tuple-element.168), kind=kOutput, calls=%fused_computation.clone.1 | convolution fusion | flops 135262208 | bytes 737792 | tf_op jit(solution)/shard_map/while/body/eval_jaxpr/dot_general | solution.py:13
  58.4 1.5 %multiply_reduce_fusion.2 = f32[16,256]{1,0:T(8,128)S(1)} fusion(f32[128,256]{1,0:T(8,128)S(1)} %convert_element_type.9, bf16[16,16,128,128]{3,2,1,0:T(8,128)(2,1)} %get-tuple-element.167, s32[]{:T(128)} %get-tuple-element.159, bf16[128,256]{1,0:T(8,128)(2,1)S(1)} %get-tuple-element.168), kind=kOutput, calls=%fused_computation.clone.1 | convolution fusion | flops 135262208 | bytes 737792 | tf_op jit(solution)/shard_map/while/body/eval_jaxpr/dot_general | solution.py:13
  60.6 8.9 %all-reduce.6.cloned.1.call-done = f32[256,256]{0,1:T(8,128)} async-done(((f32[256,256]{0,1:T(8,128)}), f32[256,256]{0,1:T(8,128)}) %all-reduce.6.cloned.1.call-update) | async-done | bytes 262160 | tf_op jit(solution)/shard_map/psum | solution.py:32
  70.8 11.7 %cholesky.49 = f32[128,128]{1,0:T(8,128)S(1)} custom-call(f32[128,128]{1,0:T(8,128)S(1)} %cholesky.115), custom_call_target="Cholesky" | custom-call | tf_op jit(solution)/shard_map/jit(cholesky)/cholesky | solution.py:42
  82.5 9.8 %custom-call.18 = f32[1,128,128]{1,2,0:T(8,128)S(1)} custom-call(f32[1,128,128]{2,1,0:T(8,128)S(1)} %get-tuple-element.75), custom_call_target="InvertDiagBlocksLowerTriangular" | custom-call | tf_op jit(solution)/shard_map/jit(cholesky)/cholesky | solution.py:42
  92.8 11.7 %cholesky.103 = f32[128,128]{1,0:T(8,128)S(1)} custom-call(f32[128,128]{1,0:T(8,128)S(1)} %convolution_subtract_fusion), custom_call_target="Cholesky" | custom-call | tf_op jit(solution)/shard_map/jit(cholesky)/cholesky | solution.py:42
  107.0 4.3 %while.12 = (s32[]{:T(128)}, f32[256,256]{0,1:T(8,128)S(1)}, s32[2,2]{1,0:T(2,128)S(1)}, f32[2,128,128]{2,1,0:T(8,128)S(1)}, s32[]{:T(128)}) while((s32[]{:T(128)}, f32[256,256]{0,1:T(8,128)S(1)}, s32[2,2]{1,0:T(2,128)S(1)}, f32[2,128,128]{2,1,0:T(8,128)S(1)}, s32[]{:T(128)}) %tuple.37), condition=%wide.while_cond, body=%wide.while_body.sunk | while | flops 2 | bytes 393321 | solution.py:43
  111.3 19.9 %custom-call.19 = f32[2,128,128]{1,2,0:T(8,128)S(1)} custom-call(f32[2,128,128]{2,1,0:T(8,128)S(1)} %get-tuple-element.40), custom_call_target="InvertDiagBlocksLowerTriangular" | custom-call | tf_op jit(solution)/shard_map/jit(_cho_solve)/triangular_solve | solution.py:43
  (81 shorter events, 24.0 us)
Async XLA Ops:
  7.4 53.2 %all-reduce.4.cloned.1.call-start = ((), (), s32[]{:S(2)}) async-start(), calls=%async_computation.1 | async-start | bytes 524288 | tf_op jit(solution)/shard_map/psum | solution.py:31
  10.5 59.0 %all-reduce.6.cloned.1.call-start = ((), (), s32[]{:S(2)}) async-start(), calls=%async_computation.2 | async-start | bytes 524288 | tf_op jit(solution)/shard_map/psum | solution.py:32
  26.7 104.5 %reduce-scatter.2.cloned.1.call-start = ((), (), s32[]{:S(2)}) async-start(), calls=%async_computation.3 | async-start | bytes 294912 | tf_op jit(solution)/shard_map/reduce_scatter | solution.py:36
Sparse Core Ops, SparseCore 0:
  10.7 38.3 all-reduce.3
  51.4 18.0 all-reduce.5
Sparse Core Ops, SparseCore 1:
  60.6 31.9 reduce-scatter.1
where the time goes:
time: 143 us; the launch traced here: 142 us
  other arithmetic  55.8 us (39%)
  matrix products  28.6 us (20%)
  blocking collectives  17.4 us (12%)
  between operations  16.3 us (11%)
  local copies, waits for them, and re-layouts  14.6 us (10%)
  waiting for transfers between devices  9.01 us (6%)
    another operation x6, other arithmetic, body(): lower = jnp.linalg.cholesky(normal_matrix)  34 us
    dot_general x16, matrix products, contract(): jnp.dot(block.reshape(rows * width_j, width_k), c_wide, preferred_element...  23.6 us
    another operation x3, other arithmetic, body(): solved = jax.scipy.linalg.cho_solve((lower, True), mine.T)  19.9 us
    all_gather x1, blocking collectives, body(): c_wide = lax.all_gather(factor_c, 'ja', axis=1, tiled=True)  15.2 us
    dynamic_update_slice x16, local copies, waits for them, and re-layouts, partial_rows(): result = lax.map(lambda piece: contract(piece, b_wide, c_wide), pieces)  9.71 us
    psum x1, waiting for transfers between devices, body(): lax.psum(jnp.dot(c_wide.T, c_wide, preferred_element_type=jnp.float32), '...  8.92 us
    another operation x10, local copies, waits for them, and re-layouts  4.22 us
  transfers between devices with their start and end apart: 3, of which 1 were waited for; matrix products, arithmetic and copies ran while one was open for 67% of the time, Pallas kernels for 0%

commit v1 on v0

v1 whole, which is shorter than its diff:
```python
import functools

import jax
import jax.numpy as jnp
from jax import lax
from jax.experimental import pallas as pl
from jax.experimental.pallas import tpu as pltpu
from jax.sharding import PartitionSpec as P

ridge_weight = 0.1
exact = lax.Precision.HIGHEST
vmem = pl.BlockSpec(memory_space=pltpu.VMEM)
smem = pl.BlockSpec(memory_space=pltpu.SMEM)
hbm = pl.BlockSpec(memory_space=pl.ANY)


def shift(n, s):
    return [(i, (i + s) % n) for i in range(n)]


def wrap(x, n):
    return lax.rem(x + n, n)


def mttkrp_kernel(nj, nk, height_b, flipped, where, block, *refs):
    c_parts, refs = refs[:nj], refs[nj:]
    b_parts, refs = refs[:nk], refs[nk:]
    out, held, c_rows, b_rows, arrived = refs
    me_j, me_k = where[0], where[1]
    owned = out.shape[2]

    def owner_rows(turn):
        t, u = nk - 1 - turn // nj, turn % nj
        to = wrap(me_j + u, nj) * nk + wrap(me_k + t, nk)
        return t, u, pl.multiple_of(to * owned, owned)

    def load(turn):
        _, _, first = owner_rows(turn)
        rows = pl.ds(first, owned)
        return pltpu.make_async_copy(block.at[rows], held.at[rows], arrived.at[turn])

    for turn in range(nj * nk):
        load(turn).start()
    width_c = c_parts[0].shape[0] - height_b
    for s in range(nj):
        at = pl.multiple_of(wrap(me_j - s, nj) * width_c, width_c)
        c_rows[pl.ds(at, width_c), :] = c_parts[s][height_b:, :]
    for t in range(nk):
        at = pl.multiple_of(wrap(me_k - t, nk) * height_b, height_b)
        if flipped:
            b_rows[pl.ds(at, height_b), :] = b_parts[t][:height_b, :]
        else:
            at = pl.multiple_of(wrap(me_k - t, nk) * 128, 128)
            b_rows[:, pl.ds(at, 128)] = b_parts[t][:height_b, :]
    c_wide = c_rows[...].T
    b_wide = (b_rows[...].T if flipped else b_rows[...]).astype(jnp.float32)

    def step(turn, _):
        load(turn).wait()
        t, u, first = owner_rows(turn)
        sums = []
        for i in range(owned):
            inner = jnp.dot(held[first + i], c_wide, preferred_element_type=jnp.float32)
            sums.append(jnp.sum(inner * b_wide, axis=0, keepdims=True))
        out[t, u] = jnp.concatenate(sums, axis=0)
        return 0

    lax.fori_loop(0, nj * nk, step, 0)


def mttkrp(where, tensor, c_parts, b_parts, height_b, flipped, nj, nk, rank):
    rows, width_j, width_k = tensor.shape
    owned = rows // (nj * nk)
    b_shape = (rank, width_j) if flipped else (width_j, rank)
    return pl.pallas_call(
        functools.partial(mttkrp_kernel, nj, nk, height_b, flipped),
        out_shape=jax.ShapeDtypeStruct((nk, nj, owned, rank), jnp.float32),
        in_specs=[smem, hbm] + [vmem] * (nj + nk),
        out_specs=vmem,
        scratch_shapes=[
            pltpu.VMEM(tensor.shape, tensor.dtype),
            pltpu.VMEM((rank, width_k), tensor.dtype),
            pltpu.VMEM(b_shape, tensor.dtype),
            pltpu.SemaphoreType.DMA((nj * nk,)),
        ],
        compiler_params=pltpu.CompilerParams(vmem_limit_bytes=40 * 2**20),
        cost_estimate=pl.CostEstimate(
            flops=2 * rows * width_j * width_k * rank,
            bytes_accessed=2 * rows * width_j * width_k,
            transcendentals=0,
        ),
    )(where, tensor, *c_parts, *b_parts)


def column(x, q):
    return jnp.broadcast_to(x[:, q : q + 1], x.shape)


def row(x, q):
    return jnp.broadcast_to(x[q : q + 1, :], x.shape)


def invert(a, step=16):
    size = a.shape[0]
    groups, per = size // 8, step // 8
    rows = [a[8 * i : 8 * i + 8, :] for i in range(groups)]
    lane = lax.broadcasted_iota(jnp.int32, (8, size), 1)
    sub = lax.broadcasted_iota(jnp.int32, (8, size), 0)
    for first in range(0, size, step):
        g0 = first // 8
        cols = [[column(r, first + q) for q in range(step)] for r in rows]
        inside = (lane >= first) & (lane < first + step)
        panel = rows[g0 : g0 + per]
        c = [[cols[g0 + i][q] for i in range(per)] for q in range(step)]
        for q in range(step):
            gq, sq = q // 8, q % 8
            here = sub == sq
            inv = 1.0 / row(c[q][gq], sq)
            pivot_row = jnp.where(lane == first + q, inv, row(panel[gq], sq) * inv)
            for i in range(per):
                new = jnp.where(lane == first + q, 0.0, panel[i]) - c[q][i] * pivot_row
                panel[i] = jnp.where(here, pivot_row, new) if i == gq else new
            for p in range(q + 1, step):
                scaled = row(c[p][gq], sq) * inv
                for i in range(per):
                    new = c[p][i] - c[q][i] * scaled
                    c[p][i] = jnp.where(here, scaled, new) if i == gq else new
        spread = [row(panel[q // 8], q % 8) for q in range(step)]
        for i in range(groups):
            if g0 <= i < g0 + per:
                rows[i] = panel[i - g0]
                continue
            update = cols[i][0] * spread[0]
            for q in range(1, step):
                update = update + cols[i][q] * spread[q]
            rows[i] = jnp.where(inside, 0.0, rows[i]) - update
    return jnp.concatenate(rows, axis=0)


def dot_t(x, y):
    return lax.dot_general(
        x, y, (((1,), (1,)), ((), ())), preferred_element_type=jnp.float32, precision=exact
    )


def head_kernel(nj, nk, height_b, flipped, where, *refs):
    parts, refs = refs[: nj * nk], refs[nj * nk :]
    top_out, cross_out, rest_out, b_all, c_all = refs
    me_j, me_k = where[0], where[1]
    half = cross_out.shape[0]
    width_c = parts[0].shape[0] - height_b
    height = b_all.shape[1]
    for s in range(nj):
        for t in range(nk):
            part = parts[s * nk + t]
            at = pl.multiple_of(wrap(me_j - s, nj) * width_c, width_c)
            c_all[t, pl.ds(at, width_c), :] = part[height_b:, :]
            if flipped:
                at = pl.multiple_of(wrap(me_k - t, nk) * height_b, height_b)
                b_all[s, pl.ds(at, height_b), :] = part[:height_b, :]
            else:
                at = pl.multiple_of(wrap(me_k - t, nk) * 128, 128)
                b_all[s, :, pl.ds(at, 128)] = part[:height_b, :]

    def gram(x, contracted):
        dims = (((contracted,), (contracted,)), ((), ()))
        return lax.dot_general(x, x, dims, preferred_element_type=jnp.float32)

    if flipped:
        gram_b = sum(gram(b_all[s], 1) for s in range(nj))
    else:
        gram_b = gram(b_all[...].reshape(nj * height, 2 * half), 0)
    gram_c = sum(gram(c_all[t], 1) for t in range(nk))
    size = 2 * half
    diagonal = lax.broadcasted_iota(jnp.int32, (size, size), 0) == lax.broadcasted_iota(
        jnp.int32, (size, size), 1
    )
    normal = gram_b * gram_c + jnp.where(diagonal, ridge_weight, 0.0)
    top = invert(normal[:half, :half])
    right = normal[:half, half:]
    cross = jnp.dot(top, right, precision=exact, preferred_element_type=jnp.float32)
    top_out[...] = top
    cross_out[...] = cross
    rest_out[...] = normal[half:, half:] - jnp.dot(
        right.T, cross, precision=exact, preferred_element_type=jnp.float32
    )


def tail_kernel(*refs):
    rows, (top, cross, rest, out) = refs[:-4], refs[-4:]
    half = cross.shape[0]
    mine = rows[0][...]
    for r in rows[1:]:
        mine = mine + r[...]
    left, right = mine[:, :half], mine[:, half:]
    dot = functools.partial(jnp.dot, precision=exact, preferred_element_type=jnp.float32)
    reduced = right - dot(left, cross[...])
    partial = dot(left, top[...])
    solved = dot(reduced, invert(rest[...]))
    out[:, half:] = solved
    out[:, :half] = partial - dot_t(solved, cross[...])


def body(tensor, factor_b, factor_c):
    nj, nk = lax.axis_size("ja"), lax.axis_size("ka")
    where = jnp.stack([lax.axis_index("ja"), lax.axis_index("ka")]).astype(jnp.int32)
    rank = factor_b.shape[1] * nk
    half = rank // 2
    flipped = factor_b.shape[1] % 128 != 0
    part_b = factor_b.T if flipped else factor_b
    height_b = part_b.shape[0]
    mine = jnp.concatenate([part_b, factor_c.T], axis=0)
    line = [mine] + [lax.ppermute(mine, "ja", shift(nj, s)) for s in range(1, nj)]
    parts = [[x] + [lax.ppermute(x, "ka", shift(nk, t)) for t in range(1, nk)] for x in line]
    sums = mttkrp(where, tensor, line, parts[0], height_b, flipped, nj, nk, rank)
    total = sums[0]
    for t in range(1, nk):
        total = total + lax.ppermute(sums[t], "ka", shift(nk, t))
    rows = [total[0]] + [lax.ppermute(total[u], "ja", shift(nj, u)) for u in range(1, nj)]
    flat = [x for group in parts for x in group]
    square = jax.ShapeDtypeStruct((half, half), jnp.float32)
    b_shape = (nj, rank, part_b.shape[1]) if flipped else (nj, height_b, rank)
    top, cross, rest = pl.pallas_call(
        functools.partial(head_kernel, nj, nk, height_b, flipped),
        out_shape=[square] * 3,
        in_specs=[smem] + [vmem] * len(flat),
        out_specs=[vmem] * 3,
        scratch_shapes=[
            pltpu.VMEM(b_shape, factor_b.dtype),
            pltpu.VMEM((nk, rank, factor_c.shape[0]), factor_c.dtype),
        ],
        compiler_params=pltpu.CompilerParams(vmem_limit_bytes=40 * 2**20),
        cost_estimate=pl.CostEstimate(flops=10**10, bytes_accessed=2**20, transcendentals=0),
    )(where, *flat)
    return pl.pallas_call(
        tail_kernel,
        out_shape=jax.ShapeDtypeStruct((rows[0].shape[0], rank), jnp.float32),
        in_specs=[vmem] * (len(rows) + 3),
        out_specs=vmem,
        compiler_params=pltpu.CompilerParams(vmem_limit_bytes=40 * 2**20),
        cost_estimate=pl.CostEstimate(flops=10**10, bytes_accessed=2**20, transcendentals=0),
    )(*rows, top, cross, rest)


def solution(mesh):
    placed = (P("ia", "ja", "ka"), P("ja", "ka"), P("ka", "ja"))
    return jax.shard_map(
        body, mesh=mesh, in_specs=placed, out_specs=P(("ia", "ja", "ka"), None), check_vma=False
    )
```

time: 143 us -> 41.6 us (0.29)
  other arithmetic: 55.8 us -> 0.87 us
  matrix products: 28.6 us -> 0 us
  Pallas kernels: 0 us -> 20.8 us
  blocking collectives: 17.4 us -> 0 us
  between operations: 16.3 us -> 0.08 us
  local copies, waits for them, and re-layouts: 14.6 us -> 3.4 us
  starting transfers between devices: 0.09 us -> 10.9 us
  waiting for transfers between devices: 9.01 us -> 5.3 us
    another operation x9 -> x1, other arithmetic: 53.9 us -> 0.07 us  [body(): jnp.stack([lax.axis_index('ja'), lax.axis_index('ka')]).astype(jnp.int32)]
    dot_general x18 -> x0, matrix products: 25.4 us -> none  [the longest x16 23.6 us: contract(): jnp.dot(block.reshape(rows * width_j, width_k), c_wide, preferred_element...]
    pallas_call x0 -> x3, Pallas kernels: none -> 20.8 us  [the longest x1 7.1 us: mttkrp(): pl.pallas_call(functools.partial(mttkrp_kernel, nj, nk, height_b, flipped...]
    all_gather x2 -> x0, blocking collectives: 17.4 us -> none  [the longest x1 15.2 us: body(): c_wide = lax.all_gather(factor_c, 'ja', axis=1, tiled=True)]
    ppermute x0 -> x11, starting transfers between devices: none -> 10.9 us  [the longest x3 5.62 us: body(): lax.ppermute(mine, 'ja', shift(nj, s))]
    dynamic_update_slice x16 -> x0, local copies, waits for them, and re-layouts: 9.71 us -> none  [partial_rows(): result = lax.map(lambda piece: contract(piece, b_wide, c_wide), pieces)]
    psum x2 -> x0, waiting for transfers between devices: 8.94 us -> none  [the longest x1 8.92 us: body(): lax.psum(jnp.dot(c_wide.T, c_wide, preferred_element_type=jnp.float32), '...]
    ppermute x0 -> x11, waiting for transfers between devices: none -> 5.3 us  [the longest x3 4.95 us: body(): lax.ppermute(mine, 'ja', shift(nj, s))]
  transfers between devices with their start and end apart: 3 -> 11, of which waited for: 1 -> 3; matrix products, arithmetic and copies ran while one was open for 67% -> 0% of each run, Pallas kernels for 0% -> 17%
where the time goes in v1:
time: 41.6 us; the launch traced here: 41.4 us
  Pallas kernels  20.8 us (50%)
  starting transfers between devices  10.9 us (26%)
  waiting for transfers between devices  5.3 us (13%)
  local copies, waits for them, and re-layouts  3.4 us (8%)
  other arithmetic  0.87 us (2%)
    pallas_call x1, Pallas kernels, mttkrp(): pl.pallas_call(functools.partial(mttkrp_kernel, nj, nk, height_b, flipped...  7.1 us
    pallas_call x1, Pallas kernels, body(): pl.pallas_call(functools.partial(head_kernel, nj, nk, height_b, flipped),...  6.99 us
    pallas_call x1, Pallas kernels, body(): pl.pallas_call(tail_kernel, out_shape=jax.ShapeDtypeStruct((rows[0].shape...  6.72 us
    ppermute x3, starting transfers between devices, body(): lax.ppermute(mine, 'ja', shift(nj, s))  5.62 us
    ppermute x3, waiting for transfers between devices, body(): lax.ppermute(mine, 'ja', shift(nj, s))  4.95 us
    ppermute x3, starting transfers between devices, body(): lax.ppermute(total[u], 'ja', shift(nj, u))  3.71 us
    unnamed x2, local copies, waits for them, and re-layouts  3.38 us
    ppermute x4, starting transfers between devices, body(): lax.ppermute(x, 'ka', shift(nk, t))  1.5 us
  transfers between devices with their start and end apart: 11, of which 3 were waited for; matrix products, arithmetic and copies ran while one was open for 0% of the time, Pallas kernels for 17%

profile of v1, /device:TPU:0, one launch (start us, length us, event | category | flops | bytes accessed | tf_op | source)
XLA Modules:
  0.0 41.4 jit_solution(4298068622114945799)
XLA Ops:
  0.0 0.8 %pad_maximum_fusion.refs_0_.refs_4_ = bf16[192,128]{1,0:T(8,128)(2,1)S(1)} fusion(bf16[64,128]{1,0:T(8,128)(2,1)} %bitcast.17, bf16[128,128]{1,0:T(8,128)(2,1)} %param.4), kind=kLoop, calls=%fused_computation.3 | loop fusion | flops 98304 | bytes 98304 | tf_op jit(solution)/shard_map/concatenate | solution.py:212
  0.8 0.5 %collective-permute-start.3 = (bf16[192,128]{1,0:T(8,128)(2,1)S(1)}, bf16[192,128]{1,0:T(8,128)(2,1)S(1)}, u32[]{:S(2)}, u32[]{:S(2)}) collective-permute-start(bf16[192,128]{1,0:T(8,128)(2,1)S(1)} %pad_maximum_fusion.refs_0_.refs_4_), channel_id=1, source_target_pairs={{0,1},{1,0},{2,3},{3,2},{4,5},{5,4},{6,7},{7,6},{8,9},{9,8},{10,11... | collective-permute-start | bytes 147464 | tf_op jit(solution)/shard_map/ppermute | solution.py:214
  1.3 4.6 %collective-permute-start.2 = (bf16[192,128]{1,0:T(8,128)(2,1)S(1)}, bf16[192,128]{1,0:T(8,128)(2,1)S(1)}, u32[]{:S(2)}, u32[]{:S(2)}) collective-permute-start(bf16[192,128]{1,0:T(8,128)(2,1)S(1)} %pad_maximum_fusion.refs_0_.refs_4_), channel_id=1, source_target_pairs={{0,6},{2,0},{4,2},{6,4},{1,7},{3,1},{5,3},{7,5},{8,14},{10,8},{12,... | collective-permute-start | bytes 147464 | tf_op jit(solution)/shard_map/ppermute | solution.py:213
  5.9 0.0 collective-permute-start.1
  5.9 1.0 %collective-permute-start = (bf16[192,128]{1,0:T(8,128)(2,1)S(1)}, bf16[192,128]{1,0:T(8,128)(2,1)S(1)}, u32[]{:S(2)}, u32[]{:S(2)}) collective-permute-start(bf16[192,128]{1,0:T(8,128)(2,1)S(1)} %pad_maximum_fusion.refs_0_.refs_4_), channel_id=1, source_target_pairs={{0,2},{2,4},{4,6},{6,0},{1,3},{3,5},{5,7},{7,1},{8,10},{10,12},{12... | collective-permute-start | bytes 147464 | tf_op jit(solution)/shard_map/ppermute | solution.py:213
  6.9 0.1 pad_add_fusion.where
  7.0 0.0 collective-permute-done.3.refs_5_.refs_1_
  7.0 1.0 %collective-permute-done.2.refs_3_.refs_6_ = bf16[192,128]{1,0:T(8,128)(2,1)S(1)} collective-permute-done((bf16[192,128]{1,0:T(8,128)(2,1)S(1)}, bf16[192,128]{1,0:T(8,128)(2,1)S(1)}, u32[]{:S(2)}, u32[]{:S(2)}) %collective-permute-start.2) | collective-permute-done | bytes 49184 | tf_op jit(solution)/shard_map/ppermute | solution.py:213
  8.0 3.9 %collective-permute-done.1.refs_2_.refs_4_ = bf16[192,128]{1,0:T(8,128)(2,1)S(1)} collective-permute-done((bf16[192,128]{1,0:T(8,128)(2,1)S(1)}, bf16[192,128]{1,0:T(8,128)(2,1)S(1)}, u32[]{:S(2)}, u32[]{:S(2)}) %collective-permute-start.1) | collective-permute-done | bytes 49184 | tf_op jit(solution)/shard_map/ppermute | solution.py:213
  11.9 0.0 collective-permute-done.refs_1_.refs_2_
  11.9 3.4 %copy-done = bf16[256,128,128]{2,1,0:T(8,128)(2,1)S(1)} copy-done((bf16[256,128,128]{2,1,0:T(8,128)(2,1)S(1)}, bf16[256,128,128]{2,1,0:T(8,128)(2,1)}, u32[]{:S(2)}) %copy-start) | copy-done | bytes 8388632
  15.3 7.1 %shard_map.37 = f32[2,4,32,256]{3,2,1,0:T(8,128)S(1)} custom-call(s32[2]{0:T(128)S(1)} %pad_add_fusion.where, bf16[256,128,128]{2,1,0:T(8,128)(2,1)S(1)} %copy-done, bf16[192,128]{1,0:T(8,128)(2,1)S(1)} %pad_maximum_fusion.refs_0_.refs_4_, bf16[192,128]{1,0:T(8,128)(2,1)S(1)} %collective-permute-done.refs_1_.refs_2_, ...), custom_call_target="tpu_custom_call" | custom-call | flops 2147483648 | bytes 8388608 | tf_op jit(solution)/shard_map/pallas_call | solution.py:75
  22.4 0.1 collective-permute-start.4
  22.5 0.5 %collective-permute-start.10 = (bf16[192,128]{1,0:T(8,128)(2,1)S(1)}, bf16[192,128]{1,0:T(8,128)(2,1)S(1)}, u32[]{:S(2)}, u32[]{:S(2)}) collective-permute-start(bf16[192,128]{1,0:T(8,128)(2,1)S(1)} %collective-permute-done.2.refs_3_.refs_6_), channel_id=1, source_target_pairs={{0,1},{1,0},{2,3},{3,2},{4,5},{5,4},{6,7},{7,6},{8,9},{9,8},{10,11... | collective-permute-start | bytes 147464 | tf_op jit(solution)/shard_map/ppermute | solution.py:214
  23.0 0.1 collective-permute-start.9
  23.1 0.4 %collective-permute-start.8 = (bf16[192,128]{1,0:T(8,128)(2,1)S(1)}, bf16[192,128]{1,0:T(8,128)(2,1)S(1)}, u32[]{:S(2)}, u32[]{:S(2)}) collective-permute-start(bf16[192,128]{1,0:T(8,128)(2,1)S(1)} %collective-permute-done.refs_1_.refs_2_), channel_id=1, source_target_pairs={{0,1},{1,0},{2,3},{3,2},{4,5},{5,4},{6,7},{7,6},{8,9},{9,8},{10,11... | collective-permute-start | bytes 147464 | tf_op jit(solution)/shard_map/ppermute | solution.py:214
  23.5 0.3 collective-permute-done.4
  23.9 2.0 %collective-permute-start.7 = (f32[32,256]{1,0:T(8,128)S(1)}, f32[32,256]{1,0:T(8,128)S(1)}, u32[]{:S(2)}, u32[]{:S(2)}) collective-permute-start(f32[32,256]{1,0:T(8,128)S(1)} %get-tuple-element.11), channel_id=1, source_target_pairs={{0,6},{2,0},{4,2},{6,4},{1,7},{3,1},{5,3},{7,5},{8,14},{10,8},{12,... | collective-permute-start | bytes 98312 | tf_op jit(solution)/shard_map/ppermute | solution.py:219
  25.8 0.0 collective-permute-start.6
  25.8 0.0 collective-permute-done.10.refs_7_
  25.8 1.7 %collective-permute-start.5 = (f32[32,256]{1,0:T(8,128)S(1)}, f32[32,256]{1,0:T(8,128)S(1)}, u32[]{:S(2)}, u32[]{:S(2)}) collective-permute-start(f32[32,256]{1,0:T(8,128)S(1)} %get-tuple-element.13), channel_id=1, source_target_pairs={{0,2},{2,4},{4,6},{6,0},{1,3},{3,5},{5,7},{7,1},{8,10},{10,12},{12... | collective-permute-start | bytes 98312 | tf_op jit(solution)/shard_map/ppermute | solution.py:219
  27.6 7.0 %shard_map.38 = (f32[128,128]{1,0:T(8,128)S(1)}, f32[128,128]{1,0:T(8,128)S(1)}, f32[128,128]{1,0:T(8,128)S(1)}) custom-call(s32[2]{0:T(128)S(1)} %pad_add_fusion.where, bf16[192,128]{1,0:T(8,128)(2,1)S(1)} %pad_maximum_fusion.refs_0_.refs_4_, bf16[192,128]{1,0:T(8,128)(2,1)S(1)} %collective-permute-done.3.refs_5_.refs_1_, ...), custom_call_target="tpu_custom_call" | custom-call | flops 10000000000 | bytes 1048576 | tf_op jit(solution)/shard_map/pallas_call | solution.py:223
  34.6 0.0 collective-permute-done.7.refs_3_
  34.6 6.7 %shard_map.39 = f32[32,256]{1,0:T(8,128)} custom-call(f32[32,256]{1,0:T(8,128)S(1)} %get-tuple-element.14.refs_0_, f32[32,256]{1,0:T(8,128)S(1)} %collective-permute-done.5.refs_1_, f32[32,256]{1,0:T(8,128)S(1)} %collective-permute-done.6.refs_2_, f32[32,256]{1,0:T(8,128)S(1)} %collective-permute-done.7.refs_3_, f32[128,128]{1,0:T(8,128)S(1)} %get-tuple-element.8.refs_4_, ...), custom_call_target="tpu_custom_call" | custom-call | flops 10000000000 | bytes 1048576 | tf_op jit(solution)/shard_map/pallas_call | solution.py:235
  (8 shorter events, 0.1 us)
Async XLA Ops:
  0.8 6.2 %collective-permute-start.3 = (bf16[192,128]{1,0:T(8,128)(2,1)S(1)}, bf16[192,128]{1,0:T(8,128)(2,1)S(1)}, u32[]{:S(2)}, u32[]{:S(2)}) collective-permute-start(bf16[192,128]{1,0:T(8,128)(2,1)S(1)} %pad_maximum_fusion.refs_0_.refs_4_), channel_id=1, source_target_pairs={{0,1},{1,0},{2,3},{3,2},{4,5},{5,4},{6,7},{7,6},{8,9},{9,8},{10,11... | collective-permute-start | bytes 147464 | tf_op jit(solution)/shard_map/ppermute | solution.py:214
  1.3 6.7 %collective-permute-start.2 = (bf16[192,128]{1,0:T(8,128)(2,1)S(1)}, bf16[192,128]{1,0:T(8,128)(2,1)S(1)}, u32[]{:S(2)}, u32[]{:S(2)}) collective-permute-start(bf16[192,128]{1,0:T(8,128)(2,1)S(1)} %pad_maximum_fusion.refs_0_.refs_4_), channel_id=1, source_target_pairs={{0,6},{2,0},{4,2},{6,4},{1,7},{3,1},{5,3},{7,5},{8,14},{10,8},{12,... | collective-permute-start | bytes 147464 | tf_op jit(solution)/shard_map/ppermute | solution.py:213
  5.9 6.0 %collective-permute-start.1 = (bf16[192,128]{1,0:T(8,128)(2,1)S(1)}, bf16[192,128]{1,0:T(8,128)(2,1)S(1)}, u32[]{:S(2)}, u32[]{:S(2)}) collective-permute-start(bf16[192,128]{1,0:T(8,128)(2,1)S(1)} %pad_maximum_fusion.refs_0_.refs_4_), channel_id=1, source_target_pairs={{0,4},{2,6},{4,0},{6,2},{1,5},{3,7},{5,1},{7,3},{8,12},{10,14},{12... | collective-permute-start | bytes 147464 | tf_op jit(solution)/shard_map/ppermute | solution.py:213
  5.9 6.0 %collective-permute-start = (bf16[192,128]{1,0:T(8,128)(2,1)S(1)}, bf16[192,128]{1,0:T(8,128)(2,1)S(1)}, u32[]{:S(2)}, u32[]{:S(2)}) collective-permute-start(bf16[192,128]{1,0:T(8,128)(2,1)S(1)} %pad_maximum_fusion.refs_0_.refs_4_), channel_id=1, source_target_pairs={{0,2},{2,4},{4,6},{6,0},{1,3},{3,5},{5,7},{7,1},{8,10},{10,12},{12... | collective-permute-start | bytes 147464 | tf_op jit(solution)/shard_map/ppermute | solution.py:213
  11.9 3.4 %copy-start = (bf16[256,128,128]{2,1,0:T(8,128)(2,1)S(1)}, bf16[256,128,128]{2,1,0:T(8,128)(2,1)}, u32[]{:S(2)}) copy-start(bf16[256,128,128]{2,1,0:T(8,128)(2,1)} %block.1) | copy-start | bytes 25165828
  22.4 1.4 %collective-permute-start.4 = (f32[4,32,256]{2,1,0:T(8,128)S(1)}, f32[4,32,256]{2,1,0:T(8,128)S(1)}, u32[]{:S(2)}, u32[]{:S(2)}) collective-permute-start(f32[4,32,256]{2,1,0:T(8,128)S(1)} %slice_bitcast_fusion), channel_id=1, source_target_pairs={{0,1},{1,0},{2,3},{3,2},{4,5},{5,4},{6,7},{7,6},{8,9},{9,8},{10,11... | collective-permute-start | bytes 393224 | tf_op jit(solution)/shard_map/ppermute | solution.py:218
  22.5 3.3 %collective-permute-start.10 = (bf16[192,128]{1,0:T(8,128)(2,1)S(1)}, bf16[192,128]{1,0:T(8,128)(2,1)S(1)}, u32[]{:S(2)}, u32[]{:S(2)}) collective-permute-start(bf16[192,128]{1,0:T(8,128)(2,1)S(1)} %collective-permute-done.2.refs_3_.refs_6_), channel_id=1, source_target_pairs={{0,1},{1,0},{2,3},{3,2},{4,5},{5,4},{6,7},{7,6},{8,9},{9,8},{10,11... | collective-permute-start | bytes 147464 | tf_op jit(solution)/shard_map/ppermute | solution.py:214
  23.0 4.6 %collective-permute-start.9 = (bf16[192,128]{1,0:T(8,128)(2,1)S(1)}, bf16[192,128]{1,0:T(8,128)(2,1)S(1)}, u32[]{:S(2)}, u32[]{:S(2)}) collective-permute-start(bf16[192,128]{1,0:T(8,128)(2,1)S(1)} %collective-permute-done.1.refs_2_.refs_4_), channel_id=1, source_target_pairs={{0,1},{1,0},{2,3},{3,2},{4,5},{5,4},{6,7},{7,6},{8,9},{9,8},{10,11... | collective-permute-start | bytes 147464 | tf_op jit(solution)/shard_map/ppermute | solution.py:214
  23.1 4.5 %collective-permute-start.8 = (bf16[192,128]{1,0:T(8,128)(2,1)S(1)}, bf16[192,128]{1,0:T(8,128)(2,1)S(1)}, u32[]{:S(2)}, u32[]{:S(2)}) collective-permute-start(bf16[192,128]{1,0:T(8,128)(2,1)S(1)} %collective-permute-done.refs_1_.refs_2_), channel_id=1, source_target_pairs={{0,1},{1,0},{2,3},{3,2},{4,5},{5,4},{6,7},{7,6},{8,9},{9,8},{10,11... | collective-permute-start | bytes 147464 | tf_op jit(solution)/shard_map/ppermute | solution.py:214
  23.9 10.7 %collective-permute-start.7 = (f32[32,256]{1,0:T(8,128)S(1)}, f32[32,256]{1,0:T(8,128)S(1)}, u32[]{:S(2)}, u32[]{:S(2)}) collective-permute-start(f32[32,256]{1,0:T(8,128)S(1)} %get-tuple-element.11), channel_id=1, source_target_pairs={{0,6},{2,0},{4,2},{6,4},{1,7},{3,1},{5,3},{7,5},{8,14},{10,8},{12,... | collective-permute-start | bytes 98312 | tf_op jit(solution)/shard_map/ppermute | solution.py:219
  25.8 8.8 %collective-permute-start.6 = (f32[32,256]{1,0:T(8,128)S(1)}, f32[32,256]{1,0:T(8,128)S(1)}, u32[]{:S(2)}, u32[]{:S(2)}) collective-permute-start(f32[32,256]{1,0:T(8,128)S(1)} %get-tuple-element.12), channel_id=1, source_target_pairs={{0,4},{2,6},{4,0},{6,2},{1,5},{3,7},{5,1},{7,3},{8,12},{10,14},{12... | collective-permute-start | bytes 98312 | tf_op jit(solution)/shard_map/ppermute | solution.py:219
  25.8 8.8 %collective-permute-start.5 = (f32[32,256]{1,0:T(8,128)S(1)}, f32[32,256]{1,0:T(8,128)S(1)}, u32[]{:S(2)}, u32[]{:S(2)}) collective-permute-start(f32[32,256]{1,0:T(8,128)S(1)} %get-tuple-element.13), channel_id=1, source_target_pairs={{0,2},{2,4},{4,6},{6,0},{1,3},{3,5},{5,7},{7,1},{8,10},{10,12},{12... | collective-permute-start | bytes 98312 | tf_op jit(solution)/shard_map/ppermute | solution.py:219

commit v2 on v0

v2 whole, which is shorter than its diff:
```python
import functools

import jax
import jax.numpy as jnp
from jax import lax
from jax.experimental import pallas as pl
from jax.experimental.pallas import tpu as pltpu
from jax.sharding import PartitionSpec as P

ridge_weight = 0.1
exact = lax.Precision.HIGHEST
vmem = pl.BlockSpec(memory_space=pltpu.VMEM)
smem = pl.BlockSpec(memory_space=pltpu.SMEM)
hbm = pl.BlockSpec(memory_space=pltpu.HBM)


def shift(n, s):
    return [(i, (i + s) % n) for i in range(n)]


def wrap(x, n):
    return lax.rem(x + n, n)


def owner(nj, nk, where, t, u):
    return wrap(where[0] + u, nj) * nk + wrap(where[1] + t, nk)


def fetch_kernel(nj, nk, where, block, held, arrived):
    owned = held.shape[2]
    copies = []
    for t in range(nk):
        for u in range(nj):
            first = pl.multiple_of(owner(nj, nk, where, t, u) * owned, owned)
            copies.append(
                pltpu.make_async_copy(
                    block.at[pl.ds(first, owned)], held.at[t, u], arrived.at[t * nj + u]
                )
            )
    for copy in copies:
        copy.start()
    for copy in copies:
        copy.wait()


def fetch(where, tensor, nj, nk):
    rows, width_j, width_k = tensor.shape
    owned = rows // (nj * nk)
    return pl.pallas_call(
        functools.partial(fetch_kernel, nj, nk),
        out_shape=jax.ShapeDtypeStruct((nk, nj, owned, width_j, width_k), tensor.dtype),
        in_specs=[smem, hbm],
        out_specs=vmem,
        scratch_shapes=[pltpu.SemaphoreType.DMA((nj * nk,))],
        compiler_params=pltpu.CompilerParams(vmem_limit_bytes=20 * 2**20),
        cost_estimate=pl.CostEstimate(
            flops=4 * 10**9, bytes_accessed=2 * rows * width_j * width_k, transcendentals=0
        ),
    )(where, tensor)


def contract(held, t, out, c_wide, b_wide):
    nj, owned = held.shape[1], held.shape[2]

    def step(u, _):
        sums = []
        for i in range(owned):
            inner = jnp.dot(held[t, u, i], c_wide, preferred_element_type=jnp.float32)
            sums.append(jnp.sum(inner * b_wide, axis=0, keepdims=True))
        out[u] = jnp.concatenate(sums, axis=0)
        return 0

    lax.fori_loop(0, nj, step, 0)


def away_kernel(nj, nk, height_b, flipped, where, held, *refs):
    line, refs = refs[:nj], refs[nj:]
    b_parts, refs = refs[:nk], refs[nk:]
    out, c_out, b_out, c_cols, b_cols, b_rows = refs
    width_c = line[0].shape[0] - height_b
    for s in range(nj):
        at = pl.multiple_of(wrap(where[0] - s, nj) * width_c, width_c)
        c_out[pl.ds(at, width_c), :] = line[s][height_b:, :]
        b_out[s] = line[s][:height_b, :]
    for t in range(nk):
        if flipped:
            at = pl.multiple_of(wrap(where[1] - t, nk) * height_b, height_b)
            b_rows[pl.ds(at, height_b), :] = b_parts[t][:height_b, :]
        else:
            at = pl.multiple_of(wrap(where[1] - t, nk) * 128, 128)
            b_rows[:, pl.ds(at, 128)] = b_parts[t][:height_b, :]
    c_cols[...] = c_out[...].T
    b_cols[...] = (b_rows[...].T if flipped else b_rows[...]).astype(jnp.float32)
    for t in range(1, nk):
        contract(held, t, out.at[t - 1], c_cols[...], b_cols[...])


def home_kernel(held, c_cols, b_cols, out):
    contract(held, 0, out, c_cols[...], b_cols[...])


def mttkrp(where, held, line, b_parts, height_b, flipped, rank):
    nk, nj, owned, width_j, width_k = held.shape
    flops = 2 * nj * owned * width_j * width_k * rank
    params = pltpu.CompilerParams(vmem_limit_bytes=20 * 2**20)

    def cost(count):
        return pl.CostEstimate(flops=count * flops, bytes_accessed=2**20, transcendentals=0)

    away, c_own, b_own, c_cols, b_cols = pl.pallas_call(
        functools.partial(away_kernel, nj, nk, height_b, flipped),
        out_shape=[
            jax.ShapeDtypeStruct((nk - 1, nj, owned, rank), jnp.float32),
            jax.ShapeDtypeStruct((rank, width_k), held.dtype),
            jax.ShapeDtypeStruct((nj, height_b, line[0].shape[1]), held.dtype),
            jax.ShapeDtypeStruct((width_k, rank), held.dtype),
            jax.ShapeDtypeStruct((width_j, rank), jnp.float32),
        ],
        in_specs=[smem] + [vmem] * (1 + nj + nk),
        out_specs=[vmem] * 5,
        scratch_shapes=[pltpu.VMEM((rank, width_j) if flipped else (width_j, rank), held.dtype)],
        compiler_params=params,
        cost_estimate=cost(nk - 1),
    )(where, held, *line, *b_parts)
    home = pl.pallas_call(
        home_kernel,
        out_shape=jax.ShapeDtypeStruct((nj, owned, rank), jnp.float32),
        in_specs=[vmem] * 3,
        out_specs=vmem,
        compiler_params=params,
        cost_estimate=cost(1),
    )(held, c_cols, b_cols)
    return home, away, c_own, b_own


def column(x, q):
    return jnp.broadcast_to(x[:, q : q + 1], x.shape)


def row(x, q):
    return jnp.broadcast_to(x[q : q + 1, :], x.shape)


def thirds(x):
    high = x.astype(jnp.bfloat16)
    x = x - high.astype(jnp.float32)
    middle = x.astype(jnp.bfloat16)
    return high, middle, (x - middle.astype(jnp.float32)).astype(jnp.bfloat16)


def stack(tiles):
    return jnp.concatenate([jnp.concatenate(r, axis=1) for r in tiles], axis=0)


def invert(a, step=16):
    size = a.shape[0]
    wide, per = size // 128, step // 8
    lane = lax.broadcasted_iota(jnp.int32, (8, 128), 1)
    sub = lax.broadcasted_iota(jnp.int32, (8, 128), 0)

    def tile(g, w):
        return a[8 * g : 8 * g + 8, 128 * w : 128 * w + 128]

    def columns(rows, w, first):
        return [[column(r[w], first + q) for r in rows] for q in range(step)]

    now = [[tile(g, w) for w in range(wide)] for g in range(per)]
    for first in range(0, size, step):
        g0, w0, lane0 = first // 8, first // 128, first % 128
        inside = (lane >= lane0) & (lane < lane0 + step)
        more = first + step < size
        panel = [list(r) for r in now]
        c = columns(now, w0, lane0)
        if more:
            ahead = [[tile(g0 + per + i, w) for w in range(wide)] for i in range(per)]
            ahead_c = columns(ahead, w0, lane0)
        scale = [jnp.zeros((8, 128), jnp.float32)] * per
        pivot = row(c[0][0], 0)
        for q in range(step):
            gq, sq = q // 8, q % 8
            here = sub == sq
            inv = 1.0 / pivot
            scale[gq] = jnp.where(here, inv, scale[gq])
            if q + 1 < step:
                gn, sn = (q + 1) // 8, (q + 1) % 8
                product = row(c[q][gn], sn) * row(c[q + 1][gq], sq)
                pivot = row(c[q + 1][gn], sn) - product * inv
            factor = [jnp.where(here, 0.0, c[q][i]) if i == gq else c[q][i] for i in range(per)]
            for i in range(per):
                unit = jnp.where(here, 1.0, 0.0) if i == gq else 0.0
                panel[i][w0] = jnp.where(lane == lane0 + q, unit, panel[i][w0])
            for w in range(wide):
                scaled = row(panel[gq][w], sq) * inv
                for i in range(per):
                    panel[i][w] = panel[i][w] - factor[i] * scaled
            for p in range(q + 1, step):
                scaled = row(c[p][gq], sq) * inv
                for i in range(per):
                    c[p][i] = c[p][i] - factor[i] * scaled
        done = [[panel[i][w] * scale[i] for w in range(wide)] for i in range(per)]
        lanes = lax.broadcasted_iota(jnp.int32, (step, size), 1)
        left = stack(now)
        left = thirds(jnp.where(lanes < first, -left, left))
        right = thirds(stack(done))
        pairs = ((0, 0), (0, 1), (1, 0), (0, 2), (1, 1), (2, 0))
        update = lax.dot_general(
            jnp.concatenate([left[i] for i, _ in pairs], axis=0),
            jnp.concatenate([right[i] for _, i in pairs], axis=0),
            (((0,), (0,)), ((), ())),
            preferred_element_type=jnp.float32,
        )
        if more:
            now = []
            for i in range(per):
                fresh = []
                for w in range(wide):
                    spread = ahead_c[0][i] * row(done[0][w], 0)
                    for q in range(1, step):
                        spread = spread + ahead_c[q][i] * row(done[q // 8][w], q % 8)
                    base = ahead[i][w]
                    base = jnp.where(inside, 0.0, base) if w == w0 else base
                    fresh.append(base - spread)
                now.append(fresh)
        for g in range(size // 8):
            for w in range(wide):
                if g0 <= g < g0 + per:
                    value = done[g - g0][w]
                elif more and g0 + per <= g < g0 + 2 * per:
                    value = now[g - g0 - per][w]
                else:
                    value = tile(g, w)
                    value = jnp.where(inside, 0.0, value) if w == w0 else value
                    value = value - update[8 * g : 8 * g + 8, 128 * w : 128 * w + 128]
                a[8 * g : 8 * g + 8, 128 * w : 128 * w + 128] = value


def inverse_kernel(nj, nk, height_b, flipped, where, *refs):
    c_parts, refs = refs[:nk], refs[nk:]
    b_parts, refs = refs[:nk], refs[nk:]
    out, b_all = refs

    def gram(x, contracted):
        dims = (((contracted,), (contracted,)), ((), ()))
        return lax.dot_general(x, x, dims, preferred_element_type=jnp.float32)

    for t in range(nk):
        if flipped:
            at = pl.multiple_of(wrap(where[1] - t, nk) * height_b, height_b)
            b_all[:, pl.ds(at, height_b), :] = b_parts[t][...]
        else:
            at = pl.multiple_of(wrap(where[1] - t, nk) * 128, 128)
            b_all[:, :, pl.ds(at, 128)] = b_parts[t][...]
    if flipped:
        gram_b = sum(gram(b_all[s], 1) for s in range(nj))
    else:
        gram_b = gram(b_all[...].reshape(nj * height_b, out.shape[1]), 0)
    gram_c = sum(gram(part[...], 1) for part in c_parts)
    diagonal = lax.broadcasted_iota(jnp.int32, out.shape, 0) == lax.broadcasted_iota(
        jnp.int32, out.shape, 1
    )
    out[...] = gram_b * gram_c + jnp.where(diagonal, ridge_weight, 0.0)
    invert(out)


def solve_kernel(*refs):
    rows, (inverse, out) = refs[:-2], refs[-2:]
    mine = rows[0][...]
    for r in rows[1:]:
        mine = mine + r[...]
    out[...] = jnp.dot(mine, inverse[...], precision=exact, preferred_element_type=jnp.float32)


def body(tensor, factor_b, factor_c):
    nj, nk = lax.axis_size("ja"), lax.axis_size("ka")
    where = jnp.stack([lax.axis_index("ja"), lax.axis_index("ka")]).astype(jnp.int32)
    rank = factor_b.shape[1] * nk
    flipped = factor_b.shape[1] % 128 != 0
    part_b = factor_b.T if flipped else factor_b
    height_b = part_b.shape[0]
    mine = jnp.concatenate([part_b, factor_c.T], axis=0)
    line = [mine] + [lax.ppermute(mine, "ja", shift(nj, s)) for s in range(1, nj)]
    b_parts = [mine] + [lax.ppermute(mine, "ka", shift(nk, t)) for t in range(1, nk)]
    held = fetch(where, tensor, nj, nk)
    total, away, c_own, b_own = mttkrp(where, held, line, b_parts, height_b, flipped, rank)
    c_parts = [c_own] + [lax.ppermute(c_own, "ka", shift(nk, t)) for t in range(1, nk)]
    b_parts = [b_own] + [lax.ppermute(b_own, "ka", shift(nk, t)) for t in range(1, nk)]
    for t in range(1, nk):
        total = total + lax.ppermute(away[t - 1], "ka", shift(nk, t))
    rows = [total[0]] + [lax.ppermute(total[u], "ja", shift(nj, u)) for u in range(1, nj)]
    b_shape = (nj, rank, part_b.shape[1]) if flipped else (nj, height_b, rank)
    inverse = pl.pallas_call(
        functools.partial(inverse_kernel, nj, nk, height_b, flipped),
        out_shape=jax.ShapeDtypeStruct((rank, rank), jnp.float32),
        in_specs=[smem] + [vmem] * (2 * nk),
        out_specs=vmem,
        scratch_shapes=[pltpu.VMEM(b_shape, factor_b.dtype)],
        compiler_params=pltpu.CompilerParams(vmem_limit_bytes=20 * 2**20),
        cost_estimate=pl.CostEstimate(flops=10**10, bytes_accessed=2**20, transcendentals=0),
    )(where, *c_parts, *b_parts)
    return pl.pallas_call(
        solve_kernel,
        out_shape=jax.ShapeDtypeStruct((rows[0].shape[0], rank), jnp.float32),
        in_specs=[vmem] * (len(rows) + 1),
        out_specs=vmem,
        compiler_params=pltpu.CompilerParams(vmem_limit_bytes=20 * 2**20),
        cost_estimate=pl.CostEstimate(flops=10**8, bytes_accessed=2**19, transcendentals=0),
    )(*rows, inverse)


def solution(mesh):
    placed = (P("ia", "ja", "ka"), P("ja", "ka"), P("ka", "ja"))
    return jax.shard_map(
        body, mesh=mesh, in_specs=placed, out_specs=P(("ia", "ja", "ka"), None), check_vma=False
    )
```

time: 143 us -> 30.3 us (0.21)
  other arithmetic: 55.8 us -> 0.88 us
  matrix products: 28.6 us -> 0 us
  blocking collectives: 17.4 us -> 0 us
  between operations: 16.3 us -> 0.11 us
  Pallas kernels: 0 us -> 14.9 us
  local copies, waits for them, and re-layouts: 14.6 us -> 3.39 us
  starting transfers between devices: 0.09 us -> 10.5 us
  waiting for transfers between devices: 9.01 us -> 0.36 us
    another operation x9 -> x1, other arithmetic: 53.9 us -> 0.07 us  [body(): jnp.stack([lax.axis_index('ja'), lax.axis_index('ka')]).astype(jnp.int32)]
    dot_general x18 -> x0, matrix products: 25.4 us -> none  [the longest x16 23.6 us: contract(): jnp.dot(block.reshape(rows * width_j, width_k), c_wide, preferred_element...]
    all_gather x2 -> x0, blocking collectives: 17.4 us -> none  [the longest x1 15.2 us: body(): c_wide = lax.all_gather(factor_c, 'ja', axis=1, tiled=True)]
    pallas_call x0 -> x5, Pallas kernels: none -> 14.9 us  [the longest x1 6.48 us: body(): pl.pallas_call(functools.partial(inverse_kernel, nj, nk, height_b, flippe...]
    ppermute x0 -> x10, starting transfers between devices: none -> 10.5 us  [the longest x3 5.62 us: body(): lax.ppermute(mine, 'ja', shift(nj, s))]
    dynamic_update_slice x16 -> x0, local copies, waits for them, and re-layouts: 9.71 us -> none  [partial_rows(): result = lax.map(lambda piece: contract(piece, b_wide, c_wide), pieces)]
    psum x2 -> x0, waiting for transfers between devices: 8.94 us -> none  [the longest x1 8.92 us: body(): lax.psum(jnp.dot(c_wide.T, c_wide, preferred_element_type=jnp.float32), '...]
    another operation x18 -> x0, local copies, waits for them, and re-layouts: 4.61 us -> none
  transfers between devices with their start and end apart: 3 -> 10, of which waited for: 1 -> 1; matrix products, arithmetic and copies ran while one was open for 67% -> 0% of each run, Pallas kernels for 0% -> 35%
where the time goes in v2:
time: 30.3 us; the launch traced here: 30.1 us
  Pallas kernels  14.9 us (49%)
  starting transfers between devices  10.5 us (35%)
  local copies, waits for them, and re-layouts  3.39 us (11%)
  other arithmetic  0.88 us (3%)
  waiting for transfers between devices  0.36 us (1%)
    pallas_call x1, Pallas kernels, body(): pl.pallas_call(functools.partial(inverse_kernel, nj, nk, height_b, flippe...  6.48 us
    ppermute x3, starting transfers between devices, body(): lax.ppermute(mine, 'ja', shift(nj, s))  5.62 us
    ppermute x3, starting transfers between devices, body(): lax.ppermute(total[u], 'ja', shift(nj, u))  3.7 us
    pallas_call x1, Pallas kernels, mttkrp(): pl.pallas_call(functools.partial(away_kernel, nj, nk, height_b, flipped),...  3.46 us
    unnamed x2, local copies, waits for them, and re-layouts  3.38 us
    pallas_call x1, Pallas kernels, mttkrp(): pl.pallas_call(home_kernel, out_shape=jax.ShapeDtypeStruct((nj, owned, ra...  2.87 us
    pallas_call x1, Pallas kernels, fetch(): pl.pallas_call(functools.partial(fetch_kernel, nj, nk), out_shape=jax.Sha...  1.21 us
    pallas_call x1, Pallas kernels, body(): pl.pallas_call(solve_kernel, out_shape=jax.ShapeDtypeStruct((rows[0].shap...  0.85 us
  transfers between devices with their start and end apart: 10, of which 1 were waited for; matrix products, arithmetic and copies ran while one was open for 0% of the time, Pallas kernels for 35%

profile of v2, /device:TPU:0, one launch (start us, length us, event | category | flops | bytes accessed | tf_op | source)
XLA Modules:
  0.0 30.1 jit_solution(17449572680948851461)
XLA Ops:
  0.0 0.8 %pad_maximum_fusion.refs_0_.refs_4_ = bf16[192,128]{1,0:T(8,128)(2,1)S(1)} fusion(bf16[64,128]{1,0:T(8,128)(2,1)} %bitcast.13, bf16[128,128]{1,0:T(8,128)(2,1)} %param.4), kind=kLoop, calls=%fused_computation | loop fusion | flops 98304 | bytes 98304 | tf_op jit(solution)/shard_map/concatenate | solution.py:280
  0.8 0.5 %collective-permute-start.3 = (bf16[192,128]{1,0:T(8,128)(2,1)S(1)}, bf16[192,128]{1,0:T(8,128)(2,1)S(1)}, u32[]{:S(2)}, u32[]{:S(2)}) collective-permute-start(bf16[192,128]{1,0:T(8,128)(2,1)S(1)} %pad_maximum_fusion.refs_0_.refs_4_), channel_id=1, source_target_pairs={{0,1},{1,0},{2,3},{3,2},{4,5},{5,4},{6,7},{7,6},{8,9},{9,8},{10,11... | collective-permute-start | bytes 147464 | tf_op jit(solution)/shard_map/ppermute | solution.py:282
  1.3 4.6 %collective-permute-start.2 = (bf16[192,128]{1,0:T(8,128)(2,1)S(1)}, bf16[192,128]{1,0:T(8,128)(2,1)S(1)}, u32[]{:S(2)}, u32[]{:S(2)}) collective-permute-start(bf16[192,128]{1,0:T(8,128)(2,1)S(1)} %pad_maximum_fusion.refs_0_.refs_4_), channel_id=1, source_target_pairs={{0,6},{2,0},{4,2},{6,4},{1,7},{3,1},{5,3},{7,5},{8,14},{10,8},{12,... | collective-permute-start | bytes 147464 | tf_op jit(solution)/shard_map/ppermute | solution.py:281
  5.9 1.0 %collective-permute-start = (bf16[192,128]{1,0:T(8,128)(2,1)S(1)}, bf16[192,128]{1,0:T(8,128)(2,1)S(1)}, u32[]{:S(2)}, u32[]{:S(2)}) collective-permute-start(bf16[192,128]{1,0:T(8,128)(2,1)S(1)} %pad_maximum_fusion.refs_0_.refs_4_), channel_id=1, source_target_pairs={{0,2},{2,4},{4,6},{6,0},{1,3},{3,5},{5,7},{7,1},{8,10},{10,12},{12... | collective-permute-start | bytes 147464 | tf_op jit(solution)/shard_map/ppermute | solution.py:281
  6.9 0.1 pad_add_fusion.where
  7.0 3.4 %copy-done = bf16[256,128,128]{2,1,0:T(8,128)(2,1)S(1)} copy-done((bf16[256,128,128]{2,1,0:T(8,128)(2,1)S(1)}, bf16[256,128,128]{2,1,0:T(8,128)(2,1)}, u32[]{:S(2)}) %copy-start) | copy-done | bytes 8388632
  10.4 1.2 %shard_map.37.held = bf16[2,4,32,128,128]{4,3,2,1,0:T(8,128)(2,1)S(1)} custom-call(s32[2]{0:T(128)S(1)} %pad_add_fusion.where, bf16[256,128,128]{2,1,0:T(8,128)(2,1)S(1)} %copy-done), custom_call_target="tpu_custom_call" | custom-call | flops 4000000000 | bytes 8388608 | tf_op jit(solution)/shard_map/pallas_call | solution.py:49
  11.6 0.0 collective-permute-done.3.refs_5_
  11.6 0.3 %collective-permute-done.1.refs_2_ = bf16[192,128]{1,0:T(8,128)(2,1)S(1)} collective-permute-done((bf16[192,128]{1,0:T(8,128)(2,1)S(1)}, bf16[192,128]{1,0:T(8,128)(2,1)S(1)}, u32[]{:S(2)}, u32[]{:S(2)}) %collective-permute-start.1) | collective-permute-done | bytes 49184 | tf_op jit(solution)/shard_map/ppermute | solution.py:281
  11.9 0.0 collective-permute-done.refs_1_
  11.9 3.5 %shard_map.38 = (f32[1,4,32,256]{3,2,1,0:T(8,128)S(1)}, bf16[256,128]{1,0:T(8,128)(2,1)S(1)}, bf16[4,128,128]{2,1,0:T(8,128)(2,1)S(1)}, bf16[128,256]{1,0:T(8,128)(2,1)S(1)}, f32[128,256]{1,0:T(8,128)S(1)}) custom-call(s32[2]{0:T(128)S(1)} %pad_add_fusion.where, bf16[2,4,32,128,128]{4,3,2,1,0:T(8,128)(2,1)S(1)} %shard_map.37.held, ...), custom_call_target="tpu_custom_call" | custom-call | flops 1073741824 | bytes 1048576 | tf_op jit(solution)/shard_map/pallas_call | solution.py:110
  15.4 0.1 collective-permute-start.4
  15.5 0.5 %collective-permute-start.8 = (bf16[256,128]{1,0:T(8,128)(2,1)S(1)}, bf16[256,128]{1,0:T(8,128)(2,1)S(1)}, u32[]{:S(2)}, u32[]{:S(2)}) collective-permute-start(bf16[256,128]{1,0:T(8,128)(2,1)S(1)} %get-tuple-element.13.refs_0_), channel_id=1, source_target_pairs={{0,1},{1,0},{2,3},{3,2},{4,5},{5,4},{6,7},{7,6},{8,9},{9,8},{10,11... | collective-permute-start | bytes 196616 | tf_op jit(solution)/shard_map/ppermute | solution.py:285
  16.0 0.1 collective-permute-start.9
  16.1 2.9 %shard_map.39 = f32[4,32,256]{2,1,0:T(8,128)S(1)} custom-call(bf16[2,4,32,128,128]{4,3,2,1,0:T(8,128)(2,1)S(1)} %shard_map.37.held, bf16[128,256]{1,0:T(8,128)(2,1)S(1)} %get-tuple-element.10.c_cols, f32[128,256]{1,0:T(8,128)S(1)} %get-tuple-element.11.b_cols), custom_call_target="tpu_custom_call" | custom-call | flops 1073741824 | bytes 1048576 | tf_op jit(solution)/shard_map/pallas_call | solution.py:125
  19.0 2.5 %collective-permute-start.7 = (f32[32,256]{1,0:T(8,128)S(1)}, f32[32,256]{1,0:T(8,128)S(1)}, u32[]{:S(2)}, u32[]{:S(2)}) collective-permute-start(f32[32,256]{1,0:T(8,128)S(1)} %get-tuple-element.15), channel_id=1, source_target_pairs={{0,6},{2,0},{4,2},{6,4},{1,7},{3,1},{5,3},{7,5},{8,14},{10,8},{12,... | collective-permute-start | bytes 98312 | tf_op jit(solution)/shard_map/ppermute | solution.py:289
  21.5 1.1 %collective-permute-start.6 = (f32[32,256]{1,0:T(8,128)S(1)}, f32[32,256]{1,0:T(8,128)S(1)}, u32[]{:S(2)}, u32[]{:S(2)}) collective-permute-start(f32[32,256]{1,0:T(8,128)S(1)} %get-tuple-element.16), channel_id=1, source_target_pairs={{0,4},{2,6},{4,0},{6,2},{1,5},{3,7},{5,1},{7,3},{8,12},{10,14},{12... | collective-permute-start | bytes 98312 | tf_op jit(solution)/shard_map/ppermute | solution.py:289
  22.7 0.0 collective-permute-start.5
  22.7 0.0 collective-permute-done.8.refs_1_
  22.7 0.0 collective-permute-done.9.refs_3_
  22.7 6.5 %shard_map.40.refs_4_ = f32[256,256]{1,0:T(8,128)S(1)} custom-call(s32[2]{0:T(128)S(1)} %pad_add_fusion.where, bf16[256,128]{1,0:T(8,128)(2,1)S(1)} %get-tuple-element.13.refs_0_, bf16[256,128]{1,0:T(8,128)(2,1)S(1)} %collective-permute-done.8.refs_1_, bf16[4,128,128]{2,1,0:T(8,128)(2,1)S(1)} %get-tuple-element.14.refs_2_, ...), custom_call_target="tpu_custom_call" | custom-call | flops 10000000000 | bytes 1048576 | tf_op jit(solution)/shard_map/pallas_call | solution.py:291
  29.2 0.0 collective-permute-done.7.refs_3_
  29.2 0.0 collective-permute-done.5.refs_1_
  29.2 0.9 %shard_map.41 = f32[32,256]{1,0:T(8,128)} custom-call(f32[32,256]{1,0:T(8,128)S(1)} %get-tuple-element.18.refs_0_, f32[32,256]{1,0:T(8,128)S(1)} %collective-permute-done.5.refs_1_, f32[32,256]{1,0:T(8,128)S(1)} %collective-permute-done.6.refs_2_, f32[32,256]{1,0:T(8,128)S(1)} %collective-permute-done.7.refs_3_, f32[256,256]{1,0:T(8,128)S(1)} %shard_map.40.refs_4_), custom_call_target="tpu_custom_call" | custom-call | flops 100000000 | bytes 524288 | tf_op jit(solution)/shard_map/pallas_call | solution.py:300
  (7 shorter events, 0.0 us)
Async XLA Ops:
  0.8 10.8 %collective-permute-start.3 = (bf16[192,128]{1,0:T(8,128)(2,1)S(1)}, bf16[192,128]{1,0:T(8,128)(2,1)S(1)}, u32[]{:S(2)}, u32[]{:S(2)}) collective-permute-start(bf16[192,128]{1,0:T(8,128)(2,1)S(1)} %pad_maximum_fusion.refs_0_.refs_4_), channel_id=1, source_target_pairs={{0,1},{1,0},{2,3},{3,2},{4,5},{5,4},{6,7},{7,6},{8,9},{9,8},{10,11... | collective-permute-start | bytes 147464 | tf_op jit(solution)/shard_map/ppermute | solution.py:282
  1.3 10.3 %collective-permute-start.2 = (bf16[192,128]{1,0:T(8,128)(2,1)S(1)}, bf16[192,128]{1,0:T(8,128)(2,1)S(1)}, u32[]{:S(2)}, u32[]{:S(2)}) collective-permute-start(bf16[192,128]{1,0:T(8,128)(2,1)S(1)} %pad_maximum_fusion.refs_0_.refs_4_), channel_id=1, source_target_pairs={{0,6},{2,0},{4,2},{6,4},{1,7},{3,1},{5,3},{7,5},{8,14},{10,8},{12,... | collective-permute-start | bytes 147464 | tf_op jit(solution)/shard_map/ppermute | solution.py:281
  5.9 6.0 %collective-permute-start.1 = (bf16[192,128]{1,0:T(8,128)(2,1)S(1)}, bf16[192,128]{1,0:T(8,128)(2,1)S(1)}, u32[]{:S(2)}, u32[]{:S(2)}) collective-permute-start(bf16[192,128]{1,0:T(8,128)(2,1)S(1)} %pad_maximum_fusion.refs_0_.refs_4_), channel_id=1, source_target_pairs={{0,4},{2,6},{4,0},{6,2},{1,5},{3,7},{5,1},{7,3},{8,12},{10,14},{12... | collective-permute-start | bytes 147464 | tf_op jit(solution)/shard_map/ppermute | solution.py:281
  5.9 6.0 %collective-permute-start = (bf16[192,128]{1,0:T(8,128)(2,1)S(1)}, bf16[192,128]{1,0:T(8,128)(2,1)S(1)}, u32[]{:S(2)}, u32[]{:S(2)}) collective-permute-start(bf16[192,128]{1,0:T(8,128)(2,1)S(1)} %pad_maximum_fusion.refs_0_.refs_4_), channel_id=1, source_target_pairs={{0,2},{2,4},{4,6},{6,0},{1,3},{3,5},{5,7},{7,1},{8,10},{10,12},{12... | collective-permute-start | bytes 147464 | tf_op jit(solution)/shard_map/ppermute | solution.py:281
  7.0 3.4 %copy-start = (bf16[256,128,128]{2,1,0:T(8,128)(2,1)S(1)}, bf16[256,128,128]{2,1,0:T(8,128)(2,1)}, u32[]{:S(2)}) copy-start(bf16[256,128,128]{2,1,0:T(8,128)(2,1)} %block.1) | copy-start | bytes 25165828
  15.4 3.5 %collective-permute-start.4 = (f32[4,32,256]{2,1,0:T(8,128)S(1)}, f32[4,32,256]{2,1,0:T(8,128)S(1)}, u32[]{:S(2)}, u32[]{:S(2)}) collective-permute-start(f32[4,32,256]{2,1,0:T(8,128)S(1)} %bitcast.12), channel_id=1, source_target_pairs={{0,1},{1,0},{2,3},{3,2},{4,5},{5,4},{6,7},{7,6},{8,9},{9,8},{10,11... | collective-permute-start | bytes 393224 | tf_op jit(solution)/shard_map/ppermute | solution.py:288
  15.5 7.2 %collective-permute-start.8 = (bf16[256,128]{1,0:T(8,128)(2,1)S(1)}, bf16[256,128]{1,0:T(8,128)(2,1)S(1)}, u32[]{:S(2)}, u32[]{:S(2)}) collective-permute-start(bf16[256,128]{1,0:T(8,128)(2,1)S(1)} %get-tuple-element.13.refs_0_), channel_id=1, source_target_pairs={{0,1},{1,0},{2,3},{3,2},{4,5},{5,4},{6,7},{7,6},{8,9},{9,8},{10,11... | collective-permute-start | bytes 196616 | tf_op jit(solution)/shard_map/ppermute | solution.py:285
  16.0 6.7 %collective-permute-start.9 = (bf16[4,128,128]{2,1,0:T(8,128)(2,1)S(1)}, bf16[4,128,128]{2,1,0:T(8,128)(2,1)S(1)}, u32[]{:S(2)}, u32[]{:S(2)}) collective-permute-start(bf16[4,128,128]{2,1,0:T(8,128)(2,1)S(1)} %get-tuple-element.14.refs_2_), channel_id=1, source_target_pairs={{0,1},{1,0},{2,3},{3,2},{4,5},{5,4},{6,7},{7,6},{8,9},{9,8},{10,11... | collective-permute-start | bytes 393224 | tf_op jit(solution)/shard_map/ppermute | solution.py:286
  19.0 10.2 %collective-permute-start.7 = (f32[32,256]{1,0:T(8,128)S(1)}, f32[32,256]{1,0:T(8,128)S(1)}, u32[]{:S(2)}, u32[]{:S(2)}) collective-permute-start(f32[32,256]{1,0:T(8,128)S(1)} %get-tuple-element.15), channel_id=1, source_target_pairs={{0,6},{2,0},{4,2},{6,4},{1,7},{3,1},{5,3},{7,5},{8,14},{10,8},{12,... | collective-permute-start | bytes 98312 | tf_op jit(solution)/shard_map/ppermute | solution.py:289
  21.5 7.7 %collective-permute-start.6 = (f32[32,256]{1,0:T(8,128)S(1)}, f32[32,256]{1,0:T(8,128)S(1)}, u32[]{:S(2)}, u32[]{:S(2)}) collective-permute-start(f32[32,256]{1,0:T(8,128)S(1)} %get-tuple-element.16), channel_id=1, source_target_pairs={{0,4},{2,6},{4,0},{6,2},{1,5},{3,7},{5,1},{7,3},{8,12},{10,14},{12... | collective-permute-start | bytes 98312 | tf_op jit(solution)/shard_map/ppermute | solution.py:289
  22.7 6.6 %collective-permute-start.5 = (f32[32,256]{1,0:T(8,128)S(1)}, f32[32,256]{1,0:T(8,128)S(1)}, u32[]{:S(2)}, u32[]{:S(2)}) collective-permute-start(f32[32,256]{1,0:T(8,128)S(1)} %get-tuple-element.17), channel_id=1, source_target_pairs={{0,2},{2,4},{4,6},{6,0},{1,3},{3,5},{5,7},{7,1},{8,10},{10,12},{12... | collective-permute-start | bytes 98312 | tf_op jit(solution)/shard_map/ppermute | solution.py:289

commit v3 on v2

--- a/solution.py
+++ b/solution.py
@@ -23,18 +23,25 @@
 
 
 def owner(nj, nk, where, t, u):
-    return wrap(where[0] + u, nj) * nk + wrap(where[1] + t, nk)
+    return lax.bitwise_xor(where[0], u) * nk + wrap(where[1] + t, nk)
+
+
+def halving_order(nj):
+    order = [0]
+    while len(order) < nj:
+        order = [2 * u for u in order] + [2 * u + 1 for u in order]
+    return order
 
 
 def fetch_kernel(nj, nk, where, block, held, arrived):
     owned = held.shape[2]
     copies = []
     for t in range(nk):
-        for u in range(nj):
+        for slot, u in enumerate(halving_order(nj)):
             first = pl.multiple_of(owner(nj, nk, where, t, u) * owned, owned)
             copies.append(
                 pltpu.make_async_copy(
-                    block.at[pl.ds(first, owned)], held.at[t, u], arrived.at[t * nj + u]
+                    block.at[pl.ds(first, owned)], held.at[t, slot], arrived.at[t * nj + slot]
                 )
             )
     for copy in copies:
@@ -52,7 +59,7 @@
         in_specs=[smem, hbm],
         out_specs=vmem,
         scratch_shapes=[pltpu.SemaphoreType.DMA((nj * nk,))],
-        compiler_params=pltpu.CompilerParams(vmem_limit_bytes=20 * 2**20),
+        compiler_params=pltpu.CompilerParams(vmem_limit_bytes=42 * 2**20),
         cost_estimate=pl.CostEstimate(
             flops=4 * 10**9, bytes_accessed=2 * rows * width_j * width_k, transcendentals=0
         ),
@@ -62,15 +69,12 @@
 def contract(held, t, out, c_wide, b_wide):
     nj, owned = held.shape[1], held.shape[2]
 
-    def step(u, _):
+    for u in range(nj):
         sums = []
         for i in range(owned):
             inner = jnp.dot(held[t, u, i], c_wide, preferred_element_type=jnp.float32)
             sums.append(jnp.sum(inner * b_wide, axis=0, keepdims=True))
         out[u] = jnp.concatenate(sums, axis=0)
-        return 0
-
-    lax.fori_loop(0, nj, step, 0)
 
 
 def away_kernel(nj, nk, height_b, flipped, where, held, *refs):
@@ -152,7 +156,7 @@
     return jnp.concatenate([jnp.concatenate(r, axis=1) for r in tiles], axis=0)
 
 
-def invert(a, step=16):
+def invert(a, begin, end, step=16):
     size = a.shape[0]
     wide, per = size // 128, step // 8
     lane = lax.broadcasted_iota(jnp.int32, (8, 128), 1)
@@ -164,8 +168,8 @@
     def columns(rows, w, first):
         return [[column(r[w], first + q) for r in rows] for q in range(step)]
 
-    now = [[tile(g, w) for w in range(wide)] for g in range(per)]
-    for first in range(0, size, step):
+    now = [[tile(begin // 8 + g, w) for w in range(wide)] for g in range(per)]
+    for first in range(begin, end, step):
         g0, w0, lane0 = first // 8, first // 128, first % 128
         inside = (lane >= lane0) & (lane < lane0 + step)
         more = first + step < size
@@ -259,14 +263,16 @@
         jnp.int32, out.shape, 1
     )
     out[...] = gram_b * gram_c + jnp.where(diagonal, ridge_weight, 0.0)
-    invert(out)
-
-
-def solve_kernel(*refs):
-    rows, (inverse, out) = refs[:-2], refs[-2:]
-    mine = rows[0][...]
-    for r in rows[1:]:
-        mine = mine + r[...]
+    invert(out, 0, out.shape[0] // 2)
+
+
+def rest_kernel(half_done, out):
+    out[...] = half_done[...]
+    invert(out, out.shape[0] // 2, out.shape[0])
+
+
+def solve_kernel(kept, received, inverse, out):
+    mine = kept[0] + received[0]
     out[...] = jnp.dot(mine, inverse[...], precision=exact, preferred_element_type=jnp.float32)
 
 
@@ -286,25 +292,41 @@
     b_parts = [b_own] + [lax.ppermute(b_own, "ka", shift(nk, t)) for t in range(1, nk)]
     for t in range(1, nk):
         total = total + lax.ppermute(away[t - 1], "ka", shift(nk, t))
-    rows = [total[0]] + [lax.ppermute(total[u], "ja", shift(nj, u)) for u in range(1, nj)]
     b_shape = (nj, rank, part_b.shape[1]) if flipped else (nj, height_b, rank)
+    params = pltpu.CompilerParams(vmem_limit_bytes=20 * 2**20)
+    cost = pl.CostEstimate(flops=5 * 10**9, bytes_accessed=2**20, transcendentals=0)
+    square = jax.ShapeDtypeStruct((rank, rank), jnp.float32)
+    half_done = pl.pallas_call(
+        functools.partial(inverse_kernel, nj, nk, height_b, flipped),
+        out_shape=square,
+        in_specs=[smem] + [vmem] * (2 * nk),
+        out_specs=vmem,
+        scratch_shapes=[pltpu.VMEM(b_shape, factor_b.dtype)],
+        compiler_params=params,
+        cost_estimate=cost,
+    )(where, *c_parts, *b_parts)
+    bit = 1
+    while bit < nj:
+        kept, sent = jnp.split(total, 2, axis=0)
+        received = lax.ppermute(sent, "ja", [(i, i ^ bit) for i in range(nj)])
+        total = kept if 2 * bit == nj else kept + received
+        bit *= 2
     inverse = pl.pallas_call(
-        functools.partial(inverse_kernel, nj, nk, height_b, flipped),
-        out_shape=jax.ShapeDtypeStruct((rank, rank), jnp.float32),
-        in_specs=[smem] + [vmem] * (2 * nk),
-        out_specs=vmem,
-        scratch_shapes=[pltpu.VMEM(b_shape, factor_b.dtype)],
-        compiler_params=pltpu.CompilerParams(vmem_limit_bytes=20 * 2**20),
-        cost_estimate=pl.CostEstimate(flops=10**10, bytes_accessed=2**20, transcendentals=0),
-    )(where, *c_parts, *b_parts)
+        rest_kernel,
+        out_shape=square,
+        in_specs=[vmem],
+        out_specs=vmem,
+        compiler_params=params,
+        cost_estimate=cost,
+    )(half_done)
     return pl.pallas_call(
         solve_kernel,
-        out_shape=jax.ShapeDtypeStruct((rows[0].shape[0], rank), jnp.float32),
-        in_specs=[vmem] * (len(rows) + 1),
-        out_specs=vmem,
-        compiler_params=pltpu.CompilerParams(vmem_limit_bytes=20 * 2**20),
+        out_shape=jax.ShapeDtypeStruct(kept.shape[1:], jnp.float32),
+        in_specs=[vmem] * 3,
+        out_specs=vmem,
+        compiler_params=params,
         cost_estimate=pl.CostEstimate(flops=10**8, bytes_accessed=2**19, transcendentals=0),
-    )(*rows, inverse)
+    )(kept, received, inverse)
 
 
 def solution(mesh):

time: 30.3 us -> 29.8 us (0.983)
  local copies, waits for them, and re-layouts: 3.39 us -> 0.01 us
  waiting for transfers between devices: 0.36 us -> 2.35 us
  Pallas kernels: 14.9 us -> 16.8 us
  starting transfers between devices: 10.5 us -> 9.4 us
    unnamed x2 -> x0, local copies, waits for them, and re-layouts: 3.38 us -> none
    pallas_call x1, Pallas kernels: 1.21 us -> 4.02 us  [fetch(): pl.pallas_call(functools.partial(fetch_kernel, nj, nk), out_shape=jax.Sha...]
    pallas_call x1 -> x2, Pallas kernels: 0.85 us -> 3.67 us  [the longest x1 2.82 us: body(): pl.pallas_call(rest_kernel, out_shape=square, in_specs=[vmem], out_specs=...]
    pallas_call x1, Pallas kernels: 6.48 us -> 3.81 us  [body(): pl.pallas_call(functools.partial(inverse_kernel, nj, nk, height_b, flippe...]
    ppermute x3 -> x2, waiting for transfers between devices: 0.01 us -> 1.43 us  [body(): received = lax.ppermute(sent, 'ja', [(i, i ^ bit) for i in range(nj)])]
    ppermute x3 -> x2, starting transfers between devices: 3.7 us -> 2.64 us  [body(): received = lax.ppermute(sent, 'ja', [(i, i ^ bit) for i in range(nj)])]
    ppermute x3, waiting for transfers between devices: 0.34 us -> 0.91 us  [body(): lax.ppermute(mine, 'ja', shift(nj, s))]
    pallas_call x1, Pallas kernels: 2.87 us -> 2.36 us  [mttkrp(): pl.pallas_call(home_kernel, out_shape=jax.ShapeDtypeStruct((nj, owned, ra...]
  transfers between devices with their start and end apart: 10 -> 9, of which waited for: 1 -> 2; matrix products, arithmetic and copies ran while one was open for 0% -> 0% of each run, Pallas kernels for 35% -> 44%
where the time goes in v3:
time: 29.8 us; the launch traced here: 29.6 us
  Pallas kernels  16.8 us (56%)
  starting transfers between devices  9.4 us (32%)
  waiting for transfers between devices  2.35 us (8%)
  other arithmetic  0.88 us (3%)
    ppermute x3, starting transfers between devices, body(): lax.ppermute(mine, 'ja', shift(nj, s))  5.62 us
    pallas_call x1, Pallas kernels, fetch(): pl.pallas_call(functools.partial(fetch_kernel, nj, nk), out_shape=jax.Sha...  4.02 us
    pallas_call x1, Pallas kernels, body(): pl.pallas_call(functools.partial(inverse_kernel, nj, nk, height_b, flippe...  3.81 us
    pallas_call x1, Pallas kernels, mttkrp(): pl.pallas_call(functools.partial(away_kernel, nj, nk, height_b, flipped),...  2.97 us
    pallas_call x1, Pallas kernels, body(): pl.pallas_call(rest_kernel, out_shape=square, in_specs=[vmem], out_specs=...  2.82 us
    ppermute x2, starting transfers between devices, body(): received = lax.ppermute(sent, 'ja', [(i, i ^ bit) for i in range(nj)])  2.64 us
    pallas_call x1, Pallas kernels, mttkrp(): pl.pallas_call(home_kernel, out_shape=jax.ShapeDtypeStruct((nj, owned, ra...  2.36 us
    ppermute x2, waiting for transfers between devices, body(): received = lax.ppermute(sent, 'ja', [(i, i ^ bit) for i in range(nj)])  1.43 us
  transfers between devices with their start and end apart: 9, of which 2 were waited for; matrix products, arithmetic and copies ran while one was open for 0% of the time, Pallas kernels for 44%

profile of v3, /device:TPU:0, one launch (start us, length us, event | category | flops | bytes accessed | tf_op | source)
XLA Modules:
  0.0 29.6 jit_solution(2516450021623491947)
XLA Ops:
  0.0 0.8 %pad_maximum_fusion.refs_0_.refs_4_ = bf16[192,128]{1,0:T(8,128)(2,1)S(1)} fusion(bf16[64,128]{1,0:T(8,128)(2,1)} %bitcast.5, bf16[128,128]{1,0:T(8,128)(2,1)} %param.4), kind=kLoop, calls=%fused_computation.1 | loop fusion | flops 98304 | bytes 98304 | tf_op jit(solution)/shard_map/concatenate | solution.py:286
  0.8 0.5 %collective-permute-start.3 = (bf16[192,128]{1,0:T(8,128)(2,1)S(1)}, bf16[192,128]{1,0:T(8,128)(2,1)S(1)}, u32[]{:S(2)}, u32[]{:S(2)}) collective-permute-start(bf16[192,128]{1,0:T(8,128)(2,1)S(1)} %pad_maximum_fusion.refs_0_.refs_4_), channel_id=1, source_target_pairs={{0,1},{1,0},{2,3},{3,2},{4,5},{5,4},{6,7},{7,6},{8,9},{9,8},{10,11... | collective-permute-start | bytes 147464 | tf_op jit(solution)/shard_map/ppermute | solution.py:288
  1.3 4.6 %collective-permute-start.2 = (bf16[192,128]{1,0:T(8,128)(2,1)S(1)}, bf16[192,128]{1,0:T(8,128)(2,1)S(1)}, u32[]{:S(2)}, u32[]{:S(2)}) collective-permute-start(bf16[192,128]{1,0:T(8,128)(2,1)S(1)} %pad_maximum_fusion.refs_0_.refs_4_), channel_id=1, source_target_pairs={{0,6},{2,0},{4,2},{6,4},{1,7},{3,1},{5,3},{7,5},{8,14},{10,8},{12,... | collective-permute-start | bytes 147464 | tf_op jit(solution)/shard_map/ppermute | solution.py:287
  5.9 1.0 %collective-permute-start = (bf16[192,128]{1,0:T(8,128)(2,1)S(1)}, bf16[192,128]{1,0:T(8,128)(2,1)S(1)}, u32[]{:S(2)}, u32[]{:S(2)}) collective-permute-start(bf16[192,128]{1,0:T(8,128)(2,1)S(1)} %pad_maximum_fusion.refs_0_.refs_4_), channel_id=1, source_target_pairs={{0,2},{2,4},{4,6},{6,0},{1,3},{3,5},{5,7},{7,1},{8,10},{10,12},{12... | collective-permute-start | bytes 147464 | tf_op jit(solution)/shard_map/ppermute | solution.py:287
  6.9 0.1 pad_add_fusion.where
  7.0 4.0 %shard_map.37.held = bf16[2,4,32,128,128]{4,3,2,1,0:T(8,128)(2,1)S(1)} custom-call(s32[2]{0:T(128)S(1)} %pad_add_fusion.where, bf16[256,128,128]{2,1,0:T(8,128)(2,1)} %block.1), custom_call_target="tpu_custom_call" | custom-call | flops 4000000000 | bytes 8388608 | tf_op jit(solution)/shard_map/pallas_call | solution.py:56
  11.0 0.0 collective-permute-done.3.refs_5_
  11.0 0.9 %collective-permute-done.1.refs_2_ = bf16[192,128]{1,0:T(8,128)(2,1)S(1)} collective-permute-done((bf16[192,128]{1,0:T(8,128)(2,1)S(1)}, bf16[192,128]{1,0:T(8,128)(2,1)S(1)}, u32[]{:S(2)}, u32[]{:S(2)}) %collective-permute-start.1) | collective-permute-done | bytes 49184 | tf_op jit(solution)/shard_map/ppermute | solution.py:287
  11.9 0.0 collective-permute-done.refs_1_
  11.9 3.0 %shard_map.38 = (f32[1,4,32,256]{3,2,1,0:T(8,128)S(1)}, bf16[256,128]{1,0:T(8,128)(2,1)S(1)}, bf16[4,128,128]{2,1,0:T(8,128)(2,1)S(1)}, bf16[128,256]{1,0:T(8,128)(2,1)S(1)}, f32[128,256]{1,0:T(8,128)S(1)}) custom-call(s32[2]{0:T(128)S(1)} %pad_add_fusion.where, bf16[2,4,32,128,128]{4,3,2,1,0:T(8,128)(2,1)S(1)} %shard_map.37.held, ...), custom_call_target="tpu_custom_call" | custom-call | flops 1073741824 | bytes 1048576 | tf_op jit(solution)/shard_map/pallas_call | solution.py:114
  14.9 0.1 collective-permute-start.4
  15.0 0.5 %collective-permute-start.8 = (bf16[4,128,128]{2,1,0:T(8,128)(2,1)S(1)}, bf16[4,128,128]{2,1,0:T(8,128)(2,1)S(1)}, u32[]{:S(2)}, u32[]{:S(2)}) collective-permute-start(bf16[4,128,128]{2,1,0:T(8,128)(2,1)S(1)} %get-tuple-element.14.refs_2_), channel_id=1, source_target_pairs={{0,1},{1,0},{2,3},{3,2},{4,5},{5,4},{6,7},{7,6},{8,9},{9,8},{10,11... | collective-permute-start | bytes 393224 | tf_op jit(solution)/shard_map/ppermute | solution.py:292
  15.5 0.1 collective-permute-start.7
  15.6 2.4 %shard_map.39 = f32[4,32,256]{2,1,0:T(8,128)S(1)} custom-call(bf16[2,4,32,128,128]{4,3,2,1,0:T(8,128)(2,1)S(1)} %shard_map.37.held, bf16[128,256]{1,0:T(8,128)(2,1)S(1)} %get-tuple-element.10.c_cols, f32[128,256]{1,0:T(8,128)S(1)} %get-tuple-element.11.b_cols), custom_call_target="tpu_custom_call" | custom-call | flops 1073741824 | bytes 1048576 | tf_op jit(solution)/shard_map/pallas_call | solution.py:129
  17.9 0.0 collective-permute-done.4
  18.0 1.7 %collective-permute-start.5 = (f32[2,32,256]{2,1,0:T(8,128)S(1)}, f32[2,32,256]{2,1,0:T(8,128)S(1)}, u32[]{:S(2)}, u32[]{:S(2)}) collective-permute-start(f32[2,32,256]{2,1,0:T(8,128)S(1)} %split.17), channel_id=1, source_target_pairs={{0,2},{2,0},{4,6},{6,4},{1,3},{3,1},{5,7},{7,5},{8,10},{10,8},{12,... | collective-permute-start | bytes 196616 | tf_op jit(solution)/shard_map/ppermute | solution.py:311
  19.6 0.0 collective-permute-done.7.refs_1_
  19.6 0.0 collective-permute-done.8.refs_3_
  19.7 3.8 %shard_map.40.half_done = f32[256,256]{1,0:T(8,128)S(1)} custom-call(s32[2]{0:T(128)S(1)} %pad_add_fusion.where, bf16[256,128]{1,0:T(8,128)(2,1)S(1)} %get-tuple-element.13.refs_0_, bf16[256,128]{1,0:T(8,128)(2,1)S(1)} %collective-permute-done.7.refs_1_, bf16[4,128,128]{2,1,0:T(8,128)(2,1)S(1)} %get-tuple-element.14.refs_2_, ...), custom_call_target="tpu_custom_call" | custom-call | flops 5000000000 | bytes 1048576 | tf_op jit(solution)/shard_map/pallas_call | solution.py:299
  23.5 0.0 collective-permute-done.5
  23.5 1.0 %collective-permute-start.6 = (f32[1,32,256]{2,1,0:T(8,128)S(1)}, f32[1,32,256]{2,1,0:T(8,128)S(1)}, u32[]{:S(2)}, u32[]{:S(2)}) collective-permute-start(f32[1,32,256]{2,1,0:T(8,128)S(1)} %get-tuple-element.15), channel_id=1, source_target_pairs={{0,4},{2,6},{4,0},{6,2},{1,5},{3,7},{5,1},{7,3},{8,12},{10,14},{12... | collective-permute-start | bytes 98312 | tf_op jit(solution)/shard_map/ppermute | solution.py:311
  24.5 2.8 %shard_map.41.inverse = f32[256,256]{1,0:T(8,128)S(1)} custom-call(f32[256,256]{1,0:T(8,128)S(1)} %shard_map.40.half_done), custom_call_target="tpu_custom_call" | custom-call | flops 5000000000 | bytes 1048576 | tf_op jit(solution)/shard_map/pallas_call | solution.py:314
  27.3 1.4 %collective-permute-done.6.received = f32[1,32,256]{2,1,0:T(8,128)S(1)} collective-permute-done((f32[1,32,256]{2,1,0:T(8,128)S(1)}, f32[1,32,256]{2,1,0:T(8,128)S(1)}, u32[]{:S(2)}, u32[]{:S(2)}) %collective-permute-start.6) | collective-permute-done | bytes 32800 | tf_op jit(solution)/shard_map/ppermute | solution.py:311
  28.7 0.8 %shard_map.42 = f32[32,256]{1,0:T(8,128)} custom-call(f32[1,32,256]{2,1,0:T(8,128)S(1)} %get-tuple-element.16.kept, f32[1,32,256]{2,1,0:T(8,128)S(1)} %collective-permute-done.6.received, f32[256,256]{1,0:T(8,128)S(1)} %shard_map.41.inverse), custom_call_target="tpu_custom_call" | custom-call | flops 100000000 | bytes 524288 | tf_op jit(solution)/shard_map/pallas_call | solution.py:322
  (6 shorter events, 0.0 us)
Async XLA Ops:
  0.8 10.2 %collective-permute-start.3 = (bf16[192,128]{1,0:T(8,128)(2,1)S(1)}, bf16[192,128]{1,0:T(8,128)(2,1)S(1)}, u32[]{:S(2)}, u32[]{:S(2)}) collective-permute-start(bf16[192,128]{1,0:T(8,128)(2,1)S(1)} %pad_maximum_fusion.refs_0_.refs_4_), channel_id=1, source_target_pairs={{0,1},{1,0},{2,3},{3,2},{4,5},{5,4},{6,7},{7,6},{8,9},{9,8},{10,11... | collective-permute-start | bytes 147464 | tf_op jit(solution)/shard_map/ppermute | solution.py:288
  1.3 9.7 %collective-permute-start.2 = (bf16[192,128]{1,0:T(8,128)(2,1)S(1)}, bf16[192,128]{1,0:T(8,128)(2,1)S(1)}, u32[]{:S(2)}, u32[]{:S(2)}) collective-permute-start(bf16[192,128]{1,0:T(8,128)(2,1)S(1)} %pad_maximum_fusion.refs_0_.refs_4_), channel_id=1, source_target_pairs={{0,6},{2,0},{4,2},{6,4},{1,7},{3,1},{5,3},{7,5},{8,14},{10,8},{12,... | collective-permute-start | bytes 147464 | tf_op jit(solution)/shard_map/ppermute | solution.py:287
  5.9 6.0 %collective-permute-start.1 = (bf16[192,128]{1,0:T(8,128)(2,1)S(1)}, bf16[192,128]{1,0:T(8,128)(2,1)S(1)}, u32[]{:S(2)}, u32[]{:S(2)}) collective-permute-start(bf16[192,128]{1,0:T(8,128)(2,1)S(1)} %pad_maximum_fusion.refs_0_.refs_4_), channel_id=1, source_target_pairs={{0,4},{2,6},{4,0},{6,2},{1,5},{3,7},{5,1},{7,3},{8,12},{10,14},{12... | collective-permute-start | bytes 147464 | tf_op jit(solution)/shard_map/ppermute | solution.py:287
  5.9 6.0 %collective-permute-start = (bf16[192,128]{1,0:T(8,128)(2,1)S(1)}, bf16[192,128]{1,0:T(8,128)(2,1)S(1)}, u32[]{:S(2)}, u32[]{:S(2)}) collective-permute-start(bf16[192,128]{1,0:T(8,128)(2,1)S(1)} %pad_maximum_fusion.refs_0_.refs_4_), channel_id=1, source_target_pairs={{0,2},{2,4},{4,6},{6,0},{1,3},{3,5},{5,7},{7,1},{8,10},{10,12},{12... | collective-permute-start | bytes 147464 | tf_op jit(solution)/shard_map/ppermute | solution.py:287
  14.9 3.0 %collective-permute-start.4 = (f32[4,32,256]{2,1,0:T(8,128)S(1)}, f32[4,32,256]{2,1,0:T(8,128)S(1)}, u32[]{:S(2)}, u32[]{:S(2)}) collective-permute-start(f32[4,32,256]{2,1,0:T(8,128)S(1)} %bitcast.4), channel_id=1, source_target_pairs={{0,1},{1,0},{2,3},{3,2},{4,5},{5,4},{6,7},{7,6},{8,9},{9,8},{10,11... | collective-permute-start | bytes 393224 | tf_op jit(solution)/shard_map/ppermute | solution.py:294
  15.0 4.7 %collective-permute-start.8 = (bf16[4,128,128]{2,1,0:T(8,128)(2,1)S(1)}, bf16[4,128,128]{2,1,0:T(8,128)(2,1)S(1)}, u32[]{:S(2)}, u32[]{:S(2)}) collective-permute-start(bf16[4,128,128]{2,1,0:T(8,128)(2,1)S(1)} %get-tuple-element.14.refs_2_), channel_id=1, source_target_pairs={{0,1},{1,0},{2,3},{3,2},{4,5},{5,4},{6,7},{7,6},{8,9},{9,8},{10,11... | collective-permute-start | bytes 393224 | tf_op jit(solution)/shard_map/ppermute | solution.py:292
  15.5 4.2 %collective-permute-start.7 = (bf16[256,128]{1,0:T(8,128)(2,1)S(1)}, bf16[256,128]{1,0:T(8,128)(2,1)S(1)}, u32[]{:S(2)}, u32[]{:S(2)}) collective-permute-start(bf16[256,128]{1,0:T(8,128)(2,1)S(1)} %get-tuple-element.13.refs_0_), channel_id=1, source_target_pairs={{0,1},{1,0},{2,3},{3,2},{4,5},{5,4},{6,7},{7,6},{8,9},{9,8},{10,11... | collective-permute-start | bytes 196616 | tf_op jit(solution)/shard_map/ppermute | solution.py:291
  18.0 5.5 %collective-permute-start.5 = (f32[2,32,256]{2,1,0:T(8,128)S(1)}, f32[2,32,256]{2,1,0:T(8,128)S(1)}, u32[]{:S(2)}, u32[]{:S(2)}) collective-permute-start(f32[2,32,256]{2,1,0:T(8,128)S(1)} %split.17), channel_id=1, source_target_pairs={{0,2},{2,0},{4,6},{6,4},{1,3},{3,1},{5,7},{7,5},{8,10},{10,8},{12,... | collective-permute-start | bytes 196616 | tf_op jit(solution)/shard_map/ppermute | solution.py:311
  23.5 5.2 %collective-permute-start.6 = (f32[1,32,256]{2,1,0:T(8,128)S(1)}, f32[1,32,256]{2,1,0:T(8,128)S(1)}, u32[]{:S(2)}, u32[]{:S(2)}) collective-permute-start(f32[1,32,256]{2,1,0:T(8,128)S(1)} %get-tuple-element.15), channel_id=1, source_target_pairs={{0,4},{2,6},{4,0},{6,2},{1,5},{3,7},{5,1},{7,3},{8,12},{10,14},{12... | collective-permute-start | bytes 98312 | tf_op jit(solution)/shard_map/ppermute | solution.py:311

commit v4 on v3

v4 whole, which is shorter than its diff:
```python
import functools

import jax
import jax.numpy as jnp
from jax import lax
from jax.experimental import pallas as pl
from jax.experimental.pallas import tpu as pltpu
from jax.sharding import PartitionSpec as P


ridge_weight = 0.1
exact = lax.Precision.HIGHEST
vmem = pl.BlockSpec(memory_space=pltpu.VMEM)
smem = pl.BlockSpec(memory_space=pltpu.SMEM)
hbm = pl.BlockSpec(memory_space=pltpu.HBM)


def shift(n, s):
    return [(i, (i + s) % n) for i in range(n)]


def wrap(x, n):
    return lax.rem(x + n, n)


def owner(nk, where, t, u):
    return lax.bitwise_xor(where[0], u) * nk + wrap(where[1] + t, nk)


def halving_order(nj):
    order = [0]
    while len(order) < nj:
        order = [2 * u for u in order] + [2 * u + 1 for u in order]
    return order


def copies(nj, nk, where, block, held, arrived, t):
    owned = held.shape[1]
    made = []
    for slot, u in enumerate(halving_order(nj)):
        first = pl.multiple_of(owner(nk, where, t, u) * owned, owned)
        rows = block.at[pl.ds(first, owned)]
        made.append(pltpu.make_async_copy(rows, held.at[slot], arrived.at[slot]))
    return made


def fetch_kernel(nj, nk, where, block, held, arrived):
    made = []
    for t in range(1, nk):
        made += copies(nj, nk, where, block, held.at[t - 1], arrived.at[t - 1], t)
    for copy in made:
        copy.start()
    for copy in made:
        copy.wait()


def fetch(where, tensor, nj, nk):
    rows, width_j, width_k = tensor.shape
    owned = rows // (nj * nk)
    return pl.pallas_call(
        functools.partial(fetch_kernel, nj, nk),
        out_shape=jax.ShapeDtypeStruct((nk - 1, nj, owned, width_j, width_k), tensor.dtype),
        in_specs=[smem, hbm],
        out_specs=vmem,
        scratch_shapes=[pltpu.SemaphoreType.DMA((nk - 1, nj))],
        compiler_params=pltpu.CompilerParams(vmem_limit_bytes=46 * 2**20),
        cost_estimate=pl.CostEstimate(
            flops=2 * 10**9, bytes_accessed=rows * width_j * width_k, transcendentals=0
        ),
    )(where, tensor)


def contract(held, out, c_wide, b_wide):
    count, owned = held.shape[0], held.shape[1]
    for u in range(count):
        sums = []
        for i in range(owned):
            inner = jnp.dot(held[u, i], c_wide, preferred_element_type=jnp.float32)
            sums.append(jnp.sum(inner * b_wide, axis=0, keepdims=True))
        out[u] = jnp.concatenate(sums, axis=0)


def away_kernel(nj, nk, height_b, flipped, where, block, held, *refs):
    line, refs = refs[:nj], refs[nj:]
    b_parts, refs = refs[:nk], refs[nk:]
    out, own, c_cols, b_cols, home_held, b_rows, arrived = refs
    rank = c_cols.shape[1]
    home = copies(nj, nk, where, block, home_held, arrived, 0)
    for copy in home:
        copy.start()
    width_c = line[0].shape[0] - height_b
    for s in range(nj):
        at = pl.multiple_of(wrap(where[0] - s, nj) * width_c, width_c)
        own[pl.ds(at, width_c), :] = line[s][height_b:, :]
        own[rank + s * height_b : rank + (s + 1) * height_b, :] = line[s][:height_b, :]
    for t in range(nk):
        if flipped:
            at = pl.multiple_of(wrap(where[1] - t, nk) * height_b, height_b)
            b_rows[pl.ds(at, height_b), :] = b_parts[t][:height_b, :]
        else:
            at = pl.multiple_of(wrap(where[1] - t, nk) * 128, 128)
            b_rows[:, pl.ds(at, 128)] = b_parts[t][:height_b, :]
    c_cols[...] = own[:rank, :].T
    b_cols[...] = (b_rows[...].T if flipped else b_rows[...]).astype(jnp.float32)
    for t in range(1, nk):
        contract(held.at[t - 1], out.at[t - 1], c_cols[...], b_cols[...])
    for copy in home:
        copy.wait()


def home_kernel(begin, count, held, c_cols, b_cols, out):
    contract(held.at[begin : begin + count], out, c_cols[...], b_cols[...])


def flops_of(rows, held, rank):
    return pl.CostEstimate(
        flops=2 * rows * held.shape[-2] * held.shape[-1] * rank,
        bytes_accessed=2**20,
        transcendentals=0,
    )


def contract_away(where, tensor, held, line, b_parts, height_b, flipped, rank):
    _, nj, owned, width_j, width_k = held.shape
    nk = len(b_parts)
    width = line[0].shape[1]
    return pl.pallas_call(
        functools.partial(away_kernel, nj, nk, height_b, flipped),
        out_shape=[
            jax.ShapeDtypeStruct((nk - 1, nj, owned, rank), jnp.float32),
            jax.ShapeDtypeStruct((rank + nj * height_b, width), held.dtype),
            jax.ShapeDtypeStruct((width_k, rank), held.dtype),
            jax.ShapeDtypeStruct((width_j, rank), jnp.float32),
            jax.ShapeDtypeStruct(held.shape[1:], held.dtype),
        ],
        in_specs=[smem, hbm] + [vmem] * (1 + nj + nk),
        out_specs=[vmem] * 5,
        scratch_shapes=[
            pltpu.VMEM((rank, width_j) if flipped else (width_j, rank), held.dtype),
            pltpu.SemaphoreType.DMA((nj,)),
        ],
        compiler_params=pltpu.CompilerParams(vmem_limit_bytes=44 * 2**20),
        cost_estimate=flops_of((nk - 1) * nj * owned, held, rank),
    )(where, tensor, held, *line, *b_parts)


def contract_home(begin, count, held, c_cols, b_cols):
    _, owned, _, _ = held.shape
    rank = c_cols.shape[1]
    return pl.pallas_call(
        functools.partial(home_kernel, begin, count),
        out_shape=jax.ShapeDtypeStruct((count, owned, rank), jnp.float32),
        in_specs=[vmem] * 3,
        out_specs=vmem,
        compiler_params=pltpu.CompilerParams(vmem_limit_bytes=20 * 2**20),
        cost_estimate=flops_of(count * owned, held, rank),
    )(held, c_cols, b_cols)


def column(x, q):
    return jnp.take_along_axis(x, jnp.full(x.shape, q, jnp.int32), axis=1)


def row(x, q):
    return jnp.broadcast_to(x[q : q + 1, :], x.shape)


def thirds(x):
    high = x.astype(jnp.bfloat16)
    x = x - high.astype(jnp.float32)
    middle = x.astype(jnp.bfloat16)
    return high, middle, (x - middle.astype(jnp.float32)).astype(jnp.bfloat16)


def stack(tiles):
    return jnp.concatenate([jnp.concatenate(r, axis=1) for r in tiles], axis=0)


def invert(a, begin, end, step=16):
    size = a.shape[0]
    wide, per = size // 128, step // 8
    lane = lax.broadcasted_iota(jnp.int32, (8, 128), 1)
    sub = lax.broadcasted_iota(jnp.int32, (8, 128), 0)

    def tile(g, w):
        return a[8 * g : 8 * g + 8, 128 * w : 128 * w + 128]

    def columns(rows, w, first):
        return [[column(r[w], first + q) for r in rows] for q in range(step)]

    now = [[tile(begin // 8 + g, w) for w in range(wide)] for g in range(per)]
    for first in range(begin, end, step):
        g0, w0, lane0 = first // 8, first // 128, first % 128
        inside = (lane >= lane0) & (lane < lane0 + step)
        more = first + step < size
        panel = [list(r) for r in now]
        c = columns(now, w0, lane0)
        if more:
            ahead = [[tile(g0 + per + i, w) for w in range(wide)] for i in range(per)]
            ahead_c = columns(ahead, w0, lane0)
        scale = [jnp.zeros((8, 128), jnp.float32)] * per
        pivot = row(c[0][0], 0)
        for i in range(per):
            unit = jnp.where(lane == sub + (lane0 + 8 * i), 1.0, 0.0)
            panel[i][w0] = jnp.where(inside, unit, panel[i][w0])
        for q in range(step):
            gq, sq = q // 8, q % 8
            here = sub == sq
            inv = 1.0 / pivot
            scale[gq] = jnp.where(here, inv, scale[gq])
            if q + 1 < step:
                gn, sn = (q + 1) // 8, (q + 1) % 8
                product = row(c[q][gn], sn) * row(c[q + 1][gq], sq)
                pivot = row(c[q + 1][gn], sn) - product * inv
            factor = [jnp.where(here, 0.0, c[q][i]) if i == gq else c[q][i] for i in range(per)]
            factor = [f * inv for f in factor]
            for p in range(q + 1, step):
                pivot_row = row(c[p][gq], sq)
                for i in range(per):
                    c[p][i] = c[p][i] - factor[i] * pivot_row
            for w in range(wide):
                pivot_row = row(panel[gq][w], sq)
                for i in range(per):
                    panel[i][w] = panel[i][w] - factor[i] * pivot_row
        done = [[panel[i][w] * scale[i] for w in range(wide)] for i in range(per)]
        lanes = lax.broadcasted_iota(jnp.int32, (step, size), 1)
        left = stack(now)
        left = thirds(jnp.where(lanes < first, -left, left))
        right = thirds(stack(done))
        pairs = ((0, 0), (0, 1), (1, 0), (0, 2), (1, 1), (2, 0))
        update = lax.dot_general(
            jnp.concatenate([left[i] for i, _ in pairs], axis=0),
            jnp.concatenate([right[i] for _, i in pairs], axis=0),
            (((0,), (0,)), ((), ())),
            preferred_element_type=jnp.float32,
        )
        if more:
            now = []
            for i in range(per):
                fresh = []
                for w in range(wide):
                    terms = [ahead_c[q][i] * row(done[q // 8][w], q % 8) for q in range(step)]
                    while len(terms) > 1:
                        terms = [x + y for x, y in zip(terms[::2], terms[1::2])]
                    spread = terms[0]
                    base = ahead[i][w]
                    base = jnp.where(inside, 0.0, base) if w == w0 else base
                    fresh.append(base - spread)
                now.append(fresh)
        for g in range(size // 8):
            for w in range(wide):
                if g0 <= g < g0 + per:
                    value = done[g - g0][w]
                elif more and g0 + per <= g < g0 + 2 * per:
                    value = now[g - g0 - per][w]
                else:
                    value = tile(g, w)
                    value = jnp.where(inside, 0.0, value) if w == w0 else value
                    value = value - update[8 * g : 8 * g + 8, 128 * w : 128 * w + 128]
                a[8 * g : 8 * g + 8, 128 * w : 128 * w + 128] = value


def inverse_kernel(nj, nk, height_b, flipped, blocks, where, *refs):
    owns, (out, b_all) = refs[:nk], refs[nk:]
    rank = out.shape[1]

    def gram(x, contracted):
        dims = (((contracted,), (contracted,)), ((), ()))
        return lax.dot_general(x, x, dims, preferred_element_type=jnp.float32)

    for t in range(nk):
        part = owns[t][rank:, :].reshape(nj, height_b, owns[t].shape[1])
        if flipped:
            at = pl.multiple_of(wrap(where[1] - t, nk) * height_b, height_b)
            b_all[:, pl.ds(at, height_b), :] = part
        else:
            at = pl.multiple_of(wrap(where[1] - t, nk) * 128, 128)
            b_all[:, :, pl.ds(at, 128)] = part
    if flipped:
        gram_b = sum(gram(b_all[s], 1) for s in range(nj))
    else:
        gram_b = gram(b_all[...].reshape(nj * height_b, rank), 0)
    gram_c = sum(gram(own[:rank, :], 1) for own in owns)
    diagonal = lax.broadcasted_iota(jnp.int32, out.shape, 0) == lax.broadcasted_iota(
        jnp.int32, out.shape, 1
    )
    out[...] = gram_b * gram_c + jnp.where(diagonal, ridge_weight, 0.0)
    invert(out, 0, blocks)


def rest_kernel(blocks, half_done, out):
    out[...] = half_done[...]
    invert(out, blocks, out.shape[0])


def solve_kernel(kept, received, inverse, out):
    mine = kept[0] + received[0]
    out[...] = jnp.dot(mine, inverse[...], precision=exact, preferred_element_type=jnp.float32)


def send(x, axis, n, s):
    return lax.ppermute(x, axis, shift(n, s))


def update(tensor, factor_b, factor_c):
    nj, nk = lax.axis_size("ja"), lax.axis_size("ka")
    where = jnp.stack([lax.axis_index("ja"), lax.axis_index("ka")]).astype(jnp.int32)
    rank = factor_b.shape[1] * nk
    flipped = factor_b.shape[1] % 128 != 0
    part_b = factor_b.T if flipped else factor_b
    height_b = part_b.shape[0]
    mine = jnp.concatenate([part_b, factor_c.T], axis=0)
    line = [mine] + [send(mine, "ja", nj, s) for s in range(1, nj)]
    b_parts = [mine] + [send(mine, "ka", nk, t) for t in range(1, nk)]
    held = fetch(where, tensor, nj, nk)
    away, own, c_cols, b_cols, held = contract_away(
        where, tensor, held, line, b_parts, height_b, flipped, rank
    )
    half = nj // 2
    sent = contract_home(half, half, held, c_cols, b_cols)
    for t in range(1, nk):
        received = send(away[t - 1], "ka", nk, t)
        sent = sent + received[half:]
        away_kept = received[:half] if t == 1 else away_kept + received[:half]
    owns = [own] + [send(own, "ka", nk, t) for t in range(1, nk)]
    kept = contract_home(0, half, held, c_cols, b_cols)
    kept = kept + away_kept
    params = pltpu.CompilerParams(vmem_limit_bytes=20 * 2**20)
    cost = pl.CostEstimate(flops=5 * 10**9, bytes_accessed=2**20, transcendentals=0)
    square = jax.ShapeDtypeStruct((rank, rank), jnp.float32)
    blocks = rank // 64 * 16
    b_shape = (nj, rank, mine.shape[1]) if flipped else (nj, height_b, rank)
    half_done = pl.pallas_call(
        functools.partial(inverse_kernel, nj, nk, height_b, flipped, blocks),
        out_shape=square,
        in_specs=[smem] + [vmem] * nk,
        out_specs=vmem,
        scratch_shapes=[pltpu.VMEM(b_shape, mine.dtype)],
        compiler_params=params,
        cost_estimate=cost,
    )(where, *owns)
    bit = 1
    while True:
        received = lax.ppermute(sent, "ja", [(i, i ^ bit) for i in range(nj)])
        bit *= 2
        if bit == nj:
            break
        kept, sent = jnp.split(kept + received, 2, axis=0)
    inverse = pl.pallas_call(
        functools.partial(rest_kernel, blocks),
        out_shape=square,
        in_specs=[vmem],
        out_specs=vmem,
        compiler_params=params,
        cost_estimate=cost,
    )(half_done)
    return pl.pallas_call(
        solve_kernel,
        out_shape=jax.ShapeDtypeStruct(kept.shape[1:], jnp.float32),
        in_specs=[vmem] * 3,
        out_specs=vmem,
        compiler_params=params,
        cost_estimate=pl.CostEstimate(flops=10**8, bytes_accessed=2**19, transcendentals=0),
    )(kept, received, inverse)


def solution(mesh):
    placed = (P("ia", "ja", "ka"), P("ja", "ka"), P("ka", "ja"))
    return jax.shard_map(
        update, mesh=mesh, in_specs=placed, out_specs=P(("ia", "ja", "ka"), None), check_vma=False
    )
```

time: 29.8 us -> 31.6 us (1.060)
  waiting for transfers between devices: 2.35 us -> 4.92 us
  starting transfers between devices: 9.4 us -> 8.44 us
    ppermute x9 -> x8, waiting for transfers between devices: 2.35 us -> 4.92 us  [the longest x2 2.67 us: update(): received = lax.ppermute(sent, 'ja', [(i, i ^ bit) for i in range(nj)])]
    pallas_call x5 -> x6, Pallas kernels: 12.8 us -> 14.3 us  [the longest x1 5.06 us: contract_away(): pl.pallas_call(functools.partial(away_kernel, nj, nk, height_b, flipped),...]
    pallas_call x1, Pallas kernels: 4.02 us -> 2.75 us  [fetch(): pl.pallas_call(functools.partial(fetch_kernel, nj, nk), out_shape=jax.Sha...]
    ppermute x9 -> x8, starting transfers between devices: 9.4 us -> 8.44 us  [the longest x6 6.37 us: send(): return lax.ppermute(x, axis, shift(n, s))]
  transfers between devices with their start and end apart: 9 -> 8, of which waited for: 2 -> 3; matrix products, arithmetic and copies ran while one was open for 0% -> 0% of each run, Pallas kernels for 44% -> 35%
where the time goes in v4:
time: 31.6 us; the launch traced here: 31.4 us
  Pallas kernels  17 us (54%)
  starting transfers between devices  8.44 us (27%)
  waiting for transfers between devices  4.92 us (16%)
  other arithmetic  0.88 us (3%)
    ppermute x6, starting transfers between devices, send(): return lax.ppermute(x, axis, shift(n, s))  6.37 us
    pallas_call x1, Pallas kernels, contract_away(): pl.pallas_call(functools.partial(away_kernel, nj, nk, height_b, flipped),...  5.06 us
    pallas_call x1, Pallas kernels, update(): pl.pallas_call(functools.partial(rest_kernel, blocks), out_shape=square,...  3.73 us
    pallas_call x1, Pallas kernels, fetch(): pl.pallas_call(functools.partial(fetch_kernel, nj, nk), out_shape=jax.Sha...  2.75 us
    ppermute x2, waiting for transfers between devices, update(): received = lax.ppermute(sent, 'ja', [(i, i ^ bit) for i in range(nj)])  2.67 us
    pallas_call x2, Pallas kernels, contract_home(): pl.pallas_call(functools.partial(home_kernel, begin, count), out_shape=ja...  2.5 us
    ppermute x6, waiting for transfers between devices, send(): return lax.ppermute(x, axis, shift(n, s))  2.26 us
    pallas_call x1, Pallas kernels, update(): pl.pallas_call(functools.partial(inverse_kernel, nj, nk, height_b, flippe...  2.15 us
  transfers between devices with their start and end apart: 8, of which 3 were waited for; matrix products, arithmetic and copies ran while one was open for 0% of the time, Pallas kernels for 35%

profile of v4, /device:TPU:0, one launch (start us, length us, event | category | flops | bytes accessed | tf_op | source)
XLA Modules:
  0.0 31.4 jit_solution(10322860515298076918)
XLA Ops:
  0.0 0.8 %pad_maximum_fusion.refs_0_.refs_4_ = bf16[192,128]{1,0:T(8,128)(2,1)S(1)} fusion(bf16[64,128]{1,0:T(8,128)(2,1)} %bitcast.5, bf16[128,128]{1,0:T(8,128)(2,1)} %param.4), kind=kLoop, calls=%fused_computation.3 | loop fusion | flops 98304 | bytes 98304 | tf_op jit(solution)/shard_map/concatenate | solution.py:312
  0.8 0.5 %collective-permute-start.3 = (bf16[192,128]{1,0:T(8,128)(2,1)S(1)}, bf16[192,128]{1,0:T(8,128)(2,1)S(1)}, u32[]{:S(2)}, u32[]{:S(2)}) collective-permute-start(bf16[192,128]{1,0:T(8,128)(2,1)S(1)} %pad_maximum_fusion.refs_0_.refs_4_), channel_id=1, source_target_pairs={{0,1},{1,0},{2,3},{3,2},{4,5},{5,4},{6,7},{7,6},{8,9},{9,8},{10,11... | collective-permute-start | bytes 147464 | tf_op jit(solution)/shard_map/ppermute | solution.py:302
  1.3 4.6 %collective-permute-start.2 = (bf16[192,128]{1,0:T(8,128)(2,1)S(1)}, bf16[192,128]{1,0:T(8,128)(2,1)S(1)}, u32[]{:S(2)}, u32[]{:S(2)}) collective-permute-start(bf16[192,128]{1,0:T(8,128)(2,1)S(1)} %pad_maximum_fusion.refs_0_.refs_4_), channel_id=1, source_target_pairs={{0,6},{2,0},{4,2},{6,4},{1,7},{3,1},{5,3},{7,5},{8,14},{10,8},{12,... | collective-permute-start | bytes 147464 | tf_op jit(solution)/shard_map/ppermute | solution.py:302
  5.9 0.0 collective-permute-start.1
  5.9 1.0 %collective-permute-start = (bf16[192,128]{1,0:T(8,128)(2,1)S(1)}, bf16[192,128]{1,0:T(8,128)(2,1)S(1)}, u32[]{:S(2)}, u32[]{:S(2)}) collective-permute-start(bf16[192,128]{1,0:T(8,128)(2,1)S(1)} %pad_maximum_fusion.refs_0_.refs_4_), channel_id=1, source_target_pairs={{0,2},{2,4},{4,6},{6,0},{1,3},{3,5},{5,7},{7,1},{8,10},{10,12},{12... | collective-permute-start | bytes 147464 | tf_op jit(solution)/shard_map/ppermute | solution.py:302
  6.9 0.1 pad_add_fusion.where
  7.0 2.8 %shard_map.37.held = bf16[1,4,32,128,128]{4,3,2,1,0:T(8,128)(2,1)S(1)} custom-call(s32[2]{0:T(128)S(1)} %pad_add_fusion.where, bf16[256,128,128]{2,1,0:T(8,128)(2,1)} %block.3), custom_call_target="tpu_custom_call" | custom-call | flops 2000000000 | bytes 4194304 | tf_op jit(solution)/shard_map/pallas_call | solution.py:60
  9.7 0.0 collective-permute-done.3.refs_5_
  9.7 0.0 collective-permute-done.2.refs_3_
  9.8 2.2 %collective-permute-done.1.refs_2_ = bf16[192,128]{1,0:T(8,128)(2,1)S(1)} collective-permute-done((bf16[192,128]{1,0:T(8,128)(2,1)S(1)}, bf16[192,128]{1,0:T(8,128)(2,1)S(1)}, u32[]{:S(2)}, u32[]{:S(2)}) %collective-permute-start.1) | collective-permute-done | bytes 49184 | tf_op jit(solution)/shard_map/ppermute | solution.py:302
  11.9 0.0 collective-permute-done.refs_1_
  11.9 5.1 %shard_map.38 = (f32[1,4,32,256]{3,2,1,0:T(8,128)S(1)}, bf16[768,128]{1,0:T(8,128)(2,1)S(1)}, bf16[128,256]{1,0:T(8,128)(2,1)S(1)}, f32[128,256]{1,0:T(8,128)S(1)}, bf16[4,32,128,128]{3,2,1,0:T(8,128)(2,1)S(1)}) custom-call(s32[2]{0:T(128)S(1)} %pad_add_fusion.where, bf16[256,128,128]{2,1,0:T(8,128)(2,1)} %block.3, ...), custom_call_target="tpu_custom_call" | custom-call | flops 1073741824 | bytes 1048576 | tf_op jit(solution)/shard_map/pallas_call | solution.py:127
  17.0 0.1 collective-permute-start.4
  17.1 1.3 %shard_map.40 = f32[2,32,256]{2,1,0:T(8,128)S(1)} custom-call(bf16[4,32,128,128]{3,2,1,0:T(8,128)(2,1)S(1)} %get-tuple-element.10.held, bf16[128,256]{1,0:T(8,128)(2,1)S(1)} %get-tuple-element.11.c_cols, f32[128,256]{1,0:T(8,128)S(1)} %get-tuple-element.12.b_cols), custom_call_target="tpu_custom_call" | custom-call | flops 536870912 | bytes 1048576 | tf_op jit(solution)/shard_map/pallas_call | solution.py:150
  18.3 0.1 collective-permute-done.4
  18.4 0.4 %collective-permute-start.5 = (f32[2,32,256]{2,1,0:T(8,128)S(1)}, f32[2,32,256]{2,1,0:T(8,128)S(1)}, u32[]{:S(2)}, u32[]{:S(2)}) collective-permute-start(f32[2,32,256]{2,1,0:T(8,128)S(1)} %slice_add_fusion), channel_id=1, source_target_pairs={{0,2},{2,0},{4,6},{6,4},{1,3},{3,1},{5,7},{7,5},{8,10},{10,8},{12,... | collective-permute-start | bytes 196616 | tf_op jit(solution)/shard_map/ppermute | solution.py:344
  18.8 0.2 collective-permute-start.7
  19.0 1.2 %shard_map.39 = f32[2,32,256]{2,1,0:T(8,128)S(1)} custom-call(bf16[4,32,128,128]{3,2,1,0:T(8,128)(2,1)S(1)} %get-tuple-element.10.held, bf16[128,256]{1,0:T(8,128)(2,1)S(1)} %get-tuple-element.11.c_cols, f32[128,256]{1,0:T(8,128)S(1)} %get-tuple-element.12.b_cols), custom_call_target="tpu_custom_call" | custom-call | flops 536870912 | bytes 1048576 | tf_op jit(solution)/shard_map/pallas_call | solution.py:150
  20.3 2.7 %collective-permute-done.5 = f32[2,32,256]{2,1,0:T(8,128)S(1)} collective-permute-done((f32[2,32,256]{2,1,0:T(8,128)S(1)}, f32[2,32,256]{2,1,0:T(8,128)S(1)}, u32[]{:S(2)}, u32[]{:S(2)}) %collective-permute-start.5) | collective-permute-done | bytes 65568 | tf_op jit(solution)/shard_map/ppermute | solution.py:344
  22.9 1.7 %collective-permute-start.6 = (f32[1,32,256]{2,1,0:T(8,128)S(1)}, f32[1,32,256]{2,1,0:T(8,128)S(1)}, u32[]{:S(2)}, u32[]{:S(2)}) collective-permute-start(f32[1,32,256]{2,1,0:T(8,128)S(1)} %get-tuple-element.15), channel_id=1, source_target_pairs={{0,4},{2,6},{4,0},{6,2},{1,5},{3,7},{5,1},{7,3},{8,12},{10,14},{12... | collective-permute-start | bytes 98312 | tf_op jit(solution)/shard_map/ppermute | solution.py:344
  24.6 0.0 collective-permute-done.7.refs_1_
  24.6 2.1 %shard_map.41.half_done = f32[256,256]{1,0:T(8,128)S(1)} custom-call(s32[2]{0:T(128)S(1)} %pad_add_fusion.where, bf16[768,128]{1,0:T(8,128)(2,1)S(1)} %get-tuple-element.14.refs_0_, bf16[768,128]{1,0:T(8,128)(2,1)S(1)} %collective-permute-done.7.refs_1_), custom_call_target="tpu_custom_call" | custom-call | flops 5000000000 | bytes 1048576 | tf_op jit(solution)/shard_map/pallas_call | solution.py:333
  26.8 3.7 %shard_map.42.inverse = f32[256,256]{1,0:T(8,128)S(1)} custom-call(f32[256,256]{1,0:T(8,128)S(1)} %shard_map.41.half_done), custom_call_target="tpu_custom_call" | custom-call | flops 5000000000 | bytes 1048576 | tf_op jit(solution)/shard_map/pallas_call | solution.py:349
  30.5 0.8 %shard_map.43 = f32[32,256]{1,0:T(8,128)} custom-call(f32[1,32,256]{2,1,0:T(8,128)S(1)} %get-tuple-element.16.kept, f32[1,32,256]{2,1,0:T(8,128)S(1)} %collective-permute-done.6.received, f32[256,256]{1,0:T(8,128)S(1)} %shard_map.42.inverse), custom_call_target="tpu_custom_call" | custom-call | flops 100000000 | bytes 524288 | tf_op jit(solution)/shard_map/pallas_call | solution.py:357
  (4 shorter events, 0.0 us)
Async XLA Ops:
  0.8 9.0 %collective-permute-start.3 = (bf16[192,128]{1,0:T(8,128)(2,1)S(1)}, bf16[192,128]{1,0:T(8,128)(2,1)S(1)}, u32[]{:S(2)}, u32[]{:S(2)}) collective-permute-start(bf16[192,128]{1,0:T(8,128)(2,1)S(1)} %pad_maximum_fusion.refs_0_.refs_4_), channel_id=1, source_target_pairs={{0,1},{1,0},{2,3},{3,2},{4,5},{5,4},{6,7},{7,6},{8,9},{9,8},{10,11... | collective-permute-start | bytes 147464 | tf_op jit(solution)/shard_map/ppermute | solution.py:302
  1.3 8.5 %collective-permute-start.2 = (bf16[192,128]{1,0:T(8,128)(2,1)S(1)}, bf16[192,128]{1,0:T(8,128)(2,1)S(1)}, u32[]{:S(2)}, u32[]{:S(2)}) collective-permute-start(bf16[192,128]{1,0:T(8,128)(2,1)S(1)} %pad_maximum_fusion.refs_0_.refs_4_), channel_id=1, source_target_pairs={{0,6},{2,0},{4,2},{6,4},{1,7},{3,1},{5,3},{7,5},{8,14},{10,8},{12,... | collective-permute-start | bytes 147464 | tf_op jit(solution)/shard_map/ppermute | solution.py:302
  5.9 6.0 %collective-permute-start.1 = (bf16[192,128]{1,0:T(8,128)(2,1)S(1)}, bf16[192,128]{1,0:T(8,128)(2,1)S(1)}, u32[]{:S(2)}, u32[]{:S(2)}) collective-permute-start(bf16[192,128]{1,0:T(8,128)(2,1)S(1)} %pad_maximum_fusion.refs_0_.refs_4_), channel_id=1, source_target_pairs={{0,4},{2,6},{4,0},{6,2},{1,5},{3,7},{5,1},{7,3},{8,12},{10,14},{12... | collective-permute-start | bytes 147464 | tf_op jit(solution)/shard_map/ppermute | solution.py:302
  5.9 6.0 %collective-permute-start = (bf16[192,128]{1,0:T(8,128)(2,1)S(1)}, bf16[192,128]{1,0:T(8,128)(2,1)S(1)}, u32[]{:S(2)}, u32[]{:S(2)}) collective-permute-start(bf16[192,128]{1,0:T(8,128)(2,1)S(1)} %pad_maximum_fusion.refs_0_.refs_4_), channel_id=1, source_target_pairs={{0,2},{2,4},{4,6},{6,0},{1,3},{3,5},{5,7},{7,1},{8,10},{10,12},{12... | collective-permute-start | bytes 147464 | tf_op jit(solution)/shard_map/ppermute | solution.py:302
  17.0 1.4 %collective-permute-start.4 = (f32[4,32,256]{2,1,0:T(8,128)S(1)}, f32[4,32,256]{2,1,0:T(8,128)S(1)}, u32[]{:S(2)}, u32[]{:S(2)}) collective-permute-start(f32[4,32,256]{2,1,0:T(8,128)S(1)} %bitcast.4), channel_id=1, source_target_pairs={{0,1},{1,0},{2,3},{3,2},{4,5},{5,4},{6,7},{7,6},{8,9},{9,8},{10,11... | collective-permute-start | bytes 393224 | tf_op jit(solution)/shard_map/ppermute | solution.py:302
  18.4 4.5 %collective-permute-start.5 = (f32[2,32,256]{2,1,0:T(8,128)S(1)}, f32[2,32,256]{2,1,0:T(8,128)S(1)}, u32[]{:S(2)}, u32[]{:S(2)}) collective-permute-start(f32[2,32,256]{2,1,0:T(8,128)S(1)} %slice_add_fusion), channel_id=1, source_target_pairs={{0,2},{2,0},{4,6},{6,4},{1,3},{3,1},{5,7},{7,5},{8,10},{10,8},{12,... | collective-permute-start | bytes 196616 | tf_op jit(solution)/shard_map/ppermute | solution.py:344
  18.8 5.8 %collective-permute-start.7 = (bf16[768,128]{1,0:T(8,128)(2,1)S(1)}, bf16[768,128]{1,0:T(8,128)(2,1)S(1)}, u32[]{:S(2)}, u32[]{:S(2)}) collective-permute-start(bf16[768,128]{1,0:T(8,128)(2,1)S(1)} %get-tuple-element.14.refs_0_), channel_id=1, source_target_pairs={{0,1},{1,0},{2,3},{3,2},{4,5},{5,4},{6,7},{7,6},{8,9},{9,8},{10,11... | collective-permute-start | bytes 589832 | tf_op jit(solution)/shard_map/ppermute | solution.py:302
  22.9 7.6 %collective-permute-start.6 = (f32[1,32,256]{2,1,0:T(8,128)S(1)}, f32[1,32,256]{2,1,0:T(8,128)S(1)}, u32[]{:S(2)}, u32[]{:S(2)}) collective-permute-start(f32[1,32,256]{2,1,0:T(8,128)S(1)} %get-tuple-element.15), channel_id=1, source_target_pairs={{0,4},{2,6},{4,0},{6,2},{1,5},{3,7},{5,1},{7,3},{8,12},{10,14},{12... | collective-permute-start | bytes 98312 | tf_op jit(solution)/shard_map/ppermute | solution.py:344

commit v5 on v4

--- a/solution.py
+++ b/solution.py
@@ -34,23 +34,17 @@
     return order
 
 
-def copies(nj, nk, where, block, held, arrived, t):
-    owned = held.shape[1]
-    made = []
-    for slot, u in enumerate(halving_order(nj)):
-        first = pl.multiple_of(owner(nk, where, t, u) * owned, owned)
-        rows = block.at[pl.ds(first, owned)]
-        made.append(pltpu.make_async_copy(rows, held.at[slot], arrived.at[slot]))
-    return made
-
-
 def fetch_kernel(nj, nk, where, block, held, arrived):
-    made = []
-    for t in range(1, nk):
-        made += copies(nj, nk, where, block, held.at[t - 1], arrived.at[t - 1], t)
-    for copy in made:
+    owned = held.shape[2]
+    copies = []
+    for t in range(nk):
+        for slot, u in enumerate(halving_order(nj)):
+            first = pl.multiple_of(owner(nk, where, t, u) * owned, owned)
+            rows = block.at[pl.ds(first, owned)]
+            copies.append(pltpu.make_async_copy(rows, held.at[t, slot], arrived.at[t, slot]))
+    for copy in copies:
         copy.start()
-    for copy in made:
+    for copy in copies:
         copy.wait()
 
 
@@ -59,13 +53,13 @@
     owned = rows // (nj * nk)
     return pl.pallas_call(
         functools.partial(fetch_kernel, nj, nk),
-        out_shape=jax.ShapeDtypeStruct((nk - 1, nj, owned, width_j, width_k), tensor.dtype),
+        out_shape=jax.ShapeDtypeStruct((nk, nj, owned, width_j, width_k), tensor.dtype),
         in_specs=[smem, hbm],
         out_specs=vmem,
-        scratch_shapes=[pltpu.SemaphoreType.DMA((nk - 1, nj))],
-        compiler_params=pltpu.CompilerParams(vmem_limit_bytes=46 * 2**20),
+        scratch_shapes=[pltpu.SemaphoreType.DMA((nk, nj))],
+        compiler_params=pltpu.CompilerParams(vmem_limit_bytes=42 * 2**20),
         cost_estimate=pl.CostEstimate(
-            flops=2 * 10**9, bytes_accessed=rows * width_j * width_k, transcendentals=0
+            flops=4 * 10**9, bytes_accessed=2 * rows * width_j * width_k, transcendentals=0
         ),
     )(where, tensor)
 
@@ -80,14 +74,11 @@
         out[u] = jnp.concatenate(sums, axis=0)
 
 
-def away_kernel(nj, nk, height_b, flipped, where, block, held, *refs):
+def away_kernel(nj, nk, height_b, flipped, where, held, *refs):
     line, refs = refs[:nj], refs[nj:]
     b_parts, refs = refs[:nk], refs[nk:]
-    out, own, c_cols, b_cols, home_held, b_rows, arrived = refs
+    out, own, c_cols, b_cols, b_rows = refs
     rank = c_cols.shape[1]
-    home = copies(nj, nk, where, block, home_held, arrived, 0)
-    for copy in home:
-        copy.start()
     width_c = line[0].shape[0] - height_b
     for s in range(nj):
         at = pl.multiple_of(wrap(where[0] - s, nj) * width_c, width_c)
@@ -103,13 +94,11 @@
     c_cols[...] = own[:rank, :].T
     b_cols[...] = (b_rows[...].T if flipped else b_rows[...]).astype(jnp.float32)
     for t in range(1, nk):
-        contract(held.at[t - 1], out.at[t - 1], c_cols[...], b_cols[...])
-    for copy in home:
-        copy.wait()
+        contract(held.at[t], out.at[t - 1], c_cols[...], b_cols[...])
 
 
 def home_kernel(begin, count, held, c_cols, b_cols, out):
-    contract(held.at[begin : begin + count], out, c_cols[...], b_cols[...])
+    contract(held.at[0, begin : begin + count], out, c_cols[...], b_cols[...])
 
 
 def flops_of(rows, held, rank):
@@ -120,9 +109,8 @@
     )
 
 
-def contract_away(where, tensor, held, line, b_parts, height_b, flipped, rank):
-    _, nj, owned, width_j, width_k = held.shape
-    nk = len(b_parts)
+def contract_away(where, held, line, b_parts, height_b, flipped, rank):
+    nk, nj, owned, width_j, width_k = held.shape
     width = line[0].shape[1]
     return pl.pallas_call(
         functools.partial(away_kernel, nj, nk, height_b, flipped),
@@ -131,21 +119,17 @@
             jax.ShapeDtypeStruct((rank + nj * height_b, width), held.dtype),
             jax.ShapeDtypeStruct((width_k, rank), held.dtype),
             jax.ShapeDtypeStruct((width_j, rank), jnp.float32),
-            jax.ShapeDtypeStruct(held.shape[1:], held.dtype),
         ],
-        in_specs=[smem, hbm] + [vmem] * (1 + nj + nk),
-        out_specs=[vmem] * 5,
-        scratch_shapes=[
-            pltpu.VMEM((rank, width_j) if flipped else (width_j, rank), held.dtype),
-            pltpu.SemaphoreType.DMA((nj,)),
-        ],
-        compiler_params=pltpu.CompilerParams(vmem_limit_bytes=44 * 2**20),
+        in_specs=[smem] + [vmem] * (1 + nj + nk),
+        out_specs=[vmem] * 4,
+        scratch_shapes=[pltpu.VMEM((rank, width_j) if flipped else (width_j, rank), held.dtype)],
+        compiler_params=pltpu.CompilerParams(vmem_limit_bytes=20 * 2**20),
         cost_estimate=flops_of((nk - 1) * nj * owned, held, rank),
-    )(where, tensor, held, *line, *b_parts)
+    )(where, held, *line, *b_parts)
 
 
 def contract_home(begin, count, held, c_cols, b_cols):
-    _, owned, _, _ = held.shape
+    _, _, owned, _, _ = held.shape
     rank = c_cols.shape[1]
     return pl.pallas_call(
         functools.partial(home_kernel, begin, count),
@@ -313,8 +297,8 @@
     line = [mine] + [send(mine, "ja", nj, s) for s in range(1, nj)]
     b_parts = [mine] + [send(mine, "ka", nk, t) for t in range(1, nk)]
     held = fetch(where, tensor, nj, nk)
-    away, own, c_cols, b_cols, held = contract_away(
-        where, tensor, held, line, b_parts, height_b, flipped, rank
+    away, own, c_cols, b_cols = contract_away(
+        where, held, line, b_parts, height_b, flipped, rank
     )
     half = nj // 2
     sent = contract_home(half, half, held, c_cols, b_cols)

time: 31.6 us -> 29.5 us (0.934)
  waiting for transfers between devices: 4.92 us -> 2.41 us
  starting transfers between devices: 8.44 us -> 9.68 us
  Pallas kernels: 17 us -> 16.2 us
    pallas_call x1, Pallas kernels: 5.06 us -> 2.98 us  [contract_away(): pl.pallas_call(functools.partial(away_kernel, nj, nk, height_b, flipped),...]
    ppermute x6, waiting for transfers between devices: 2.26 us -> 0.99 us  [send(): return lax.ppermute(x, axis, shift(n, s))]
    pallas_call x1, Pallas kernels: 2.75 us -> 4.02 us  [fetch(): pl.pallas_call(functools.partial(fetch_kernel, nj, nk), out_shape=jax.Sha...]
    ppermute x2, starting transfers between devices: 2.08 us -> 3.34 us  [update(): received = lax.ppermute(sent, 'ja', [(i, i ^ bit) for i in range(nj)])]
    ppermute x2, waiting for transfers between devices: 2.67 us -> 1.43 us  [update(): received = lax.ppermute(sent, 'ja', [(i, i ^ bit) for i in range(nj)])]
  transfers between devices with their start and end apart: 8 -> 8, of which waited for: 3 -> 3; matrix products, arithmetic and copies ran while one was open for 0% -> 0% of each run, Pallas kernels for 35% -> 42%
where the time goes in v5:
time: 29.5 us; the launch traced here: 29.3 us
  Pallas kernels  16.2 us (55%)
  starting transfers between devices  9.68 us (33%)
  waiting for transfers between devices  2.41 us (8%)
  other arithmetic  0.88 us (3%)
    ppermute x6, starting transfers between devices, send(): return lax.ppermute(x, axis, shift(n, s))  6.34 us
    pallas_call x1, Pallas kernels, fetch(): pl.pallas_call(functools.partial(fetch_kernel, nj, nk), out_shape=jax.Sha...  4.02 us
    pallas_call x1, Pallas kernels, update(): pl.pallas_call(functools.partial(rest_kernel, blocks), out_shape=square,...  3.74 us
    ppermute x2, starting transfers between devices, update(): received = lax.ppermute(sent, 'ja', [(i, i ^ bit) for i in range(nj)])  3.34 us
    pallas_call x1, Pallas kernels, contract_away(): pl.pallas_call(functools.partial(away_kernel, nj, nk, height_b, flipped),...  2.98 us
    pallas_call x2, Pallas kernels, contract_home(): pl.pallas_call(functools.partial(home_kernel, begin, count), out_shape=ja...  2.5 us
    pallas_call x1, Pallas kernels, update(): pl.pallas_call(functools.partial(inverse_kernel, nj, nk, height_b, flippe...  2.15 us
    ppermute x2, waiting for transfers between devices, update(): received = lax.ppermute(sent, 'ja', [(i, i ^ bit) for i in range(nj)])  1.43 us
  transfers between devices with their start and end apart: 8, of which 3 were waited for; matrix products, arithmetic and copies ran while one was open for 0% of the time, Pallas kernels for 42%

profile of v5, /device:TPU:0, one launch (start us, length us, event | category | flops | bytes accessed | tf_op | source)
XLA Modules:
  0.0 29.3 jit_solution(16929986256136484202)
XLA Ops:
  0.0 0.8 %pad_maximum_fusion.refs_0_.refs_4_ = bf16[192,128]{1,0:T(8,128)(2,1)S(1)} fusion(bf16[64,128]{1,0:T(8,128)(2,1)} %bitcast.5, bf16[128,128]{1,0:T(8,128)(2,1)} %param.4), kind=kLoop, calls=%fused_computation.3 | loop fusion | flops 98304 | bytes 98304 | tf_op jit(solution)/shard_map/concatenate | solution.py:296
  0.8 0.5 %collective-permute-start.3 = (bf16[192,128]{1,0:T(8,128)(2,1)S(1)}, bf16[192,128]{1,0:T(8,128)(2,1)S(1)}, u32[]{:S(2)}, u32[]{:S(2)}) collective-permute-start(bf16[192,128]{1,0:T(8,128)(2,1)S(1)} %pad_maximum_fusion.refs_0_.refs_4_), channel_id=1, source_target_pairs={{0,1},{1,0},{2,3},{3,2},{4,5},{5,4},{6,7},{7,6},{8,9},{9,8},{10,11... | collective-permute-start | bytes 147464 | tf_op jit(solution)/shard_map/ppermute | solution.py:286
  1.3 4.6 %collective-permute-start.2 = (bf16[192,128]{1,0:T(8,128)(2,1)S(1)}, bf16[192,128]{1,0:T(8,128)(2,1)S(1)}, u32[]{:S(2)}, u32[]{:S(2)}) collective-permute-start(bf16[192,128]{1,0:T(8,128)(2,1)S(1)} %pad_maximum_fusion.refs_0_.refs_4_), channel_id=1, source_target_pairs={{0,6},{2,0},{4,2},{6,4},{1,7},{3,1},{5,3},{7,5},{8,14},{10,8},{12,... | collective-permute-start | bytes 147464 | tf_op jit(solution)/shard_map/ppermute | solution.py:286
  5.9 0.0 collective-permute-start.1
  5.9 1.0 %collective-permute-start = (bf16[192,128]{1,0:T(8,128)(2,1)S(1)}, bf16[192,128]{1,0:T(8,128)(2,1)S(1)}, u32[]{:S(2)}, u32[]{:S(2)}) collective-permute-start(bf16[192,128]{1,0:T(8,128)(2,1)S(1)} %pad_maximum_fusion.refs_0_.refs_4_), channel_id=1, source_target_pairs={{0,2},{2,4},{4,6},{6,0},{1,3},{3,5},{5,7},{7,1},{8,10},{10,12},{12... | collective-permute-start | bytes 147464 | tf_op jit(solution)/shard_map/ppermute | solution.py:286
  6.9 0.1 pad_add_fusion.where
  7.0 4.0 %shard_map.37.held = bf16[2,4,32,128,128]{4,3,2,1,0:T(8,128)(2,1)S(1)} custom-call(s32[2]{0:T(128)S(1)} %pad_add_fusion.where, bf16[256,128,128]{2,1,0:T(8,128)(2,1)} %block.1), custom_call_target="tpu_custom_call" | custom-call | flops 4000000000 | bytes 8388608 | tf_op jit(solution)/shard_map/pallas_call | solution.py:54
  11.0 0.0 collective-permute-done.2.refs_3_
  11.0 0.9 %collective-permute-done.1.refs_2_ = bf16[192,128]{1,0:T(8,128)(2,1)S(1)} collective-permute-done((bf16[192,128]{1,0:T(8,128)(2,1)S(1)}, bf16[192,128]{1,0:T(8,128)(2,1)S(1)}, u32[]{:S(2)}, u32[]{:S(2)}) %collective-permute-start.1) | collective-permute-done | bytes 49184 | tf_op jit(solution)/shard_map/ppermute | solution.py:286
  11.9 0.0 collective-permute-done.refs_1_
  11.9 3.0 %shard_map.38 = (f32[1,4,32,256]{3,2,1,0:T(8,128)S(1)}, bf16[768,128]{1,0:T(8,128)(2,1)S(1)}, bf16[128,256]{1,0:T(8,128)(2,1)S(1)}, f32[128,256]{1,0:T(8,128)S(1)}) custom-call(s32[2]{0:T(128)S(1)} %pad_add_fusion.where, bf16[2,4,32,128,128]{4,3,2,1,0:T(8,128)(2,1)S(1)} %shard_map.37.held, bf16[192,128]{1,0:T(8,128)(2,1)S(1)} %pad_maximum_fusion.refs_0_.refs_4_, ...), custom_call_target="tpu_custom_call" | custom-call | flops 1073741824 | bytes 1048576 | tf_op jit(solution)/shard_map/pallas_call | solution.py:115
  14.9 0.1 collective-permute-start.4
  15.0 1.3 %shard_map.40 = f32[2,32,256]{2,1,0:T(8,128)S(1)} custom-call(bf16[2,4,32,128,128]{4,3,2,1,0:T(8,128)(2,1)S(1)} %shard_map.37.held, bf16[128,256]{1,0:T(8,128)(2,1)S(1)} %get-tuple-element.9.c_cols, f32[128,256]{1,0:T(8,128)S(1)} %get-tuple-element.10.b_cols), custom_call_target="tpu_custom_call" | custom-call | flops 536870912 | bytes 1048576 | tf_op jit(solution)/shard_map/pallas_call | solution.py:134
  16.2 0.1 collective-permute-done.4
  16.3 1.7 %collective-permute-start.5 = (f32[2,32,256]{2,1,0:T(8,128)S(1)}, f32[2,32,256]{2,1,0:T(8,128)S(1)}, u32[]{:S(2)}, u32[]{:S(2)}) collective-permute-start(f32[2,32,256]{2,1,0:T(8,128)S(1)} %slice_add_fusion), channel_id=1, source_target_pairs={{0,2},{2,0},{4,6},{6,4},{1,3},{3,1},{5,7},{7,5},{8,10},{10,8},{12,... | collective-permute-start | bytes 196616 | tf_op jit(solution)/shard_map/ppermute | solution.py:328
  18.0 0.2 collective-permute-start.7
  18.2 1.3 %shard_map.39 = f32[2,32,256]{2,1,0:T(8,128)S(1)} custom-call(bf16[2,4,32,128,128]{4,3,2,1,0:T(8,128)(2,1)S(1)} %shard_map.37.held, bf16[128,256]{1,0:T(8,128)(2,1)S(1)} %get-tuple-element.9.c_cols, f32[128,256]{1,0:T(8,128)S(1)} %get-tuple-element.10.b_cols), custom_call_target="tpu_custom_call" | custom-call | flops 536870912 | bytes 1048576 | tf_op jit(solution)/shard_map/pallas_call | solution.py:134
  19.4 1.4 %collective-permute-done.5 = f32[2,32,256]{2,1,0:T(8,128)S(1)} collective-permute-done((f32[2,32,256]{2,1,0:T(8,128)S(1)}, f32[2,32,256]{2,1,0:T(8,128)S(1)}, u32[]{:S(2)}, u32[]{:S(2)}) %collective-permute-start.5) | collective-permute-done | bytes 65568 | tf_op jit(solution)/shard_map/ppermute | solution.py:328
  20.9 1.7 %collective-permute-start.6 = (f32[1,32,256]{2,1,0:T(8,128)S(1)}, f32[1,32,256]{2,1,0:T(8,128)S(1)}, u32[]{:S(2)}, u32[]{:S(2)}) collective-permute-start(f32[1,32,256]{2,1,0:T(8,128)S(1)} %get-tuple-element.13), channel_id=1, source_target_pairs={{0,4},{2,6},{4,0},{6,2},{1,5},{3,7},{5,1},{7,3},{8,12},{10,14},{12... | collective-permute-start | bytes 98312 | tf_op jit(solution)/shard_map/ppermute | solution.py:328
  22.5 0.0 collective-permute-done.7.refs_1_
  22.6 2.1 %shard_map.41.half_done = f32[256,256]{1,0:T(8,128)S(1)} custom-call(s32[2]{0:T(128)S(1)} %pad_add_fusion.where, bf16[768,128]{1,0:T(8,128)(2,1)S(1)} %get-tuple-element.12.refs_0_, bf16[768,128]{1,0:T(8,128)(2,1)S(1)} %collective-permute-done.7.refs_1_), custom_call_target="tpu_custom_call" | custom-call | flops 5000000000 | bytes 1048576 | tf_op jit(solution)/shard_map/pallas_call | solution.py:317
  24.7 3.7 %shard_map.42.inverse = f32[256,256]{1,0:T(8,128)S(1)} custom-call(f32[256,256]{1,0:T(8,128)S(1)} %shard_map.41.half_done), custom_call_target="tpu_custom_call" | custom-call | flops 5000000000 | bytes 1048576 | tf_op jit(solution)/shard_map/pallas_call | solution.py:333
  28.5 0.0 collective-permute-done.6.received
  28.5 0.8 %shard_map.43 = f32[32,256]{1,0:T(8,128)} custom-call(f32[1,32,256]{2,1,0:T(8,128)S(1)} %get-tuple-element.14.kept, f32[1,32,256]{2,1,0:T(8,128)S(1)} %collective-permute-done.6.received, f32[256,256]{1,0:T(8,128)S(1)} %shard_map.42.inverse), custom_call_target="tpu_custom_call" | custom-call | flops 100000000 | bytes 524288 | tf_op jit(solution)/shard_map/pallas_call | solution.py:341
  (4 shorter events, 0.0 us)
Async XLA Ops:
  0.8 10.2 %collective-permute-start.3 = (bf16[192,128]{1,0:T(8,128)(2,1)S(1)}, bf16[192,128]{1,0:T(8,128)(2,1)S(1)}, u32[]{:S(2)}, u32[]{:S(2)}) collective-permute-start(bf16[192,128]{1,0:T(8,128)(2,1)S(1)} %pad_maximum_fusion.refs_0_.refs_4_), channel_id=1, source_target_pairs={{0,1},{1,0},{2,3},{3,2},{4,5},{5,4},{6,7},{7,6},{8,9},{9,8},{10,11... | collective-permute-start | bytes 147464 | tf_op jit(solution)/shard_map/ppermute | solution.py:286
  1.3 9.7 %collective-permute-start.2 = (bf16[192,128]{1,0:T(8,128)(2,1)S(1)}, bf16[192,128]{1,0:T(8,128)(2,1)S(1)}, u32[]{:S(2)}, u32[]{:S(2)}) collective-permute-start(bf16[192,128]{1,0:T(8,128)(2,1)S(1)} %pad_maximum_fusion.refs_0_.refs_4_), channel_id=1, source_target_pairs={{0,6},{2,0},{4,2},{6,4},{1,7},{3,1},{5,3},{7,5},{8,14},{10,8},{12,... | collective-permute-start | bytes 147464 | tf_op jit(solution)/shard_map/ppermute | solution.py:286
  5.9 6.0 %collective-permute-start.1 = (bf16[192,128]{1,0:T(8,128)(2,1)S(1)}, bf16[192,128]{1,0:T(8,128)(2,1)S(1)}, u32[]{:S(2)}, u32[]{:S(2)}) collective-permute-start(bf16[192,128]{1,0:T(8,128)(2,1)S(1)} %pad_maximum_fusion.refs_0_.refs_4_), channel_id=1, source_target_pairs={{0,4},{2,6},{4,0},{6,2},{1,5},{3,7},{5,1},{7,3},{8,12},{10,14},{12... | collective-permute-start | bytes 147464 | tf_op jit(solution)/shard_map/ppermute | solution.py:286
  5.9 6.0 %collective-permute-start = (bf16[192,128]{1,0:T(8,128)(2,1)S(1)}, bf16[192,128]{1,0:T(8,128)(2,1)S(1)}, u32[]{:S(2)}, u32[]{:S(2)}) collective-permute-start(bf16[192,128]{1,0:T(8,128)(2,1)S(1)} %pad_maximum_fusion.refs_0_.refs_4_), channel_id=1, source_target_pairs={{0,2},{2,4},{4,6},{6,0},{1,3},{3,5},{5,7},{7,1},{8,10},{10,12},{12... | collective-permute-start | bytes 147464 | tf_op jit(solution)/shard_map/ppermute | solution.py:286
  14.9 1.4 %collective-permute-start.4 = (f32[4,32,256]{2,1,0:T(8,128)S(1)}, f32[4,32,256]{2,1,0:T(8,128)S(1)}, u32[]{:S(2)}, u32[]{:S(2)}) collective-permute-start(f32[4,32,256]{2,1,0:T(8,128)S(1)} %bitcast.4), channel_id=1, source_target_pairs={{0,1},{1,0},{2,3},{3,2},{4,5},{5,4},{6,7},{7,6},{8,9},{9,8},{10,11... | collective-permute-start | bytes 393224 | tf_op jit(solution)/shard_map/ppermute | solution.py:286
  16.3 4.5 %collective-permute-start.5 = (f32[2,32,256]{2,1,0:T(8,128)S(1)}, f32[2,32,256]{2,1,0:T(8,128)S(1)}, u32[]{:S(2)}, u32[]{:S(2)}) collective-permute-start(f32[2,32,256]{2,1,0:T(8,128)S(1)} %slice_add_fusion), channel_id=1, source_target_pairs={{0,2},{2,0},{4,6},{6,4},{1,3},{3,1},{5,7},{7,5},{8,10},{10,8},{12,... | collective-permute-start | bytes 196616 | tf_op jit(solution)/shard_map/ppermute | solution.py:328
  18.0 4.6 %collective-permute-start.7 = (bf16[768,128]{1,0:T(8,128)(2,1)S(1)}, bf16[768,128]{1,0:T(8,128)(2,1)S(1)}, u32[]{:S(2)}, u32[]{:S(2)}) collective-permute-start(bf16[768,128]{1,0:T(8,128)(2,1)S(1)} %get-tuple-element.12.refs_0_), channel_id=1, source_target_pairs={{0,1},{1,0},{2,3},{3,2},{4,5},{5,4},{6,7},{7,6},{8,9},{9,8},{10,11... | collective-permute-start | bytes 589832 | tf_op jit(solution)/shard_map/ppermute | solution.py:286
  20.9 7.6 %collective-permute-start.6 = (f32[1,32,256]{2,1,0:T(8,128)S(1)}, f32[1,32,256]{2,1,0:T(8,128)S(1)}, u32[]{:S(2)}, u32[]{:S(2)}) collective-permute-start(f32[1,32,256]{2,1,0:T(8,128)S(1)} %get-tuple-element.13), channel_id=1, source_target_pairs={{0,4},{2,6},{4,0},{6,2},{1,5},{3,7},{5,1},{7,3},{8,12},{10,14},{12... | collective-permute-start | bytes 98312 | tf_op jit(solution)/shard_map/ppermute | solution.py:328

commit v6 on v5

--- a/solution.py
+++ b/solution.py
@@ -94,11 +94,12 @@
     c_cols[...] = own[:rank, :].T
     b_cols[...] = (b_rows[...].T if flipped else b_rows[...]).astype(jnp.float32)
     for t in range(1, nk):
-        contract(held.at[t], out.at[t - 1], c_cols[...], b_cols[...])
-
-
-def home_kernel(begin, count, held, c_cols, b_cols, out):
-    contract(held.at[0, begin : begin + count], out, c_cols[...], b_cols[...])
+        contract(held.at[t, nj // 2 :], out.at[t - 1], c_cols[...], b_cols[...])
+
+
+def rows_kernel(turns, begin, count, held, c_cols, b_cols, out):
+    for slot, t in enumerate(turns):
+        contract(held.at[t, begin : begin + count], out.at[slot], c_cols[...], b_cols[...])
 
 
 def flops_of(rows, held, rank):
@@ -115,7 +116,7 @@
     return pl.pallas_call(
         functools.partial(away_kernel, nj, nk, height_b, flipped),
         out_shape=[
-            jax.ShapeDtypeStruct((nk - 1, nj, owned, rank), jnp.float32),
+            jax.ShapeDtypeStruct((nk - 1, nj // 2, owned, rank), jnp.float32),
             jax.ShapeDtypeStruct((rank + nj * height_b, width), held.dtype),
             jax.ShapeDtypeStruct((width_k, rank), held.dtype),
             jax.ShapeDtypeStruct((width_j, rank), jnp.float32),
@@ -124,20 +125,19 @@
         out_specs=[vmem] * 4,
         scratch_shapes=[pltpu.VMEM((rank, width_j) if flipped else (width_j, rank), held.dtype)],
         compiler_params=pltpu.CompilerParams(vmem_limit_bytes=20 * 2**20),
-        cost_estimate=flops_of((nk - 1) * nj * owned, held, rank),
+        cost_estimate=flops_of((nk - 1) * nj * owned // 2, held, rank),
     )(where, held, *line, *b_parts)
 
 
-def contract_home(begin, count, held, c_cols, b_cols):
-    _, _, owned, _, _ = held.shape
-    rank = c_cols.shape[1]
+def contract_rows(turns, begin, count, held, c_cols, b_cols):
+    owned, rank = held.shape[2], c_cols.shape[1]
     return pl.pallas_call(
-        functools.partial(home_kernel, begin, count),
-        out_shape=jax.ShapeDtypeStruct((count, owned, rank), jnp.float32),
+        functools.partial(rows_kernel, turns, begin, count),
+        out_shape=jax.ShapeDtypeStruct((len(turns), count, owned, rank), jnp.float32),
         in_specs=[vmem] * 3,
         out_specs=vmem,
         compiler_params=pltpu.CompilerParams(vmem_limit_bytes=20 * 2**20),
-        cost_estimate=flops_of(count * owned, held, rank),
+        cost_estimate=flops_of(len(turns) * count * owned, held, rank),
     )(held, c_cols, b_cols)
 
 
@@ -244,8 +244,8 @@
                 a[8 * g : 8 * g + 8, 128 * w : 128 * w + 128] = value
 
 
-def inverse_kernel(nj, nk, height_b, flipped, blocks, where, *refs):
-    owns, (out, b_all) = refs[:nk], refs[nk:]
+def first_kernel(nj, nk, height_b, flipped, blocks, where, held, c_cols, b_cols, *refs):
+    owns, (kept, out, b_all) = refs[:nk], refs[nk:]
     rank = out.shape[1]
 
     def gram(x, contracted):
@@ -269,6 +269,7 @@
         jnp.int32, out.shape, 1
     )
     out[...] = gram_b * gram_c + jnp.where(diagonal, ridge_weight, 0.0)
+    contract(held.at[0, : nj // 2], kept, c_cols[...], b_cols[...])
     invert(out, 0, blocks)
 
 
@@ -301,35 +302,34 @@
         where, held, line, b_parts, height_b, flipped, rank
     )
     half = nj // 2
-    sent = contract_home(half, half, held, c_cols, b_cols)
-    for t in range(1, nk):
-        received = send(away[t - 1], "ka", nk, t)
-        sent = sent + received[half:]
-        away_kept = received[:half] if t == 1 else away_kept + received[:half]
-    owns = [own] + [send(own, "ka", nk, t) for t in range(1, nk)]
-    kept = contract_home(0, half, held, c_cols, b_cols)
-    kept = kept + away_kept
+    turns = tuple(range(1, nk))
+    owns = [own] + [send(own, "ka", nk, t) for t in turns]
+    sent = contract_rows((0,), half, half, held, c_cols, b_cols)[0]
+    for t in turns:
+        sent = sent + send(away[t - 1], "ka", nk, t)
+    received = lax.ppermute(sent, "ja", [(i, i ^ 1) for i in range(nj)])
+    away = contract_rows(turns, 0, half, held, c_cols, b_cols)
     params = pltpu.CompilerParams(vmem_limit_bytes=20 * 2**20)
     cost = pl.CostEstimate(flops=5 * 10**9, bytes_accessed=2**20, transcendentals=0)
     square = jax.ShapeDtypeStruct((rank, rank), jnp.float32)
     blocks = rank // 64 * 16
     b_shape = (nj, rank, mine.shape[1]) if flipped else (nj, height_b, rank)
-    half_done = pl.pallas_call(
-        functools.partial(inverse_kernel, nj, nk, height_b, flipped, blocks),
-        out_shape=square,
-        in_specs=[smem] + [vmem] * nk,
-        out_specs=vmem,
+    kept, half_done = pl.pallas_call(
+        functools.partial(first_kernel, nj, nk, height_b, flipped, blocks),
+        out_shape=[jax.ShapeDtypeStruct(sent.shape, jnp.float32), square],
+        in_specs=[smem] + [vmem] * (3 + nk),
+        out_specs=[vmem] * 2,
         scratch_shapes=[pltpu.VMEM(b_shape, mine.dtype)],
         compiler_params=params,
         cost_estimate=cost,
-    )(where, *owns)
-    bit = 1
-    while True:
+    )(where, held, c_cols, b_cols, *owns)
+    for t in turns:
+        kept = kept + send(away[t - 1], "ka", nk, t)
+    bit = 2
+    while bit < nj:
+        kept, sent = jnp.split(kept + received, 2, axis=0)
         received = lax.ppermute(sent, "ja", [(i, i ^ bit) for i in range(nj)])
         bit *= 2
-        if bit == nj:
-            break
-        kept, sent = jnp.split(kept + received, 2, axis=0)
     inverse = pl.pallas_call(
         functools.partial(rest_kernel, blocks),
         out_shape=square,

time: 29.5 us -> 27.8 us (0.942)
  waiting for transfers between devices: 2.41 us -> 0.63 us
    ppermute x2 -> x1, starting transfers between devices: 3.34 us -> 0.91 us  [update(): received = lax.ppermute(sent, 'ja', [(i, i ^ bit) for i in range(nj)])]
    ppermute x6 -> x7, starting transfers between devices: 6.34 us -> 8.14 us  [send(): return lax.ppermute(x, axis, shift(n, s))]
    ppermute x2 -> x1, waiting for transfers between devices: 1.43 us -> 0.24 us  [update(): received = lax.ppermute(sent, 'ja', [(i, i ^ bit) for i in range(nj)])]
    pallas_call x1, Pallas kernels: 2.98 us -> 1.88 us  [contract_away(): pl.pallas_call(functools.partial(away_kernel, nj, nk, height_b, flipped),...]
    pallas_call x3, Pallas kernels: 4.65 us -> 5.69 us  [the longest x1 3.19 us: update(): pl.pallas_call(functools.partial(first_kernel, nj, nk, height_b, flipped,...]
    ppermute x6 -> x7, waiting for transfers between devices: 0.99 us -> 0.02 us  [send(): return lax.ppermute(x, axis, shift(n, s))]
    ppermute x0 -> x1, starting transfers between devices: none -> 0.74 us  [update(): received = lax.ppermute(sent, 'ja', [(i, i ^ 1) for i in range(nj)])]
    ppermute x0 -> x1, waiting for transfers between devices: none -> 0.38 us  [update(): received = lax.ppermute(sent, 'ja', [(i, i ^ 1) for i in range(nj)])]
  transfers between devices with their start and end apart: 8 -> 9, of which waited for: 3 -> 2; matrix products, arithmetic and copies ran while one was open for 0% -> 0% of each run, Pallas kernels for 42% -> 49%
where the time goes in v6:
time: 27.8 us; the launch traced here: 27.6 us
  Pallas kernels  16.2 us (58%)
  starting transfers between devices  9.79 us (35%)
  other arithmetic  0.88 us (3%)
  waiting for transfers between devices  0.63 us (2%)
    ppermute x7, starting transfers between devices, send(): return lax.ppermute(x, axis, shift(n, s))  8.14 us
    pallas_call x1, Pallas kernels, fetch(): pl.pallas_call(functools.partial(fetch_kernel, nj, nk), out_shape=jax.Sha...  4.02 us
    pallas_call x1, Pallas kernels, update(): pl.pallas_call(functools.partial(rest_kernel, blocks), out_shape=square,...  3.73 us
    pallas_call x1, Pallas kernels, update(): pl.pallas_call(functools.partial(first_kernel, nj, nk, height_b, flipped,...  3.19 us
    pallas_call x2, Pallas kernels, contract_rows(): pl.pallas_call(functools.partial(rows_kernel, turns, begin, count), out_s...  2.5 us
    pallas_call x1, Pallas kernels, contract_away(): pl.pallas_call(functools.partial(away_kernel, nj, nk, height_b, flipped),...  1.88 us
    ppermute x1, starting transfers between devices, update(): received = lax.ppermute(sent, 'ja', [(i, i ^ bit) for i in range(nj)])  0.91 us
    pallas_call x1, Pallas kernels, update(): pl.pallas_call(solve_kernel, out_shape=jax.ShapeDtypeStruct(kept.shape[1:...  0.85 us
  transfers between devices with their start and end apart: 9, of which 2 were waited for; matrix products, arithmetic and copies ran while one was open for 0% of the time, Pallas kernels for 49%

profile of v6, /device:TPU:0, one launch (start us, length us, event | category | flops | bytes accessed | tf_op | source)
XLA Modules:
  0.0 27.6 jit_solution(17681194777284728516)
XLA Ops:
  0.0 0.8 %pad_maximum_fusion.refs_0_.refs_4_ = bf16[192,128]{1,0:T(8,128)(2,1)S(1)} fusion(bf16[64,128]{1,0:T(8,128)(2,1)} %bitcast.9, bf16[128,128]{1,0:T(8,128)(2,1)} %param.4), kind=kLoop, calls=%fused_computation.2 | loop fusion | flops 98304 | bytes 98304 | tf_op jit(solution)/shard_map/concatenate | solution.py:297
  0.8 3.1 %collective-permute-start = (bf16[192,128]{1,0:T(8,128)(2,1)S(1)}, bf16[192,128]{1,0:T(8,128)(2,1)S(1)}, u32[]{:S(2)}, u32[]{:S(2)}) collective-permute-start(bf16[192,128]{1,0:T(8,128)(2,1)S(1)} %pad_maximum_fusion.refs_0_.refs_4_), channel_id=1, source_target_pairs={{0,2},{2,4},{4,6},{6,0},{1,3},{3,5},{5,7},{7,1},{8,10},{10,12},{12... | collective-permute-start | bytes 147464 | tf_op jit(solution)/shard_map/ppermute | solution.py:287
  3.8 2.6 %collective-permute-start.1 = (bf16[192,128]{1,0:T(8,128)(2,1)S(1)}, bf16[192,128]{1,0:T(8,128)(2,1)S(1)}, u32[]{:S(2)}, u32[]{:S(2)}) collective-permute-start(bf16[192,128]{1,0:T(8,128)(2,1)S(1)} %pad_maximum_fusion.refs_0_.refs_4_), channel_id=1, source_target_pairs={{0,4},{2,6},{4,0},{6,2},{1,5},{3,7},{5,1},{7,3},{8,12},{10,14},{12... | collective-permute-start | bytes 147464 | tf_op jit(solution)/shard_map/ppermute | solution.py:287
  6.4 1.3 %collective-permute-start.2 = (bf16[192,128]{1,0:T(8,128)(2,1)S(1)}, bf16[192,128]{1,0:T(8,128)(2,1)S(1)}, u32[]{:S(2)}, u32[]{:S(2)}) collective-permute-start(bf16[192,128]{1,0:T(8,128)(2,1)S(1)} %pad_maximum_fusion.refs_0_.refs_4_), channel_id=1, source_target_pairs={{0,6},{2,0},{4,2},{6,4},{1,7},{3,1},{5,3},{7,5},{8,14},{10,8},{12,... | collective-permute-start | bytes 147464 | tf_op jit(solution)/shard_map/ppermute | solution.py:287
  7.8 0.0 collective-permute-start.3
  7.8 0.1 pad_add_fusion.where
  7.8 4.0 %shard_map.37.held = bf16[2,4,32,128,128]{4,3,2,1,0:T(8,128)(2,1)S(1)} custom-call(s32[2]{0:T(128)S(1)} %pad_add_fusion.where, bf16[256,128,128]{2,1,0:T(8,128)(2,1)} %block.1), custom_call_target="tpu_custom_call" | custom-call | flops 4000000000 | bytes 8388608 | tf_op jit(solution)/shard_map/pallas_call | solution.py:54
  11.9 0.0 collective-permute-done.refs_1_
  11.9 0.0 collective-permute-done.1.refs_2_
  11.9 0.0 collective-permute-done.3.refs_5_
  11.9 1.9 %shard_map.38 = (f32[1,2,32,256]{3,2,1,0:T(8,128)S(1)}, bf16[768,128]{1,0:T(8,128)(2,1)S(1)}, bf16[128,256]{1,0:T(8,128)(2,1)S(1)}, f32[128,256]{1,0:T(8,128)S(1)}) custom-call(s32[2]{0:T(128)S(1)} %pad_add_fusion.where, bf16[2,4,32,128,128]{4,3,2,1,0:T(8,128)(2,1)S(1)} %shard_map.37.held, bf16[192,128]{1,0:T(8,128)(2,1)S(1)} %pad_maximum_fusion.refs_0_.refs_4_, ...), custom_call_target="tpu_custom_call" | custom-call | flops 536870912 | bytes 1048576 | tf_op jit(solution)/shard_map/pallas_call | solution.py:116
  13.8 0.6 %collective-permute-start.6 = (f32[2,32,256]{2,1,0:T(8,128)S(1)}, f32[2,32,256]{2,1,0:T(8,128)S(1)}, u32[]{:S(2)}, u32[]{:S(2)}) collective-permute-start(f32[2,32,256]{2,1,0:T(8,128)S(1)} %bitcast.8), channel_id=1, source_target_pairs={{0,1},{1,0},{2,3},{3,2},{4,5},{5,4},{6,7},{7,6},{8,9},{9,8},{10,11... | collective-permute-start | bytes 196616 | tf_op jit(solution)/shard_map/ppermute | solution.py:287
  14.4 0.1 collective-permute-start.4
  14.5 1.3 %shard_map.40 = f32[1,2,32,256]{3,2,1,0:T(8,128)S(1)} custom-call(bf16[2,4,32,128,128]{4,3,2,1,0:T(8,128)(2,1)S(1)} %shard_map.37.held, bf16[128,256]{1,0:T(8,128)(2,1)S(1)} %get-tuple-element.11.c_cols, f32[128,256]{1,0:T(8,128)S(1)} %get-tuple-element.12.b_cols), custom_call_target="tpu_custom_call" | custom-call | flops 536870912 | bytes 1048576 | tf_op jit(solution)/shard_map/pallas_call | solution.py:134
  15.7 0.5 %collective-permute-start.5 = (f32[2,32,256]{2,1,0:T(8,128)S(1)}, f32[2,32,256]{2,1,0:T(8,128)S(1)}, u32[]{:S(2)}, u32[]{:S(2)}) collective-permute-start(f32[2,32,256]{2,1,0:T(8,128)S(1)} %bitcast.7), channel_id=1, source_target_pairs={{0,1},{1,0},{2,3},{3,2},{4,5},{5,4},{6,7},{7,6},{8,9},{9,8},{10,11... | collective-permute-start | bytes 196616 | tf_op jit(solution)/shard_map/ppermute | solution.py:287
  16.2 1.2 %shard_map.41 = f32[1,2,32,256]{3,2,1,0:T(8,128)S(1)} custom-call(bf16[2,4,32,128,128]{4,3,2,1,0:T(8,128)(2,1)S(1)} %shard_map.37.held, bf16[128,256]{1,0:T(8,128)(2,1)S(1)} %get-tuple-element.11.c_cols, f32[128,256]{1,0:T(8,128)S(1)} %get-tuple-element.12.b_cols), custom_call_target="tpu_custom_call" | custom-call | flops 536870912 | bytes 1048576 | tf_op jit(solution)/shard_map/pallas_call | solution.py:134
  17.5 0.7 %collective-permute-start.7 = (f32[2,32,256]{2,1,0:T(8,128)S(1)}, f32[2,32,256]{2,1,0:T(8,128)S(1)}, u32[]{:S(2)}, u32[]{:S(2)}) collective-permute-start(f32[2,32,256]{2,1,0:T(8,128)S(1)} %bitcast_add_fusion), channel_id=1, source_target_pairs={{0,2},{2,0},{4,6},{6,4},{1,3},{3,1},{5,7},{7,5},{8,10},{10,8},{12,... | collective-permute-start | bytes 196616 | tf_op jit(solution)/shard_map/ppermute | solution.py:310
  18.2 0.0 collective-permute-done.4.refs_1_
  18.2 3.2 %shard_map.39 = (f32[2,32,256]{2,1,0:T(8,128)S(1)}, f32[256,256]{1,0:T(8,128)S(1)}) custom-call(s32[2]{0:T(128)S(1)} %pad_add_fusion.where, bf16[2,4,32,128,128]{4,3,2,1,0:T(8,128)(2,1)S(1)} %shard_map.37.held, bf16[128,256]{1,0:T(8,128)(2,1)S(1)} %get-tuple-element.11.c_cols, f32[128,256]{1,0:T(8,128)S(1)} %get-tuple-element.12.b_cols, ...), custom_call_target="tpu_custom_call" | custom-call | flops 5000000000 | bytes 1048576 | tf_op jit(solution)/shard_map/pallas_call | solution.py:317
  21.4 0.4 %collective-permute-done.7 = f32[2,32,256]{2,1,0:T(8,128)S(1)} collective-permute-done((f32[2,32,256]{2,1,0:T(8,128)S(1)}, f32[2,32,256]{2,1,0:T(8,128)S(1)}, u32[]{:S(2)}, u32[]{:S(2)}) %collective-permute-start.7) | collective-permute-done | bytes 65568 | tf_op jit(solution)/shard_map/ppermute | solution.py:310
  21.9 0.9 %collective-permute-start.8 = (f32[1,32,256]{2,1,0:T(8,128)S(1)}, f32[1,32,256]{2,1,0:T(8,128)S(1)}, u32[]{:S(2)}, u32[]{:S(2)}) collective-permute-start(f32[1,32,256]{2,1,0:T(8,128)S(1)} %get-tuple-element.17), channel_id=1, source_target_pairs={{0,4},{2,6},{4,0},{6,2},{1,5},{3,7},{5,1},{7,3},{8,12},{10,14},{12... | collective-permute-start | bytes 98312 | tf_op jit(solution)/shard_map/ppermute | solution.py:331
  22.8 3.7 %shard_map.42.inverse = f32[256,256]{1,0:T(8,128)S(1)} custom-call(f32[256,256]{1,0:T(8,128)S(1)} %get-tuple-element.16.half_done), custom_call_target="tpu_custom_call" | custom-call | flops 5000000000 | bytes 1048576 | tf_op jit(solution)/shard_map/pallas_call | solution.py:333
  26.5 0.2 collective-permute-done.8.received
  26.7 0.8 %shard_map.43 = f32[32,256]{1,0:T(8,128)} custom-call(f32[1,32,256]{2,1,0:T(8,128)S(1)} %get-tuple-element.18.kept, f32[1,32,256]{2,1,0:T(8,128)S(1)} %collective-permute-done.8.received, f32[256,256]{1,0:T(8,128)S(1)} %shard_map.42.inverse), custom_call_target="tpu_custom_call" | custom-call | flops 100000000 | bytes 524288 | tf_op jit(solution)/shard_map/pallas_call | solution.py:341
  (6 shorter events, 0.0 us)
Async XLA Ops:
  0.8 11.1 %collective-permute-start = (bf16[192,128]{1,0:T(8,128)(2,1)S(1)}, bf16[192,128]{1,0:T(8,128)(2,1)S(1)}, u32[]{:S(2)}, u32[]{:S(2)}) collective-permute-start(bf16[192,128]{1,0:T(8,128)(2,1)S(1)} %pad_maximum_fusion.refs_0_.refs_4_), channel_id=1, source_target_pairs={{0,2},{2,4},{4,6},{6,0},{1,3},{3,5},{5,7},{7,1},{8,10},{10,12},{12... | collective-permute-start | bytes 147464 | tf_op jit(solution)/shard_map/ppermute | solution.py:287
  3.8 8.1 %collective-permute-start.1 = (bf16[192,128]{1,0:T(8,128)(2,1)S(1)}, bf16[192,128]{1,0:T(8,128)(2,1)S(1)}, u32[]{:S(2)}, u32[]{:S(2)}) collective-permute-start(bf16[192,128]{1,0:T(8,128)(2,1)S(1)} %pad_maximum_fusion.refs_0_.refs_4_), channel_id=1, source_target_pairs={{0,4},{2,6},{4,0},{6,2},{1,5},{3,7},{5,1},{7,3},{8,12},{10,14},{12... | collective-permute-start | bytes 147464 | tf_op jit(solution)/shard_map/ppermute | solution.py:287
  6.4 5.5 %collective-permute-start.2 = (bf16[192,128]{1,0:T(8,128)(2,1)S(1)}, bf16[192,128]{1,0:T(8,128)(2,1)S(1)}, u32[]{:S(2)}, u32[]{:S(2)}) collective-permute-start(bf16[192,128]{1,0:T(8,128)(2,1)S(1)} %pad_maximum_fusion.refs_0_.refs_4_), channel_id=1, source_target_pairs={{0,6},{2,0},{4,2},{6,4},{1,7},{3,1},{5,3},{7,5},{8,14},{10,8},{12,... | collective-permute-start | bytes 147464 | tf_op jit(solution)/shard_map/ppermute | solution.py:287
  7.8 4.1 %collective-permute-start.3 = (bf16[192,128]{1,0:T(8,128)(2,1)S(1)}, bf16[192,128]{1,0:T(8,128)(2,1)S(1)}, u32[]{:S(2)}, u32[]{:S(2)}) collective-permute-start(bf16[192,128]{1,0:T(8,128)(2,1)S(1)} %pad_maximum_fusion.refs_0_.refs_4_), channel_id=1, source_target_pairs={{0,1},{1,0},{2,3},{3,2},{4,5},{5,4},{6,7},{7,6},{8,9},{9,8},{10,11... | collective-permute-start | bytes 147464 | tf_op jit(solution)/shard_map/ppermute | solution.py:287
  13.8 3.7 %collective-permute-start.6 = (f32[2,32,256]{2,1,0:T(8,128)S(1)}, f32[2,32,256]{2,1,0:T(8,128)S(1)}, u32[]{:S(2)}, u32[]{:S(2)}) collective-permute-start(f32[2,32,256]{2,1,0:T(8,128)S(1)} %bitcast.8), channel_id=1, source_target_pairs={{0,1},{1,0},{2,3},{3,2},{4,5},{5,4},{6,7},{7,6},{8,9},{9,8},{10,11... | collective-permute-start | bytes 196616 | tf_op jit(solution)/shard_map/ppermute | solution.py:287
  14.4 3.9 %collective-permute-start.4 = (bf16[768,128]{1,0:T(8,128)(2,1)S(1)}, bf16[768,128]{1,0:T(8,128)(2,1)S(1)}, u32[]{:S(2)}, u32[]{:S(2)}) collective-permute-start(bf16[768,128]{1,0:T(8,128)(2,1)S(1)} %get-tuple-element.13.refs_0_), channel_id=1, source_target_pairs={{0,1},{1,0},{2,3},{3,2},{4,5},{5,4},{6,7},{7,6},{8,9},{9,8},{10,11... | collective-permute-start | bytes 589832 | tf_op jit(solution)/shard_map/ppermute | solution.py:287
  15.7 5.7 %collective-permute-start.5 = (f32[2,32,256]{2,1,0:T(8,128)S(1)}, f32[2,32,256]{2,1,0:T(8,128)S(1)}, u32[]{:S(2)}, u32[]{:S(2)}) collective-permute-start(f32[2,32,256]{2,1,0:T(8,128)S(1)} %bitcast.7), channel_id=1, source_target_pairs={{0,1},{1,0},{2,3},{3,2},{4,5},{5,4},{6,7},{7,6},{8,9},{9,8},{10,11... | collective-permute-start | bytes 196616 | tf_op jit(solution)/shard_map/ppermute | solution.py:287
  17.5 4.3 %collective-permute-start.7 = (f32[2,32,256]{2,1,0:T(8,128)S(1)}, f32[2,32,256]{2,1,0:T(8,128)S(1)}, u32[]{:S(2)}, u32[]{:S(2)}) collective-permute-start(f32[2,32,256]{2,1,0:T(8,128)S(1)} %bitcast_add_fusion), channel_id=1, source_target_pairs={{0,2},{2,0},{4,6},{6,4},{1,3},{3,1},{5,7},{7,5},{8,10},{10,8},{12,... | collective-permute-start | bytes 196616 | tf_op jit(solution)/shard_map/ppermute | solution.py:310
  21.9 4.9 %collective-permute-start.8 = (f32[1,32,256]{2,1,0:T(8,128)S(1)}, f32[1,32,256]{2,1,0:T(8,128)S(1)}, u32[]{:S(2)}, u32[]{:S(2)}) collective-permute-start(f32[1,32,256]{2,1,0:T(8,128)S(1)} %get-tuple-element.17), channel_id=1, source_target_pairs={{0,4},{2,6},{4,0},{6,2},{1,5},{3,7},{5,1},{7,3},{8,12},{10,14},{12... | collective-permute-start | bytes 98312 | tf_op jit(solution)/shard_map/ppermute | solution.py:331

commit v7 on v6

--- a/solution.py
+++ b/solution.py
@@ -9,7 +9,6 @@
 
 
 ridge_weight = 0.1
-exact = lax.Precision.HIGHEST
 vmem = pl.BlockSpec(memory_space=pltpu.VMEM)
 smem = pl.BlockSpec(memory_space=pltpu.SMEM)
 hbm = pl.BlockSpec(memory_space=pltpu.HBM)
@@ -64,14 +63,30 @@
     )(where, tensor)
 
 
-def contract(held, out, c_wide, b_wide):
+def contraction(held, out, c_wide, b_wide):
     count, owned = held.shape[0], held.shape[1]
-    for u in range(count):
+    few = min(owned, 8)
+
+    def piece(u, first):
         sums = []
-        for i in range(owned):
+        for i in range(first, first + few):
             inner = jnp.dot(held[u, i], c_wide, preferred_element_type=jnp.float32)
             sums.append(jnp.sum(inner * b_wide, axis=0, keepdims=True))
-        out[u] = jnp.concatenate(sums, axis=0)
+        out[u, first : first + few, :] = jnp.concatenate(sums, axis=0)
+
+    return [
+        functools.partial(piece, u, first) for u in range(count) for first in range(0, owned, few)
+    ]
+
+
+def contract(held, out, c_wide, b_wide):
+    for piece in contraction(held, out, c_wide, b_wide):
+        piece()
+
+
+def share(pieces, turn, turns):
+    for piece in pieces[len(pieces) * turn // turns : len(pieces) * (turn + 1) // turns]:
+        piece()
 
 
 def away_kernel(nj, nk, height_b, flipped, where, held, *refs):
@@ -156,11 +171,14 @@
     return high, middle, (x - middle.astype(jnp.float32)).astype(jnp.bfloat16)
 
 
+pairs = ((0, 0), (0, 1), (1, 0), (0, 2), (1, 1), (2, 0))
+
+
 def stack(tiles):
     return jnp.concatenate([jnp.concatenate(r, axis=1) for r in tiles], axis=0)
 
 
-def invert(a, begin, end, step=16):
+def invert(a, begin, end, between=None, step=16):
     size = a.shape[0]
     wide, per = size // 128, step // 8
     lane = lax.broadcasted_iota(jnp.int32, (8, 128), 1)
@@ -177,6 +195,8 @@
         g0, w0, lane0 = first // 8, first // 128, first % 128
         inside = (lane >= lane0) & (lane < lane0 + step)
         more = first + step < size
+        if between is not None:
+            between((first - begin) // step)
         panel = [list(r) for r in now]
         c = columns(now, w0, lane0)
         if more:
@@ -211,7 +231,6 @@
         left = stack(now)
         left = thirds(jnp.where(lanes < first, -left, left))
         right = thirds(stack(done))
-        pairs = ((0, 0), (0, 1), (1, 0), (0, 2), (1, 1), (2, 0))
         update = lax.dot_general(
             jnp.concatenate([left[i] for i, _ in pairs], axis=0),
             jnp.concatenate([right[i] for _, i in pairs], axis=0),
@@ -245,8 +264,12 @@
 
 
 def first_kernel(nj, nk, height_b, flipped, blocks, where, held, c_cols, b_cols, *refs):
-    owns, (kept, out, b_all) = refs[:nk], refs[nk:]
+    owns, (away, out, b_all) = refs[:nk], refs[nk:]
     rank = out.shape[1]
+    pieces = []
+    for t in range(1, nk):
+        pieces += contraction(held.at[t, : nj // 2], away.at[t - 1], c_cols[...], b_cols[...])
+    turns = blocks // 16 + 1
 
     def gram(x, contracted):
         dims = (((contracted,), (contracted,)), ((), ()))
@@ -265,12 +288,20 @@
     else:
         gram_b = gram(b_all[...].reshape(nj * height_b, rank), 0)
     gram_c = sum(gram(own[:rank, :], 1) for own in owns)
+    share(pieces, 0, turns)
     diagonal = lax.broadcasted_iota(jnp.int32, out.shape, 0) == lax.broadcasted_iota(
         jnp.int32, out.shape, 1
     )
     out[...] = gram_b * gram_c + jnp.where(diagonal, ridge_weight, 0.0)
-    contract(held.at[0, : nj // 2], kept, c_cols[...], b_cols[...])
-    invert(out, 0, blocks)
+    invert(out, 0, blocks, lambda turn: share(pieces, turn + 1, turns))
+
+
+def middle_kernel(begin, end, held, c_cols, b_cols, started, kept, out):
+    out[...] = started[...]
+    half = kept.shape[0]
+    pieces = contraction(held.at[0, :half], kept, c_cols[...], b_cols[...])
+    turns = (end - begin) // 16
+    invert(out, begin, end, lambda turn: share(pieces, turn, turns))
 
 
 def rest_kernel(blocks, half_done, out):
@@ -279,8 +310,12 @@
 
 
 def solve_kernel(kept, received, inverse, out):
-    mine = kept[0] + received[0]
-    out[...] = jnp.dot(mine, inverse[...], precision=exact, preferred_element_type=jnp.float32)
+    left, right = thirds(kept[0] + received[0]), thirds(inverse[...])
+    out[...] = jnp.dot(
+        jnp.concatenate([left[i] for i, _ in pairs], axis=1),
+        jnp.concatenate([right[i] for _, i in pairs], axis=0),
+        preferred_element_type=jnp.float32,
+    )
 
 
 def send(x, axis, n, s):
@@ -308,21 +343,28 @@
     for t in turns:
         sent = sent + send(away[t - 1], "ka", nk, t)
     received = lax.ppermute(sent, "ja", [(i, i ^ 1) for i in range(nj)])
-    away = contract_rows(turns, 0, half, held, c_cols, b_cols)
     params = pltpu.CompilerParams(vmem_limit_bytes=20 * 2**20)
     cost = pl.CostEstimate(flops=5 * 10**9, bytes_accessed=2**20, transcendentals=0)
     square = jax.ShapeDtypeStruct((rank, rank), jnp.float32)
-    blocks = rank // 64 * 16
+    first, middle = rank // 128 * 16, rank // 256 * 80
     b_shape = (nj, rank, mine.shape[1]) if flipped else (nj, height_b, rank)
-    kept, half_done = pl.pallas_call(
-        functools.partial(first_kernel, nj, nk, height_b, flipped, blocks),
-        out_shape=[jax.ShapeDtypeStruct(sent.shape, jnp.float32), square],
+    away, started = pl.pallas_call(
+        functools.partial(first_kernel, nj, nk, height_b, flipped, first),
+        out_shape=[jax.ShapeDtypeStruct(away.shape, jnp.float32), square],
         in_specs=[smem] + [vmem] * (3 + nk),
         out_specs=[vmem] * 2,
         scratch_shapes=[pltpu.VMEM(b_shape, mine.dtype)],
         compiler_params=params,
         cost_estimate=cost,
     )(where, held, c_cols, b_cols, *owns)
+    kept, half_done = pl.pallas_call(
+        functools.partial(middle_kernel, first, middle),
+        out_shape=[jax.ShapeDtypeStruct(sent.shape, jnp.float32), square],
+        in_specs=[vmem] * 4,
+        out_specs=[vmem] * 2,
+        compiler_params=params,
+        cost_estimate=cost,
+    )(held, c_cols, b_cols, started)
     for t in turns:
         kept = kept + send(away[t - 1], "ka", nk, t)
     bit = 2
@@ -331,7 +373,7 @@
         received = lax.ppermute(sent, "ja", [(i, i ^ bit) for i in range(nj)])
         bit *= 2
     inverse = pl.pallas_call(
-        functools.partial(rest_kernel, blocks),
+        functools.partial(rest_kernel, middle),
         out_shape=square,
         in_specs=[vmem],
         out_specs=vmem,

time: 27.8 us -> 28.1 us (1.011)
  waiting for transfers between devices: 0.63 us -> 1.86 us
  Pallas kernels: 16.2 us -> 15.5 us
  starting transfers between devices: 9.79 us -> 9.39 us
    ppermute x7, starting transfers between devices: 8.14 us -> 6.75 us  [send(): return lax.ppermute(x, axis, shift(n, s))]
    pallas_call x1 -> x2, Pallas kernels: 3.73 us -> 5.11 us  [the longest x1 3.4 us: update(): pl.pallas_call(functools.partial(rest_kernel, middle), out_shape=square,...]
    pallas_call x2 -> x1, Pallas kernels: 2.5 us -> 1.25 us  [contract_rows(): pl.pallas_call(functools.partial(rows_kernel, turns, begin, count), out_s...]
    ppermute x1, starting transfers between devices: 0.74 us -> 1.66 us  [update(): received = lax.ppermute(sent, 'ja', [(i, i ^ 1) for i in range(nj)])]
    ppermute x7, waiting for transfers between devices: 0.02 us -> 0.92 us  [send(): return lax.ppermute(x, axis, shift(n, s))]
    pallas_call x1, Pallas kernels: 3.19 us -> 2.43 us  [update(): pl.pallas_call(functools.partial(first_kernel, nj, nk, height_b, flipped,...]
    ppermute x1, waiting for transfers between devices: 0.24 us -> 0.94 us  [update(): received = lax.ppermute(sent, 'ja', [(i, i ^ bit) for i in range(nj)])]
    ppermute x1, waiting for transfers between devices: 0.38 us -> 0.01 us  [update(): received = lax.ppermute(sent, 'ja', [(i, i ^ 1) for i in range(nj)])]
  transfers between devices with their start and end apart: 9 -> 9, of which waited for: 2 -> 2; matrix products, arithmetic and copies ran while one was open for 0% -> 0% of each run, Pallas kernels for 49% -> 46%
where the time goes in v7:
time: 28.1 us; the launch traced here: 27.8 us
  Pallas kernels  15.5 us (55%)
  starting transfers between devices  9.39 us (33%)
  waiting for transfers between devices  1.86 us (7%)
  other arithmetic  0.88 us (3%)
    ppermute x7, starting transfers between devices, send(): return lax.ppermute(x, axis, shift(n, s))  6.75 us
    pallas_call x1, Pallas kernels, fetch(): pl.pallas_call(functools.partial(fetch_kernel, nj, nk), out_shape=jax.Sha...  4.02 us
    pallas_call x1, Pallas kernels, update(): pl.pallas_call(functools.partial(rest_kernel, middle), out_shape=square,...  3.4 us
    pallas_call x1, Pallas kernels, update(): pl.pallas_call(functools.partial(first_kernel, nj, nk, height_b, flipped,...  2.43 us
    pallas_call x1, Pallas kernels, contract_away(): pl.pallas_call(functools.partial(away_kernel, nj, nk, height_b, flipped),...  1.87 us
    pallas_call x1, Pallas kernels, update(): pl.pallas_call(functools.partial(middle_kernel, first, middle), out_shape...  1.72 us
    ppermute x1, starting transfers between devices, update(): received = lax.ppermute(sent, 'ja', [(i, i ^ 1) for i in range(nj)])  1.66 us
    pallas_call x1, Pallas kernels, contract_rows(): pl.pallas_call(functools.partial(rows_kernel, turns, begin, count), out_s...  1.25 us
  transfers between devices with their start and end apart: 9, of which 2 were waited for; matrix products, arithmetic and copies ran while one was open for 0% of the time, Pallas kernels for 46%

profile of v7, /device:TPU:0, one launch (start us, length us, event | category | flops | bytes accessed | tf_op | source)
XLA Modules:
  0.0 27.8 jit_solution(11911233927231223359)
XLA Ops:
  0.0 0.8 %pad_maximum_fusion.refs_0_.refs_4_ = bf16[192,128]{1,0:T(8,128)(2,1)S(1)} fusion(bf16[64,128]{1,0:T(8,128)(2,1)} %bitcast.9, bf16[128,128]{1,0:T(8,128)(2,1)} %param.4), kind=kLoop, calls=%fused_computation.2 | loop fusion | flops 98304 | bytes 98304 | tf_op jit(solution)/shard_map/concatenate | solution.py:332
  0.8 0.5 %collective-permute-start.3 = (bf16[192,128]{1,0:T(8,128)(2,1)S(1)}, bf16[192,128]{1,0:T(8,128)(2,1)S(1)}, u32[]{:S(2)}, u32[]{:S(2)}) collective-permute-start(bf16[192,128]{1,0:T(8,128)(2,1)S(1)} %pad_maximum_fusion.refs_0_.refs_4_), channel_id=1, source_target_pairs={{0,1},{1,0},{2,3},{3,2},{4,5},{5,4},{6,7},{7,6},{8,9},{9,8},{10,11... | collective-permute-start | bytes 147464 | tf_op jit(solution)/shard_map/ppermute | solution.py:322
  1.3 4.6 %collective-permute-start.2 = (bf16[192,128]{1,0:T(8,128)(2,1)S(1)}, bf16[192,128]{1,0:T(8,128)(2,1)S(1)}, u32[]{:S(2)}, u32[]{:S(2)}) collective-permute-start(bf16[192,128]{1,0:T(8,128)(2,1)S(1)} %pad_maximum_fusion.refs_0_.refs_4_), channel_id=1, source_target_pairs={{0,6},{2,0},{4,2},{6,4},{1,7},{3,1},{5,3},{7,5},{8,14},{10,8},{12,... | collective-permute-start | bytes 147464 | tf_op jit(solution)/shard_map/ppermute | solution.py:322
  5.9 0.0 collective-permute-start.1
  5.9 1.0 %collective-permute-start = (bf16[192,128]{1,0:T(8,128)(2,1)S(1)}, bf16[192,128]{1,0:T(8,128)(2,1)S(1)}, u32[]{:S(2)}, u32[]{:S(2)}) collective-permute-start(bf16[192,128]{1,0:T(8,128)(2,1)S(1)} %pad_maximum_fusion.refs_0_.refs_4_), channel_id=1, source_target_pairs={{0,2},{2,4},{4,6},{6,0},{1,3},{3,5},{5,7},{7,1},{8,10},{10,12},{12... | collective-permute-start | bytes 147464 | tf_op jit(solution)/shard_map/ppermute | solution.py:322
  6.9 0.1 pad_add_fusion.where
  7.0 4.0 %shard_map.37.held = bf16[2,4,32,128,128]{4,3,2,1,0:T(8,128)(2,1)S(1)} custom-call(s32[2]{0:T(128)S(1)} %pad_add_fusion.where, bf16[256,128,128]{2,1,0:T(8,128)(2,1)} %block.1), custom_call_target="tpu_custom_call" | custom-call | flops 4000000000 | bytes 8388608 | tf_op jit(solution)/shard_map/pallas_call | solution.py:53
  11.0 0.0 collective-permute-done.2.refs_3_
  11.0 0.9 %collective-permute-done.1.refs_2_ = bf16[192,128]{1,0:T(8,128)(2,1)S(1)} collective-permute-done((bf16[192,128]{1,0:T(8,128)(2,1)S(1)}, bf16[192,128]{1,0:T(8,128)(2,1)S(1)}, u32[]{:S(2)}, u32[]{:S(2)}) %collective-permute-start.1) | collective-permute-done | bytes 49184 | tf_op jit(solution)/shard_map/ppermute | solution.py:322
  11.9 0.0 collective-permute-done.refs_1_
  11.9 1.9 %shard_map.38 = (f32[1,2,32,256]{3,2,1,0:T(8,128)S(1)}, bf16[768,128]{1,0:T(8,128)(2,1)S(1)}, bf16[128,256]{1,0:T(8,128)(2,1)S(1)}, f32[128,256]{1,0:T(8,128)S(1)}) custom-call(s32[2]{0:T(128)S(1)} %pad_add_fusion.where, bf16[2,4,32,128,128]{4,3,2,1,0:T(8,128)(2,1)S(1)} %shard_map.37.held, bf16[192,128]{1,0:T(8,128)(2,1)S(1)} %pad_maximum_fusion.refs_0_.refs_4_, ...), custom_call_target="tpu_custom_call" | custom-call | flops 536870912 | bytes 1048576 | tf_op jit(solution)/shard_map/pallas_call | solution.py:131
  13.8 0.1 collective-permute-start.6
  13.9 0.5 %collective-permute-start.4 = (bf16[768,128]{1,0:T(8,128)(2,1)S(1)}, bf16[768,128]{1,0:T(8,128)(2,1)S(1)}, u32[]{:S(2)}, u32[]{:S(2)}) collective-permute-start(bf16[768,128]{1,0:T(8,128)(2,1)S(1)} %get-tuple-element.15.refs_0_), channel_id=1, source_target_pairs={{0,1},{1,0},{2,3},{3,2},{4,5},{5,4},{6,7},{7,6},{8,9},{9,8},{10,11... | collective-permute-start | bytes 589832 | tf_op jit(solution)/shard_map/ppermute | solution.py:322
  14.4 1.3 %shard_map.41 = f32[1,2,32,256]{3,2,1,0:T(8,128)S(1)} custom-call(bf16[2,4,32,128,128]{4,3,2,1,0:T(8,128)(2,1)S(1)} %shard_map.37.held, bf16[128,256]{1,0:T(8,128)(2,1)S(1)} %get-tuple-element.13.c_cols, f32[128,256]{1,0:T(8,128)S(1)} %get-tuple-element.14.b_cols), custom_call_target="tpu_custom_call" | custom-call | flops 536870912 | bytes 1048576 | tf_op jit(solution)/shard_map/pallas_call | solution.py:149
  15.7 1.7 %collective-permute-start.7 = (f32[2,32,256]{2,1,0:T(8,128)S(1)}, f32[2,32,256]{2,1,0:T(8,128)S(1)}, u32[]{:S(2)}, u32[]{:S(2)}) collective-permute-start(f32[2,32,256]{2,1,0:T(8,128)S(1)} %bitcast_add_fusion), channel_id=1, source_target_pairs={{0,2},{2,0},{4,6},{6,4},{1,3},{3,1},{5,7},{7,5},{8,10},{10,8},{12,... | collective-permute-start | bytes 196616 | tf_op jit(solution)/shard_map/ppermute | solution.py:345
  17.3 0.0 collective-permute-done.4.refs_1_
  17.3 2.4 %shard_map.39 = (f32[1,2,32,256]{3,2,1,0:T(8,128)S(1)}, f32[256,256]{1,0:T(8,128)S(1)}) custom-call(s32[2]{0:T(128)S(1)} %pad_add_fusion.where, bf16[2,4,32,128,128]{4,3,2,1,0:T(8,128)(2,1)S(1)} %shard_map.37.held, bf16[128,256]{1,0:T(8,128)(2,1)S(1)} %get-tuple-element.13.c_cols, f32[128,256]{1,0:T(8,128)S(1)} %get-tuple-element.14.b_cols, ...), custom_call_target="tpu_custom_call" | custom-call | flops 5000000000 | bytes 1048576 | tf_op jit(solution)/shard_map/pallas_call | solution.py:351
  19.8 0.1 collective-permute-start.5
  19.9 1.7 %shard_map.40 = (f32[2,32,256]{2,1,0:T(8,128)S(1)}, f32[256,256]{1,0:T(8,128)S(1)}) custom-call(bf16[2,4,32,128,128]{4,3,2,1,0:T(8,128)(2,1)S(1)} %shard_map.37.held, bf16[128,256]{1,0:T(8,128)(2,1)S(1)} %get-tuple-element.13.c_cols, f32[128,256]{1,0:T(8,128)S(1)} %get-tuple-element.14.b_cols, f32[256,256]{1,0:T(8,128)S(1)} %get-tuple-element.16.started), custom_call_target="tpu_custom_call" | custom-call | flops 5000000000 | bytes 1048576 | tf_op jit(solution)/shard_map/pallas_call | solution.py:360
  21.6 0.0 collective-permute-done.7
  21.6 1.0 %collective-permute-start.8 = (f32[1,32,256]{2,1,0:T(8,128)S(1)}, f32[1,32,256]{2,1,0:T(8,128)S(1)}, u32[]{:S(2)}, u32[]{:S(2)}) collective-permute-start(f32[1,32,256]{2,1,0:T(8,128)S(1)} %get-tuple-element.21), channel_id=1, source_target_pairs={{0,4},{2,6},{4,0},{6,2},{1,5},{3,7},{5,1},{7,3},{8,12},{10,14},{12... | collective-permute-start | bytes 98312 | tf_op jit(solution)/shard_map/ppermute | solution.py:373
  22.6 3.4 %shard_map.42.inverse = f32[256,256]{1,0:T(8,128)S(1)} custom-call(f32[256,256]{1,0:T(8,128)S(1)} %get-tuple-element.20.half_done), custom_call_target="tpu_custom_call" | custom-call | flops 5000000000 | bytes 1048576 | tf_op jit(solution)/shard_map/pallas_call | solution.py:375
  26.0 0.9 %collective-permute-done.8.received = f32[1,32,256]{2,1,0:T(8,128)S(1)} collective-permute-done((f32[1,32,256]{2,1,0:T(8,128)S(1)}, f32[1,32,256]{2,1,0:T(8,128)S(1)}, u32[]{:S(2)}, u32[]{:S(2)}) %collective-permute-start.8) | collective-permute-done | bytes 32800 | tf_op jit(solution)/shard_map/ppermute | solution.py:373
  27.0 0.9 %shard_map.43 = f32[32,256]{1,0:T(8,128)} custom-call(f32[1,32,256]{2,1,0:T(8,128)S(1)} %get-tuple-element.22.kept, f32[1,32,256]{2,1,0:T(8,128)S(1)} %collective-permute-done.8.received, f32[256,256]{1,0:T(8,128)S(1)} %shard_map.42.inverse), custom_call_target="tpu_custom_call" | custom-call | flops 100000000 | bytes 524288 | tf_op jit(solution)/shard_map/pallas_call | solution.py:383
  (6 shorter events, 0.0 us)
Async XLA Ops:
  0.8 10.2 %collective-permute-start.3 = (bf16[192,128]{1,0:T(8,128)(2,1)S(1)}, bf16[192,128]{1,0:T(8,128)(2,1)S(1)}, u32[]{:S(2)}, u32[]{:S(2)}) collective-permute-start(bf16[192,128]{1,0:T(8,128)(2,1)S(1)} %pad_maximum_fusion.refs_0_.refs_4_), channel_id=1, source_target_pairs={{0,1},{1,0},{2,3},{3,2},{4,5},{5,4},{6,7},{7,6},{8,9},{9,8},{10,11... | collective-permute-start | bytes 147464 | tf_op jit(solution)/shard_map/ppermute | solution.py:322
  1.3 9.7 %collective-permute-start.2 = (bf16[192,128]{1,0:T(8,128)(2,1)S(1)}, bf16[192,128]{1,0:T(8,128)(2,1)S(1)}, u32[]{:S(2)}, u32[]{:S(2)}) collective-permute-start(bf16[192,128]{1,0:T(8,128)(2,1)S(1)} %pad_maximum_fusion.refs_0_.refs_4_), channel_id=1, source_target_pairs={{0,6},{2,0},{4,2},{6,4},{1,7},{3,1},{5,3},{7,5},{8,14},{10,8},{12,... | collective-permute-start | bytes 147464 | tf_op jit(solution)/shard_map/ppermute | solution.py:322
  5.9 6.0 %collective-permute-start.1 = (bf16[192,128]{1,0:T(8,128)(2,1)S(1)}, bf16[192,128]{1,0:T(8,128)(2,1)S(1)}, u32[]{:S(2)}, u32[]{:S(2)}) collective-permute-start(bf16[192,128]{1,0:T(8,128)(2,1)S(1)} %pad_maximum_fusion.refs_0_.refs_4_), channel_id=1, source_target_pairs={{0,4},{2,6},{4,0},{6,2},{1,5},{3,7},{5,1},{7,3},{8,12},{10,14},{12... | collective-permute-start | bytes 147464 | tf_op jit(solution)/shard_map/ppermute | solution.py:322
  5.9 6.0 %collective-permute-start = (bf16[192,128]{1,0:T(8,128)(2,1)S(1)}, bf16[192,128]{1,0:T(8,128)(2,1)S(1)}, u32[]{:S(2)}, u32[]{:S(2)}) collective-permute-start(bf16[192,128]{1,0:T(8,128)(2,1)S(1)} %pad_maximum_fusion.refs_0_.refs_4_), channel_id=1, source_target_pairs={{0,2},{2,4},{4,6},{6,0},{1,3},{3,5},{5,7},{7,1},{8,10},{10,12},{12... | collective-permute-start | bytes 147464 | tf_op jit(solution)/shard_map/ppermute | solution.py:322
  13.8 1.8 %collective-permute-start.6 = (f32[2,32,256]{2,1,0:T(8,128)S(1)}, f32[2,32,256]{2,1,0:T(8,128)S(1)}, u32[]{:S(2)}, u32[]{:S(2)}) collective-permute-start(f32[2,32,256]{2,1,0:T(8,128)S(1)} %bitcast.8), channel_id=1, source_target_pairs={{0,1},{1,0},{2,3},{3,2},{4,5},{5,4},{6,7},{7,6},{8,9},{9,8},{10,11... | collective-permute-start | bytes 196616 | tf_op jit(solution)/shard_map/ppermute | solution.py:322
  13.9 3.5 %collective-permute-start.4 = (bf16[768,128]{1,0:T(8,128)(2,1)S(1)}, bf16[768,128]{1,0:T(8,128)(2,1)S(1)}, u32[]{:S(2)}, u32[]{:S(2)}) collective-permute-start(bf16[768,128]{1,0:T(8,128)(2,1)S(1)} %get-tuple-element.15.refs_0_), channel_id=1, source_target_pairs={{0,1},{1,0},{2,3},{3,2},{4,5},{5,4},{6,7},{7,6},{8,9},{9,8},{10,11... | collective-permute-start | bytes 589832 | tf_op jit(solution)/shard_map/ppermute | solution.py:322
  15.7 5.9 %collective-permute-start.7 = (f32[2,32,256]{2,1,0:T(8,128)S(1)}, f32[2,32,256]{2,1,0:T(8,128)S(1)}, u32[]{:S(2)}, u32[]{:S(2)}) collective-permute-start(f32[2,32,256]{2,1,0:T(8,128)S(1)} %bitcast_add_fusion), channel_id=1, source_target_pairs={{0,2},{2,0},{4,6},{6,4},{1,3},{3,1},{5,7},{7,5},{8,10},{10,8},{12,... | collective-permute-start | bytes 196616 | tf_op jit(solution)/shard_map/ppermute | solution.py:345
  19.8 1.8 %collective-permute-start.5 = (f32[2,32,256]{2,1,0:T(8,128)S(1)}, f32[2,32,256]{2,1,0:T(8,128)S(1)}, u32[]{:S(2)}, u32[]{:S(2)}) collective-permute-start(f32[2,32,256]{2,1,0:T(8,128)S(1)} %bitcast.7), channel_id=1, source_target_pairs={{0,1},{1,0},{2,3},{3,2},{4,5},{5,4},{6,7},{7,6},{8,9},{9,8},{10,11... | collective-permute-start | bytes 196616 | tf_op jit(solution)/shard_map/ppermute | solution.py:322
  21.6 5.3 %collective-permute-start.8 = (f32[1,32,256]{2,1,0:T(8,128)S(1)}, f32[1,32,256]{2,1,0:T(8,128)S(1)}, u32[]{:S(2)}, u32[]{:S(2)}) collective-permute-start(f32[1,32,256]{2,1,0:T(8,128)S(1)} %get-tuple-element.21), channel_id=1, source_target_pairs={{0,4},{2,6},{4,0},{6,2},{1,5},{3,7},{5,1},{7,3},{8,12},{10,14},{12... | collective-permute-start | bytes 98312 | tf_op jit(solution)/shard_map/ppermute | solution.py:373

commit v8 on v7

--- a/solution.py
+++ b/solution.py
@@ -33,14 +33,19 @@
     return order
 
 
-def fetch_kernel(nj, nk, where, block, held, arrived):
-    owned = held.shape[2]
+def owner_rows(nj, nk, where, block, t, slot, owned):
+    to = owner(nk, where, t, halving_order(nj)[slot])
+    return block.at[pl.ds(pl.multiple_of(to * owned, owned), owned)]
+
+
+def fetch_kernel(nj, nk, where, block, away_held, sent_held, arrived):
+    owned, half = sent_held.shape[1], nj // 2
+    targets = [(t, slot, away_held.at[t - 1, slot]) for t in range(1, nk) for slot in range(nj)]
+    targets += [(0, slot, sent_held.at[slot - half]) for slot in range(half, nj)]
     copies = []
-    for t in range(nk):
-        for slot, u in enumerate(halving_order(nj)):
-            first = pl.multiple_of(owner(nk, where, t, u) * owned, owned)
-            rows = block.at[pl.ds(first, owned)]
-            copies.append(pltpu.make_async_copy(rows, held.at[t, slot], arrived.at[t, slot]))
+    for i, (t, slot, target) in enumerate(targets):
+        rows = owner_rows(nj, nk, where, block, t, slot, owned)
+        copies.append(pltpu.make_async_copy(rows, target, arrived.at[i]))
     for copy in copies:
         copy.start()
     for copy in copies:
@@ -52,11 +57,14 @@
     owned = rows // (nj * nk)
     return pl.pallas_call(
         functools.partial(fetch_kernel, nj, nk),
-        out_shape=jax.ShapeDtypeStruct((nk, nj, owned, width_j, width_k), tensor.dtype),
+        out_shape=[
+            jax.ShapeDtypeStruct((nk - 1, nj, owned, width_j, width_k), tensor.dtype),
+            jax.ShapeDtypeStruct((nj // 2, owned, width_j, width_k), tensor.dtype),
+        ],
         in_specs=[smem, hbm],
-        out_specs=vmem,
-        scratch_shapes=[pltpu.SemaphoreType.DMA((nk, nj))],
-        compiler_params=pltpu.CompilerParams(vmem_limit_bytes=42 * 2**20),
+        out_specs=[vmem] * 2,
+        scratch_shapes=[pltpu.SemaphoreType.DMA(((nk - 1) * nj + nj // 2,))],
+        compiler_params=pltpu.CompilerParams(vmem_limit_bytes=44 * 2**20),
         cost_estimate=pl.CostEstimate(
             flops=4 * 10**9, bytes_accessed=2 * rows * width_j * width_k, transcendentals=0
         ),
@@ -89,11 +97,29 @@
         piece()
 
 
-def away_kernel(nj, nk, height_b, flipped, where, held, *refs):
+def away_kernel(nj, nk, height_b, flipped, where, block, held, *refs):
     line, refs = refs[:nj], refs[nj:]
     b_parts, refs = refs[:nk], refs[nk:]
-    out, own, c_cols, b_cols, b_rows = refs
-    rank = c_cols.shape[1]
+    out, own, c_cols, b_cols, kept_held, b_rows, arrived = refs
+    rank, owned = c_cols.shape[1], kept_held.shape[1]
+    order = halving_order(nj)
+
+    def load(slot):
+        to = wrap(where[1], nk)
+        u = sum(jnp.where(slot == i, order[i], 0) for i in range(nj // 2))
+        to = lax.bitwise_xor(where[0], u) * nk + to
+        rows = block.at[pl.ds(pl.multiple_of(to * owned, owned), owned)]
+        return pltpu.make_async_copy(rows, kept_held.at[slot], arrived.at[slot])
+
+    def begin(slot, _):
+        load(slot).start()
+        return 0
+
+    def finish(slot, _):
+        load(slot).wait()
+        return 0
+
+    lax.fori_loop(0, nj // 2, begin, 0)
     width_c = line[0].shape[0] - height_b
     for s in range(nj):
         at = pl.multiple_of(wrap(where[0] - s, nj) * width_c, width_c)
@@ -109,12 +135,12 @@
     c_cols[...] = own[:rank, :].T
     b_cols[...] = (b_rows[...].T if flipped else b_rows[...]).astype(jnp.float32)
     for t in range(1, nk):
-        contract(held.at[t, nj // 2 :], out.at[t - 1], c_cols[...], b_cols[...])
-
-
-def rows_kernel(turns, begin, count, held, c_cols, b_cols, out):
-    for slot, t in enumerate(turns):
-        contract(held.at[t, begin : begin + count], out.at[slot], c_cols[...], b_cols[...])
+        contract(held.at[t - 1, nj // 2 :], out.at[t - 1], c_cols[...], b_cols[...])
+    lax.fori_loop(0, nj // 2, finish, 0)
+
+
+def rows_kernel(held, c_cols, b_cols, out):
+    contract(held, out, c_cols[...], b_cols[...])
 
 
 def flops_of(rows, held, rank):
@@ -125,8 +151,9 @@
     )
 
 
-def contract_away(where, held, line, b_parts, height_b, flipped, rank):
-    nk, nj, owned, width_j, width_k = held.shape
+def contract_away(where, tensor, held, line, b_parts, height_b, flipped, rank):
+    _, nj, owned, width_j, width_k = held.shape
+    nk = len(b_parts)
     width = line[0].shape[1]
     return pl.pallas_call(
         functools.partial(away_kernel, nj, nk, height_b, flipped),
@@ -135,24 +162,29 @@
             jax.ShapeDtypeStruct((rank + nj * height_b, width), held.dtype),
             jax.ShapeDtypeStruct((width_k, rank), held.dtype),
             jax.ShapeDtypeStruct((width_j, rank), jnp.float32),
+            jax.ShapeDtypeStruct((nj // 2, owned, width_j, width_k), held.dtype),
         ],
-        in_specs=[smem] + [vmem] * (1 + nj + nk),
-        out_specs=[vmem] * 4,
-        scratch_shapes=[pltpu.VMEM((rank, width_j) if flipped else (width_j, rank), held.dtype)],
-        compiler_params=pltpu.CompilerParams(vmem_limit_bytes=20 * 2**20),
+        in_specs=[smem, hbm] + [vmem] * (1 + nj + nk),
+        out_specs=[vmem] * 5,
+        scratch_shapes=[
+            pltpu.VMEM((rank, width_j) if flipped else (width_j, rank), held.dtype),
+            pltpu.SemaphoreType.DMA((nj // 2,)),
+        ],
+        compiler_params=pltpu.CompilerParams(vmem_limit_bytes=44 * 2**20),
         cost_estimate=flops_of((nk - 1) * nj * owned // 2, held, rank),
-    )(where, held, *line, *b_parts)
-
-
-def contract_rows(turns, begin, count, held, c_cols, b_cols):
-    owned, rank = held.shape[2], c_cols.shape[1]
+    )(where, tensor, held, *line, *b_parts)
+
+
+def contract_rows(held, c_cols, b_cols):
+    count, owned = held.shape[:2]
+    rank = c_cols.shape[1]
     return pl.pallas_call(
-        functools.partial(rows_kernel, turns, begin, count),
-        out_shape=jax.ShapeDtypeStruct((len(turns), count, owned, rank), jnp.float32),
+        rows_kernel,
+        out_shape=jax.ShapeDtypeStruct((count, owned, rank), jnp.float32),
         in_specs=[vmem] * 3,
         out_specs=vmem,
         compiler_params=pltpu.CompilerParams(vmem_limit_bytes=20 * 2**20),
-        cost_estimate=flops_of(len(turns) * count * owned, held, rank),
+        cost_estimate=flops_of(count * owned, held, rank),
     )(held, c_cols, b_cols)
 
 
@@ -268,7 +300,7 @@
     rank = out.shape[1]
     pieces = []
     for t in range(1, nk):
-        pieces += contraction(held.at[t, : nj // 2], away.at[t - 1], c_cols[...], b_cols[...])
+        pieces += contraction(held.at[t - 1, : nj // 2], away.at[t - 1], c_cols[...], b_cols[...])
     turns = blocks // 16 + 1
 
     def gram(x, contracted):
@@ -298,8 +330,7 @@
 
 def middle_kernel(begin, end, held, c_cols, b_cols, started, kept, out):
     out[...] = started[...]
-    half = kept.shape[0]
-    pieces = contraction(held.at[0, :half], kept, c_cols[...], b_cols[...])
+    pieces = contraction(held, kept, c_cols[...], b_cols[...])
     turns = (end - begin) // 16
     invert(out, begin, end, lambda turn: share(pieces, turn, turns))
 
@@ -332,14 +363,13 @@
     mine = jnp.concatenate([part_b, factor_c.T], axis=0)
     line = [mine] + [send(mine, "ja", nj, s) for s in range(1, nj)]
     b_parts = [mine] + [send(mine, "ka", nk, t) for t in range(1, nk)]
-    held = fetch(where, tensor, nj, nk)
-    away, own, c_cols, b_cols = contract_away(
-        where, held, line, b_parts, height_b, flipped, rank
+    away_held, sent_held = fetch(where, tensor, nj, nk)
+    away, own, c_cols, b_cols, kept_held = contract_away(
+        where, tensor, away_held, line, b_parts, height_b, flipped, rank
     )
-    half = nj // 2
     turns = tuple(range(1, nk))
     owns = [own] + [send(own, "ka", nk, t) for t in turns]
-    sent = contract_rows((0,), half, half, held, c_cols, b_cols)[0]
+    sent = contract_rows(sent_held, c_cols, b_cols)
     for t in turns:
         sent = sent + send(away[t - 1], "ka", nk, t)
     received = lax.ppermute(sent, "ja", [(i, i ^ 1) for i in range(nj)])
@@ -356,7 +386,7 @@
         scratch_shapes=[pltpu.VMEM(b_shape, mine.dtype)],
         compiler_params=params,
         cost_estimate=cost,
-    )(where, held, c_cols, b_cols, *owns)
+    )(where, away_held, c_cols, b_cols, *owns)
     kept, half_done = pl.pallas_call(
         functools.partial(middle_kernel, first, middle),
         out_shape=[jax.ShapeDtypeStruct(sent.shape, jnp.float32), square],
@@ -364,7 +394,7 @@
         out_specs=[vmem] * 2,
         compiler_params=params,
         cost_estimate=cost,
-    )(held, c_cols, b_cols, started)
+    )(kept_held, c_cols, b_cols, started)
     for t in turns:
         kept = kept + send(away[t - 1], "ka", nk, t)
     bit = 2

time: 28.1 us -> 28 us (level)
  Pallas kernels: 15.5 us -> 15.2 us
  waiting for transfers between devices: 1.86 us -> 2.16 us
    pallas_call x2, Pallas kernels: 5.28 us -> 4.65 us  [the longest x1 3.4 us: fetch(): pl.pallas_call(functools.partial(fetch_kernel, nj, nk), out_shape=[jax.Sh...]
    ppermute x7, waiting for transfers between devices: 0.92 us -> 1.54 us  [send(): return lax.ppermute(x, axis, shift(n, s))]
    ppermute x1, starting transfers between devices: 1.66 us -> 1.04 us  [update(): received = lax.ppermute(sent, 'ja', [(i, i ^ 1) for i in range(nj)])]
    ppermute x1, starting transfers between devices: 0.98 us -> 1.56 us  [update(): received = lax.ppermute(sent, 'ja', [(i, i ^ bit) for i in range(nj)])]
    ppermute x1, waiting for transfers between devices: 0.94 us -> 0.62 us  [update(): received = lax.ppermute(sent, 'ja', [(i, i ^ bit) for i in range(nj)])]
  transfers between devices with their start and end apart: 9 -> 9, of which waited for: 2 -> 2; matrix products, arithmetic and copies ran while one was open for 0% -> 0% of each run, Pallas kernels for 46% -> 44%
where the time goes in v8:
time: 28 us; the launch traced here: 27.8 us
  Pallas kernels  15.2 us (54%)
  starting transfers between devices  9.35 us (33%)
  waiting for transfers between devices  2.16 us (8%)
  other arithmetic  0.88 us (3%)
    ppermute x7, starting transfers between devices, send(): return lax.ppermute(x, axis, shift(n, s))  6.75 us
    pallas_call x1, Pallas kernels, fetch(): pl.pallas_call(functools.partial(fetch_kernel, nj, nk), out_shape=[jax.Sh...  3.4 us
    pallas_call x1, Pallas kernels, update(): pl.pallas_call(functools.partial(rest_kernel, middle), out_shape=square,...  3.4 us
    pallas_call x1, Pallas kernels, update(): pl.pallas_call(functools.partial(first_kernel, nj, nk, height_b, flipped,...  2.46 us
    pallas_call x1, Pallas kernels, contract_away(): pl.pallas_call(functools.partial(away_kernel, nj, nk, height_b, flipped),...  2.11 us
    pallas_call x1, Pallas kernels, update(): pl.pallas_call(functools.partial(middle_kernel, first, middle), out_shape...  1.76 us
    ppermute x1, starting transfers between devices, update(): received = lax.ppermute(sent, 'ja', [(i, i ^ bit) for i in range(nj)])  1.56 us
    ppermute x7, waiting for transfers between devices, send(): return lax.ppermute(x, axis, shift(n, s))  1.54 us
  transfers between devices with their start and end apart: 9, of which 2 were waited for; matrix products, arithmetic and copies ran while one was open for 0% of the time, Pallas kernels for 44%

profile of v8, /device:TPU:0, one launch (start us, length us, event | category | flops | bytes accessed | tf_op | source)
XLA Modules:
  0.0 27.8 jit_solution(15691841553749202086)
XLA Ops:
  0.0 0.8 %pad_maximum_fusion.refs_0_.refs_4_ = bf16[192,128]{1,0:T(8,128)(2,1)S(1)} fusion(bf16[64,128]{1,0:T(8,128)(2,1)} %bitcast.7, bf16[128,128]{1,0:T(8,128)(2,1)} %param.4), kind=kLoop, calls=%fused_computation.1 | loop fusion | flops 98304 | bytes 98304 | tf_op jit(solution)/shard_map/concatenate | solution.py:363
  0.8 0.5 %collective-permute-start.3 = (bf16[192,128]{1,0:T(8,128)(2,1)S(1)}, bf16[192,128]{1,0:T(8,128)(2,1)S(1)}, u32[]{:S(2)}, u32[]{:S(2)}) collective-permute-start(bf16[192,128]{1,0:T(8,128)(2,1)S(1)} %pad_maximum_fusion.refs_0_.refs_4_), channel_id=1, source_target_pairs={{0,1},{1,0},{2,3},{3,2},{4,5},{5,4},{6,7},{7,6},{8,9},{9,8},{10,11... | collective-permute-start | bytes 147464 | tf_op jit(solution)/shard_map/ppermute | solution.py:353
  1.3 4.6 %collective-permute-start.2 = (bf16[192,128]{1,0:T(8,128)(2,1)S(1)}, bf16[192,128]{1,0:T(8,128)(2,1)S(1)}, u32[]{:S(2)}, u32[]{:S(2)}) collective-permute-start(bf16[192,128]{1,0:T(8,128)(2,1)S(1)} %pad_maximum_fusion.refs_0_.refs_4_), channel_id=1, source_target_pairs={{0,6},{2,0},{4,2},{6,4},{1,7},{3,1},{5,3},{7,5},{8,14},{10,8},{12,... | collective-permute-start | bytes 147464 | tf_op jit(solution)/shard_map/ppermute | solution.py:353
  5.9 1.0 %collective-permute-start = (bf16[192,128]{1,0:T(8,128)(2,1)S(1)}, bf16[192,128]{1,0:T(8,128)(2,1)S(1)}, u32[]{:S(2)}, u32[]{:S(2)}) collective-permute-start(bf16[192,128]{1,0:T(8,128)(2,1)S(1)} %pad_maximum_fusion.refs_0_.refs_4_), channel_id=1, source_target_pairs={{0,2},{2,4},{4,6},{6,0},{1,3},{3,5},{5,7},{7,1},{8,10},{10,12},{12... | collective-permute-start | bytes 147464 | tf_op jit(solution)/shard_map/ppermute | solution.py:353
  6.9 0.1 pad_add_fusion.where
  7.0 3.4 %shard_map.37 = (bf16[1,4,32,128,128]{4,3,2,1,0:T(8,128)(2,1)S(1)}, bf16[2,32,128,128]{3,2,1,0:T(8,128)(2,1)S(1)}) custom-call(s32[2]{0:T(128)S(1)} %pad_add_fusion.where, bf16[256,128,128]{2,1,0:T(8,128)(2,1)} %block.3), custom_call_target="tpu_custom_call" | custom-call | flops 4000000000 | bytes 8388608 | tf_op jit(solution)/shard_map/pallas_call | solution.py:58
  10.4 0.0 collective-permute-done.2.refs_3_
  10.4 1.5 %collective-permute-done.1.refs_2_ = bf16[192,128]{1,0:T(8,128)(2,1)S(1)} collective-permute-done((bf16[192,128]{1,0:T(8,128)(2,1)S(1)}, bf16[192,128]{1,0:T(8,128)(2,1)S(1)}, u32[]{:S(2)}, u32[]{:S(2)}) %collective-permute-start.1) | collective-permute-done | bytes 49184 | tf_op jit(solution)/shard_map/ppermute | solution.py:353
  11.9 0.0 collective-permute-done.refs_1_
  11.9 2.1 %shard_map.38 = (f32[1,2,32,256]{3,2,1,0:T(8,128)S(1)}, bf16[768,128]{1,0:T(8,128)(2,1)S(1)}, bf16[128,256]{1,0:T(8,128)(2,1)S(1)}, f32[128,256]{1,0:T(8,128)S(1)}, bf16[2,32,128,128]{3,2,1,0:T(8,128)(2,1)S(1)}) custom-call(s32[2]{0:T(128)S(1)} %pad_add_fusion.where, bf16[256,128,128]{2,1,0:T(8,128)(2,1)} %block.3, ...), custom_call_target="tpu_custom_call" | custom-call | flops 536870912 | bytes 1048576 | tf_op jit(solution)/shard_map/pallas_call | solution.py:158
  14.0 0.1 collective-permute-start.4
  14.1 0.5 %collective-permute-start.6 = (f32[2,32,256]{2,1,0:T(8,128)S(1)}, f32[2,32,256]{2,1,0:T(8,128)S(1)}, u32[]{:S(2)}, u32[]{:S(2)}) collective-permute-start(f32[2,32,256]{2,1,0:T(8,128)S(1)} %bitcast.5), channel_id=1, source_target_pairs={{0,1},{1,0},{2,3},{3,2},{4,5},{5,4},{6,7},{7,6},{8,9},{9,8},{10,11... | collective-permute-start | bytes 196616 | tf_op jit(solution)/shard_map/ppermute | solution.py:353
  14.6 1.2 %shard_map.41 = f32[2,32,256]{2,1,0:T(8,128)S(1)} custom-call(bf16[2,32,128,128]{3,2,1,0:T(8,128)(2,1)S(1)} %get-tuple-element.24.held, bf16[128,256]{1,0:T(8,128)(2,1)S(1)} %get-tuple-element.18.c_cols, f32[128,256]{1,0:T(8,128)S(1)} %get-tuple-element.19.b_cols), custom_call_target="tpu_custom_call" | custom-call | flops 536870912 | bytes 1048576 | tf_op jit(solution)/shard_map/pallas_call | solution.py:181
  15.9 0.0 collective-permute-done.6
  15.9 1.0 %collective-permute-start.7 = (f32[2,32,256]{2,1,0:T(8,128)S(1)}, f32[2,32,256]{2,1,0:T(8,128)S(1)}, u32[]{:S(2)}, u32[]{:S(2)}) collective-permute-start(f32[2,32,256]{2,1,0:T(8,128)S(1)} %add.10), channel_id=1, source_target_pairs={{0,2},{2,0},{4,6},{6,4},{1,3},{3,1},{5,7},{7,5},{8,10},{10,8},{12,... | collective-permute-start | bytes 196616 | tf_op jit(solution)/shard_map/ppermute | solution.py:375
  16.9 0.0 collective-permute-done.4.refs_1_
  16.9 2.5 %shard_map.39 = (f32[1,2,32,256]{3,2,1,0:T(8,128)S(1)}, f32[256,256]{1,0:T(8,128)S(1)}) custom-call(s32[2]{0:T(128)S(1)} %pad_add_fusion.where, bf16[1,4,32,128,128]{4,3,2,1,0:T(8,128)(2,1)S(1)} %get-tuple-element.16.held, bf16[128,256]{1,0:T(8,128)(2,1)S(1)} %get-tuple-element.18.c_cols, f32[128,256]{1,0:T(8,128)S(1)} %get-tuple-element.19.b_cols, ...), custom_call_target="tpu_custom_call" | custom-call | flops 5000000000 | bytes 1048576 | tf_op jit(solution)/shard_map/pallas_call | solution.py:381
  19.4 0.1 collective-permute-start.5
  19.5 1.8 %shard_map.40 = (f32[2,32,256]{2,1,0:T(8,128)S(1)}, f32[256,256]{1,0:T(8,128)S(1)}) custom-call(bf16[2,32,128,128]{3,2,1,0:T(8,128)(2,1)S(1)} %get-tuple-element.17.held, bf16[128,256]{1,0:T(8,128)(2,1)S(1)} %get-tuple-element.18.c_cols, f32[128,256]{1,0:T(8,128)S(1)} %get-tuple-element.19.b_cols, f32[256,256]{1,0:T(8,128)S(1)} %get-tuple-element.21.started), custom_call_target="tpu_custom_call" | custom-call | flops 5000000000 | bytes 1048576 | tf_op jit(solution)/shard_map/pallas_call | solution.py:390
  21.3 0.0 collective-permute-done.7
  21.3 1.6 %collective-permute-start.8 = (f32[1,32,256]{2,1,0:T(8,128)S(1)}, f32[1,32,256]{2,1,0:T(8,128)S(1)}, u32[]{:S(2)}, u32[]{:S(2)}) collective-permute-start(f32[1,32,256]{2,1,0:T(8,128)S(1)} %get-tuple-element.27), channel_id=1, source_target_pairs={{0,4},{2,6},{4,0},{6,2},{1,5},{3,7},{5,1},{7,3},{8,12},{10,14},{12... | collective-permute-start | bytes 98312 | tf_op jit(solution)/shard_map/ppermute | solution.py:403
  22.9 3.4 %shard_map.42.inverse = f32[256,256]{1,0:T(8,128)S(1)} custom-call(f32[256,256]{1,0:T(8,128)S(1)} %get-tuple-element.26.half_done), custom_call_target="tpu_custom_call" | custom-call | flops 5000000000 | bytes 1048576 | tf_op jit(solution)/shard_map/pallas_call | solution.py:405
  26.3 0.6 %collective-permute-done.8.received = f32[1,32,256]{2,1,0:T(8,128)S(1)} collective-permute-done((f32[1,32,256]{2,1,0:T(8,128)S(1)}, f32[1,32,256]{2,1,0:T(8,128)S(1)}, u32[]{:S(2)}, u32[]{:S(2)}) %collective-permute-start.8) | collective-permute-done | bytes 32800 | tf_op jit(solution)/shard_map/ppermute | solution.py:403
  26.9 0.9 %shard_map.43 = f32[32,256]{1,0:T(8,128)} custom-call(f32[1,32,256]{2,1,0:T(8,128)S(1)} %get-tuple-element.28.kept, f32[1,32,256]{2,1,0:T(8,128)S(1)} %collective-permute-done.8.received, f32[256,256]{1,0:T(8,128)S(1)} %shard_map.42.inverse), custom_call_target="tpu_custom_call" | custom-call | flops 100000000 | bytes 524288 | tf_op jit(solution)/shard_map/pallas_call | solution.py:413
  (6 shorter events, 0.0 us)
Async XLA Ops:
  0.8 9.6 %collective-permute-start.3 = (bf16[192,128]{1,0:T(8,128)(2,1)S(1)}, bf16[192,128]{1,0:T(8,128)(2,1)S(1)}, u32[]{:S(2)}, u32[]{:S(2)}) collective-permute-start(bf16[192,128]{1,0:T(8,128)(2,1)S(1)} %pad_maximum_fusion.refs_0_.refs_4_), channel_id=1, source_target_pairs={{0,1},{1,0},{2,3},{3,2},{4,5},{5,4},{6,7},{7,6},{8,9},{9,8},{10,11... | collective-permute-start | bytes 147464 | tf_op jit(solution)/shard_map/ppermute | solution.py:353
  1.3 9.1 %collective-permute-start.2 = (bf16[192,128]{1,0:T(8,128)(2,1)S(1)}, bf16[192,128]{1,0:T(8,128)(2,1)S(1)}, u32[]{:S(2)}, u32[]{:S(2)}) collective-permute-start(bf16[192,128]{1,0:T(8,128)(2,1)S(1)} %pad_maximum_fusion.refs_0_.refs_4_), channel_id=1, source_target_pairs={{0,6},{2,0},{4,2},{6,4},{1,7},{3,1},{5,3},{7,5},{8,14},{10,8},{12,... | collective-permute-start | bytes 147464 | tf_op jit(solution)/shard_map/ppermute | solution.py:353
  5.9 6.0 %collective-permute-start.1 = (bf16[192,128]{1,0:T(8,128)(2,1)S(1)}, bf16[192,128]{1,0:T(8,128)(2,1)S(1)}, u32[]{:S(2)}, u32[]{:S(2)}) collective-permute-start(bf16[192,128]{1,0:T(8,128)(2,1)S(1)} %pad_maximum_fusion.refs_0_.refs_4_), channel_id=1, source_target_pairs={{0,4},{2,6},{4,0},{6,2},{1,5},{3,7},{5,1},{7,3},{8,12},{10,14},{12... | collective-permute-start | bytes 147464 | tf_op jit(solution)/shard_map/ppermute | solution.py:353
  5.9 6.0 %collective-permute-start = (bf16[192,128]{1,0:T(8,128)(2,1)S(1)}, bf16[192,128]{1,0:T(8,128)(2,1)S(1)}, u32[]{:S(2)}, u32[]{:S(2)}) collective-permute-start(bf16[192,128]{1,0:T(8,128)(2,1)S(1)} %pad_maximum_fusion.refs_0_.refs_4_), channel_id=1, source_target_pairs={{0,2},{2,4},{4,6},{6,0},{1,3},{3,5},{5,7},{7,1},{8,10},{10,12},{12... | collective-permute-start | bytes 147464 | tf_op jit(solution)/shard_map/ppermute | solution.py:353
  14.0 2.9 %collective-permute-start.4 = (bf16[768,128]{1,0:T(8,128)(2,1)S(1)}, bf16[768,128]{1,0:T(8,128)(2,1)S(1)}, u32[]{:S(2)}, u32[]{:S(2)}) collective-permute-start(bf16[768,128]{1,0:T(8,128)(2,1)S(1)} %get-tuple-element.20.refs_0_), channel_id=1, source_target_pairs={{0,1},{1,0},{2,3},{3,2},{4,5},{5,4},{6,7},{7,6},{8,9},{9,8},{10,11... | collective-permute-start | bytes 589832 | tf_op jit(solution)/shard_map/ppermute | solution.py:353
  14.1 1.8 %collective-permute-start.6 = (f32[2,32,256]{2,1,0:T(8,128)S(1)}, f32[2,32,256]{2,1,0:T(8,128)S(1)}, u32[]{:S(2)}, u32[]{:S(2)}) collective-permute-start(f32[2,32,256]{2,1,0:T(8,128)S(1)} %bitcast.5), channel_id=1, source_target_pairs={{0,1},{1,0},{2,3},{3,2},{4,5},{5,4},{6,7},{7,6},{8,9},{9,8},{10,11... | collective-permute-start | bytes 196616 | tf_op jit(solution)/shard_map/ppermute | solution.py:353
  15.9 5.4 %collective-permute-start.7 = (f32[2,32,256]{2,1,0:T(8,128)S(1)}, f32[2,32,256]{2,1,0:T(8,128)S(1)}, u32[]{:S(2)}, u32[]{:S(2)}) collective-permute-start(f32[2,32,256]{2,1,0:T(8,128)S(1)} %add.10), channel_id=1, source_target_pairs={{0,2},{2,0},{4,6},{6,4},{1,3},{3,1},{5,7},{7,5},{8,10},{10,8},{12,... | collective-permute-start | bytes 196616 | tf_op jit(solution)/shard_map/ppermute | solution.py:375
  19.4 1.9 %collective-permute-start.5 = (f32[2,32,256]{2,1,0:T(8,128)S(1)}, f32[2,32,256]{2,1,0:T(8,128)S(1)}, u32[]{:S(2)}, u32[]{:S(2)}) collective-permute-start(f32[2,32,256]{2,1,0:T(8,128)S(1)} %bitcast.6), channel_id=1, source_target_pairs={{0,1},{1,0},{2,3},{3,2},{4,5},{5,4},{6,7},{7,6},{8,9},{9,8},{10,11... | collective-permute-start | bytes 196616 | tf_op jit(solution)/shard_map/ppermute | solution.py:353
  21.3 5.6 %collective-permute-start.8 = (f32[1,32,256]{2,1,0:T(8,128)S(1)}, f32[1,32,256]{2,1,0:T(8,128)S(1)}, u32[]{:S(2)}, u32[]{:S(2)}) collective-permute-start(f32[1,32,256]{2,1,0:T(8,128)S(1)} %get-tuple-element.27), channel_id=1, source_target_pairs={{0,4},{2,6},{4,0},{6,2},{1,5},{3,7},{5,1},{7,3},{8,12},{10,14},{12... | collective-permute-start | bytes 98312 | tf_op jit(solution)/shard_map/ppermute | solution.py:403

commit v9 on v7

--- a/solution.py
+++ b/solution.py
@@ -10,7 +10,6 @@
 
 ridge_weight = 0.1
 vmem = pl.BlockSpec(memory_space=pltpu.VMEM)
-smem = pl.BlockSpec(memory_space=pltpu.SMEM)
 hbm = pl.BlockSpec(memory_space=pltpu.HBM)
 
 
@@ -33,7 +32,12 @@
     return order
 
 
-def fetch_kernel(nj, nk, where, block, held, arrived):
+def place():
+    return lax.axis_index("ja"), lax.axis_index("ka")
+
+
+def fetch_kernel(nj, nk, block, held, arrived):
+    where = place()
     owned = held.shape[2]
     copies = []
     for t in range(nk):
@@ -47,20 +51,20 @@
         copy.wait()
 
 
-def fetch(where, tensor, nj, nk):
+def fetch(tensor, nj, nk):
     rows, width_j, width_k = tensor.shape
     owned = rows // (nj * nk)
     return pl.pallas_call(
         functools.partial(fetch_kernel, nj, nk),
         out_shape=jax.ShapeDtypeStruct((nk, nj, owned, width_j, width_k), tensor.dtype),
-        in_specs=[smem, hbm],
+        in_specs=[hbm],
         out_specs=vmem,
         scratch_shapes=[pltpu.SemaphoreType.DMA((nk, nj))],
         compiler_params=pltpu.CompilerParams(vmem_limit_bytes=42 * 2**20),
         cost_estimate=pl.CostEstimate(
             flops=4 * 10**9, bytes_accessed=2 * rows * width_j * width_k, transcendentals=0
         ),
-    )(where, tensor)
+    )(tensor)
 
 
 def contraction(held, out, c_wide, b_wide):
@@ -89,7 +93,8 @@
         piece()
 
 
-def away_kernel(nj, nk, height_b, flipped, where, held, *refs):
+def away_kernel(nj, nk, height_b, flipped, held, *refs):
+    where = place()
     line, refs = refs[:nj], refs[nj:]
     b_parts, refs = refs[:nk], refs[nk:]
     out, own, c_cols, b_cols, b_rows = refs
@@ -125,7 +130,7 @@
     )
 
 
-def contract_away(where, held, line, b_parts, height_b, flipped, rank):
+def contract_away(held, line, b_parts, height_b, flipped, rank):
     nk, nj, owned, width_j, width_k = held.shape
     width = line[0].shape[1]
     return pl.pallas_call(
@@ -136,12 +141,12 @@
             jax.ShapeDtypeStruct((width_k, rank), held.dtype),
             jax.ShapeDtypeStruct((width_j, rank), jnp.float32),
         ],
-        in_specs=[smem] + [vmem] * (1 + nj + nk),
+        in_specs=[vmem] * (1 + nj + nk),
         out_specs=[vmem] * 4,
         scratch_shapes=[pltpu.VMEM((rank, width_j) if flipped else (width_j, rank), held.dtype)],
         compiler_params=pltpu.CompilerParams(vmem_limit_bytes=20 * 2**20),
         cost_estimate=flops_of((nk - 1) * nj * owned // 2, held, rank),
-    )(where, held, *line, *b_parts)
+    )(held, *line, *b_parts)
 
 
 def contract_rows(turns, begin, count, held, c_cols, b_cols):
@@ -263,7 +268,8 @@
                 a[8 * g : 8 * g + 8, 128 * w : 128 * w + 128] = value
 
 
-def first_kernel(nj, nk, height_b, flipped, blocks, where, held, c_cols, b_cols, *refs):
+def first_kernel(nj, nk, height_b, flipped, blocks, held, c_cols, b_cols, *refs):
+    where = place()
     owns, (away, out, b_all) = refs[:nk], refs[nk:]
     rank = out.shape[1]
     pieces = []
@@ -324,7 +330,6 @@
 
 def update(tensor, factor_b, factor_c):
     nj, nk = lax.axis_size("ja"), lax.axis_size("ka")
-    where = jnp.stack([lax.axis_index("ja"), lax.axis_index("ka")]).astype(jnp.int32)
     rank = factor_b.shape[1] * nk
     flipped = factor_b.shape[1] % 128 != 0
     part_b = factor_b.T if flipped else factor_b
@@ -332,9 +337,9 @@
     mine = jnp.concatenate([part_b, factor_c.T], axis=0)
     line = [mine] + [send(mine, "ja", nj, s) for s in range(1, nj)]
     b_parts = [mine] + [send(mine, "ka", nk, t) for t in range(1, nk)]
-    held = fetch(where, tensor, nj, nk)
+    held = fetch(tensor, nj, nk)
     away, own, c_cols, b_cols = contract_away(
-        where, held, line, b_parts, height_b, flipped, rank
+        held, line, b_parts, height_b, flipped, rank
     )
     half = nj // 2
     turns = tuple(range(1, nk))
@@ -346,17 +351,17 @@
     params = pltpu.CompilerParams(vmem_limit_bytes=20 * 2**20)
     cost = pl.CostEstimate(flops=5 * 10**9, bytes_accessed=2**20, transcendentals=0)
     square = jax.ShapeDtypeStruct((rank, rank), jnp.float32)
-    first, middle = rank // 128 * 16, rank // 256 * 80
+    first, middle = rank // 128 * 16, rank // 256 * 96
     b_shape = (nj, rank, mine.shape[1]) if flipped else (nj, height_b, rank)
     away, started = pl.pallas_call(
         functools.partial(first_kernel, nj, nk, height_b, flipped, first),
         out_shape=[jax.ShapeDtypeStruct(away.shape, jnp.float32), square],
-        in_specs=[smem] + [vmem] * (3 + nk),
+        in_specs=[vmem] * (3 + nk),
         out_specs=[vmem] * 2,
         scratch_shapes=[pltpu.VMEM(b_shape, mine.dtype)],
         compiler_params=params,
         cost_estimate=cost,
-    )(where, held, c_cols, b_cols, *owns)
+    )(held, c_cols, b_cols, *owns)
     kept, half_done = pl.pallas_call(
         functools.partial(middle_kernel, first, middle),
         out_shape=[jax.ShapeDtypeStruct(sent.shape, jnp.float32), square],

time: 28.1 us -> 26.7 us (0.950)
  Pallas kernels: 15.5 us -> 13.7 us
  waiting for transfers between devices: 1.86 us -> 2.48 us
    ppermute x7, waiting for transfers between devices: 0.92 us -> 1.54 us  [send(): return lax.ppermute(x, axis, shift(n, s))]
    ppermute x1, starting transfers between devices: 1.66 us -> 1.04 us  [update(): received = lax.ppermute(sent, 'ja', [(i, i ^ 1) for i in range(nj)])]
    pallas_call x1, Pallas kernels: 2.43 us -> 1.83 us  [update(): pl.pallas_call(functools.partial(first_kernel, nj, nk, height_b, flipped,...]
    ppermute x1, starting transfers between devices: 0.98 us -> 1.55 us  [update(): received = lax.ppermute(sent, 'ja', [(i, i ^ bit) for i in range(nj)])]
    pallas_call x1, Pallas kernels: 4.02 us -> 3.47 us  [fetch(): pl.pallas_call(functools.partial(fetch_kernel, nj, nk), out_shape=jax.Sha...]
    pallas_call x1, Pallas kernels: 1.87 us -> 1.33 us  [contract_away(): pl.pallas_call(functools.partial(away_kernel, nj, nk, height_b, flipped),...]
    pallas_call x1, Pallas kernels: 3.4 us -> 3.09 us  [update(): pl.pallas_call(functools.partial(rest_kernel, middle), out_shape=square,...]
  transfers between devices with their start and end apart: 9 -> 9, of which waited for: 2 -> 2; matrix products, arithmetic and copies ran while one was open for 0% -> 0% of each run, Pallas kernels for 46% -> 43%
where the time goes in v9:
time: 26.7 us; the launch traced here: 26.5 us
  Pallas kernels  13.7 us (51%)
  starting transfers between devices  9.34 us (35%)
  waiting for transfers between devices  2.48 us (9%)
  other arithmetic  0.81 us (3%)
    ppermute x7, starting transfers between devices, send(): return lax.ppermute(x, axis, shift(n, s))  6.75 us
    pallas_call x1, Pallas kernels, fetch(): pl.pallas_call(functools.partial(fetch_kernel, nj, nk), out_shape=jax.Sha...  3.47 us
    pallas_call x1, Pallas kernels, update(): pl.pallas_call(functools.partial(rest_kernel, middle), out_shape=square,...  3.09 us
    pallas_call x1, Pallas kernels, update(): pl.pallas_call(functools.partial(middle_kernel, first, middle), out_shape...  1.87 us
    pallas_call x1, Pallas kernels, update(): pl.pallas_call(functools.partial(first_kernel, nj, nk, height_b, flipped,...  1.83 us
    ppermute x1, starting transfers between devices, update(): received = lax.ppermute(sent, 'ja', [(i, i ^ bit) for i in range(nj)])  1.55 us
    ppermute x7, waiting for transfers between devices, send(): return lax.ppermute(x, axis, shift(n, s))  1.54 us
    pallas_call x1, Pallas kernels, contract_away(): pl.pallas_call(functools.partial(away_kernel, nj, nk, height_b, flipped),...  1.33 us
  transfers between devices with their start and end apart: 9, of which 2 were waited for; matrix products, arithmetic and copies ran while one was open for 0% of the time, Pallas kernels for 43%

profile of v9, /device:TPU:0, one launch (start us, length us, event | category | flops | bytes accessed | tf_op | source)
XLA Modules:
  0.0 26.5 jit_solution(1528928596759605918)
XLA Ops:
  0.0 0.8 %pad_maximum_fusion.refs_0_.refs_4_ = bf16[192,128]{1,0:T(8,128)(2,1)S(1)} fusion(bf16[64,128]{1,0:T(8,128)(2,1)} %bitcast.7, bf16[128,128]{1,0:T(8,128)(2,1)} %param.4), kind=kLoop, calls=%fused_computation.2 | loop fusion | flops 98304 | bytes 98304 | tf_op jit(solution)/shard_map/concatenate | solution.py:337
  0.8 0.5 %collective-permute-start.3 = (bf16[192,128]{1,0:T(8,128)(2,1)S(1)}, bf16[192,128]{1,0:T(8,128)(2,1)S(1)}, u32[]{:S(2)}, u32[]{:S(2)}) collective-permute-start(bf16[192,128]{1,0:T(8,128)(2,1)S(1)} %pad_maximum_fusion.refs_0_.refs_4_), channel_id=1, source_target_pairs={{0,1},{1,0},{2,3},{3,2},{4,5},{5,4},{6,7},{7,6},{8,9},{9,8},{10,11... | collective-permute-start | bytes 147464 | tf_op jit(solution)/shard_map/ppermute | solution.py:328
  1.3 4.6 %collective-permute-start.2 = (bf16[192,128]{1,0:T(8,128)(2,1)S(1)}, bf16[192,128]{1,0:T(8,128)(2,1)S(1)}, u32[]{:S(2)}, u32[]{:S(2)}) collective-permute-start(bf16[192,128]{1,0:T(8,128)(2,1)S(1)} %pad_maximum_fusion.refs_0_.refs_4_), channel_id=1, source_target_pairs={{0,6},{2,0},{4,2},{6,4},{1,7},{3,1},{5,3},{7,5},{8,14},{10,8},{12,... | collective-permute-start | bytes 147464 | tf_op jit(solution)/shard_map/ppermute | solution.py:328
  5.9 0.0 collective-permute-start.1
  5.9 1.0 %collective-permute-start = (bf16[192,128]{1,0:T(8,128)(2,1)S(1)}, bf16[192,128]{1,0:T(8,128)(2,1)S(1)}, u32[]{:S(2)}, u32[]{:S(2)}) collective-permute-start(bf16[192,128]{1,0:T(8,128)(2,1)S(1)} %pad_maximum_fusion.refs_0_.refs_4_), channel_id=1, source_target_pairs={{0,2},{2,4},{4,6},{6,0},{1,3},{3,5},{5,7},{7,1},{8,10},{10,12},{12... | collective-permute-start | bytes 147464 | tf_op jit(solution)/shard_map/ppermute | solution.py:328
  6.9 3.5 %shard_map.37.held = bf16[2,4,32,128,128]{4,3,2,1,0:T(8,128)(2,1)S(1)} custom-call(bf16[256,128,128]{2,1,0:T(8,128)(2,1)} %block.1), custom_call_target="tpu_custom_call" | custom-call | flops 4000000000 | bytes 8388608 | tf_op jit(solution)/shard_map/pallas_call | solution.py:57
  10.4 0.0 collective-permute-done.2.refs_3_
  10.4 1.5 %collective-permute-done.1.refs_2_ = bf16[192,128]{1,0:T(8,128)(2,1)S(1)} collective-permute-done((bf16[192,128]{1,0:T(8,128)(2,1)S(1)}, bf16[192,128]{1,0:T(8,128)(2,1)S(1)}, u32[]{:S(2)}, u32[]{:S(2)}) %collective-permute-start.1) | collective-permute-done | bytes 49184 | tf_op jit(solution)/shard_map/ppermute | solution.py:328
  11.9 0.0 collective-permute-done.refs_1_
  11.9 1.3 %shard_map.38 = (f32[1,2,32,256]{3,2,1,0:T(8,128)S(1)}, bf16[768,128]{1,0:T(8,128)(2,1)S(1)}, bf16[128,256]{1,0:T(8,128)(2,1)S(1)}, f32[128,256]{1,0:T(8,128)S(1)}) custom-call(bf16[2,4,32,128,128]{4,3,2,1,0:T(8,128)(2,1)S(1)} %shard_map.37.held, bf16[192,128]{1,0:T(8,128)(2,1)S(1)} %pad_maximum_fusion.refs_0_.refs_4_, ...), custom_call_target="tpu_custom_call" | custom-call | flops 536870912 | bytes 1048576 | tf_op jit(solution)/shard_map/pallas_call | solution.py:136
  13.3 0.1 collective-permute-start.6
  13.3 0.5 %collective-permute-start.4 = (bf16[768,128]{1,0:T(8,128)(2,1)S(1)}, bf16[768,128]{1,0:T(8,128)(2,1)S(1)}, u32[]{:S(2)}, u32[]{:S(2)}) collective-permute-start(bf16[768,128]{1,0:T(8,128)(2,1)S(1)} %get-tuple-element.15.refs_0_), channel_id=1, source_target_pairs={{0,1},{1,0},{2,3},{3,2},{4,5},{5,4},{6,7},{7,6},{8,9},{9,8},{10,11... | collective-permute-start | bytes 589832 | tf_op jit(solution)/shard_map/ppermute | solution.py:328
  13.8 1.2 %shard_map.41 = f32[1,2,32,256]{3,2,1,0:T(8,128)S(1)} custom-call(bf16[2,4,32,128,128]{4,3,2,1,0:T(8,128)(2,1)S(1)} %shard_map.37.held, bf16[128,256]{1,0:T(8,128)(2,1)S(1)} %get-tuple-element.13.c_cols, f32[128,256]{1,0:T(8,128)S(1)} %get-tuple-element.14.b_cols), custom_call_target="tpu_custom_call" | custom-call | flops 536870912 | bytes 1048576 | tf_op jit(solution)/shard_map/pallas_call | solution.py:154
  15.1 1.0 %collective-permute-start.7 = (f32[2,32,256]{2,1,0:T(8,128)S(1)}, f32[2,32,256]{2,1,0:T(8,128)S(1)}, u32[]{:S(2)}, u32[]{:S(2)}) collective-permute-start(f32[2,32,256]{2,1,0:T(8,128)S(1)} %bitcast_add_fusion), channel_id=1, source_target_pairs={{0,2},{2,0},{4,6},{6,4},{1,3},{3,1},{5,7},{7,5},{8,10},{10,8},{12,... | collective-permute-start | bytes 196616 | tf_op jit(solution)/shard_map/ppermute | solution.py:350
  16.2 0.0 collective-permute-done.4.refs_1_
  16.2 1.8 %shard_map.39 = (f32[1,2,32,256]{3,2,1,0:T(8,128)S(1)}, f32[256,256]{1,0:T(8,128)S(1)}) custom-call(bf16[2,4,32,128,128]{4,3,2,1,0:T(8,128)(2,1)S(1)} %shard_map.37.held, bf16[128,256]{1,0:T(8,128)(2,1)S(1)} %get-tuple-element.13.c_cols, f32[128,256]{1,0:T(8,128)S(1)} %get-tuple-element.14.b_cols, bf16[768,128]{1,0:T(8,128)(2,1)S(1)} %get-tuple-element.15.refs_0_, ...), custom_call_target="tpu_custom_call" | custom-call | flops 5000000000 | bytes 1048576 | tf_op jit(solution)/shard_map/pallas_call | solution.py:356
  18.0 0.1 collective-permute-start.5
  18.1 1.9 %shard_map.40 = (f32[2,32,256]{2,1,0:T(8,128)S(1)}, f32[256,256]{1,0:T(8,128)S(1)}) custom-call(bf16[2,4,32,128,128]{4,3,2,1,0:T(8,128)(2,1)S(1)} %shard_map.37.held, bf16[128,256]{1,0:T(8,128)(2,1)S(1)} %get-tuple-element.13.c_cols, f32[128,256]{1,0:T(8,128)S(1)} %get-tuple-element.14.b_cols, f32[256,256]{1,0:T(8,128)S(1)} %get-tuple-element.16.started), custom_call_target="tpu_custom_call" | custom-call | flops 5000000000 | bytes 1048576 | tf_op jit(solution)/shard_map/pallas_call | solution.py:365
  20.0 0.0 collective-permute-done.7
  20.0 0.0 collective-permute-done.5
  20.0 1.5 %collective-permute-start.8 = (f32[1,32,256]{2,1,0:T(8,128)S(1)}, f32[1,32,256]{2,1,0:T(8,128)S(1)}, u32[]{:S(2)}, u32[]{:S(2)}) collective-permute-start(f32[1,32,256]{2,1,0:T(8,128)S(1)} %get-tuple-element.21), channel_id=1, source_target_pairs={{0,4},{2,6},{4,0},{6,2},{1,5},{3,7},{5,1},{7,3},{8,12},{10,14},{12... | collective-permute-start | bytes 98312 | tf_op jit(solution)/shard_map/ppermute | solution.py:378
  21.6 3.1 %shard_map.42.inverse = f32[256,256]{1,0:T(8,128)S(1)} custom-call(f32[256,256]{1,0:T(8,128)S(1)} %get-tuple-element.20.half_done), custom_call_target="tpu_custom_call" | custom-call | flops 5000000000 | bytes 1048576 | tf_op jit(solution)/shard_map/pallas_call | solution.py:380
  24.7 0.9 %collective-permute-done.8.received = f32[1,32,256]{2,1,0:T(8,128)S(1)} collective-permute-done((f32[1,32,256]{2,1,0:T(8,128)S(1)}, f32[1,32,256]{2,1,0:T(8,128)S(1)}, u32[]{:S(2)}, u32[]{:S(2)}) %collective-permute-start.8) | collective-permute-done | bytes 32800 | tf_op jit(solution)/shard_map/ppermute | solution.py:378
  25.6 0.9 %shard_map.43 = f32[32,256]{1,0:T(8,128)} custom-call(f32[1,32,256]{2,1,0:T(8,128)S(1)} %get-tuple-element.22.kept, f32[1,32,256]{2,1,0:T(8,128)S(1)} %collective-permute-done.8.received, f32[256,256]{1,0:T(8,128)S(1)} %shard_map.42.inverse), custom_call_target="tpu_custom_call" | custom-call | flops 100000000 | bytes 524288 | tf_op jit(solution)/shard_map/pallas_call | solution.py:388
  (5 shorter events, 0.0 us)
Async XLA Ops:
  0.8 9.6 %collective-permute-start.3 = (bf16[192,128]{1,0:T(8,128)(2,1)S(1)}, bf16[192,128]{1,0:T(8,128)(2,1)S(1)}, u32[]{:S(2)}, u32[]{:S(2)}) collective-permute-start(bf16[192,128]{1,0:T(8,128)(2,1)S(1)} %pad_maximum_fusion.refs_0_.refs_4_), channel_id=1, source_target_pairs={{0,1},{1,0},{2,3},{3,2},{4,5},{5,4},{6,7},{7,6},{8,9},{9,8},{10,11... | collective-permute-start | bytes 147464 | tf_op jit(solution)/shard_map/ppermute | solution.py:328
  1.3 9.1 %collective-permute-start.2 = (bf16[192,128]{1,0:T(8,128)(2,1)S(1)}, bf16[192,128]{1,0:T(8,128)(2,1)S(1)}, u32[]{:S(2)}, u32[]{:S(2)}) collective-permute-start(bf16[192,128]{1,0:T(8,128)(2,1)S(1)} %pad_maximum_fusion.refs_0_.refs_4_), channel_id=1, source_target_pairs={{0,6},{2,0},{4,2},{6,4},{1,7},{3,1},{5,3},{7,5},{8,14},{10,8},{12,... | collective-permute-start | bytes 147464 | tf_op jit(solution)/shard_map/ppermute | solution.py:328
  5.9 6.0 %collective-permute-start.1 = (bf16[192,128]{1,0:T(8,128)(2,1)S(1)}, bf16[192,128]{1,0:T(8,128)(2,1)S(1)}, u32[]{:S(2)}, u32[]{:S(2)}) collective-permute-start(bf16[192,128]{1,0:T(8,128)(2,1)S(1)} %pad_maximum_fusion.refs_0_.refs_4_), channel_id=1, source_target_pairs={{0,4},{2,6},{4,0},{6,2},{1,5},{3,7},{5,1},{7,3},{8,12},{10,14},{12... | collective-permute-start | bytes 147464 | tf_op jit(solution)/shard_map/ppermute | solution.py:328
  5.9 6.0 %collective-permute-start = (bf16[192,128]{1,0:T(8,128)(2,1)S(1)}, bf16[192,128]{1,0:T(8,128)(2,1)S(1)}, u32[]{:S(2)}, u32[]{:S(2)}) collective-permute-start(bf16[192,128]{1,0:T(8,128)(2,1)S(1)} %pad_maximum_fusion.refs_0_.refs_4_), channel_id=1, source_target_pairs={{0,2},{2,4},{4,6},{6,0},{1,3},{3,5},{5,7},{7,1},{8,10},{10,12},{12... | collective-permute-start | bytes 147464 | tf_op jit(solution)/shard_map/ppermute | solution.py:328
  13.3 1.8 %collective-permute-start.6 = (f32[2,32,256]{2,1,0:T(8,128)S(1)}, f32[2,32,256]{2,1,0:T(8,128)S(1)}, u32[]{:S(2)}, u32[]{:S(2)}) collective-permute-start(f32[2,32,256]{2,1,0:T(8,128)S(1)} %bitcast.5), channel_id=1, source_target_pairs={{0,1},{1,0},{2,3},{3,2},{4,5},{5,4},{6,7},{7,6},{8,9},{9,8},{10,11... | collective-permute-start | bytes 196616 | tf_op jit(solution)/shard_map/ppermute | solution.py:328
  13.3 2.8 %collective-permute-start.4 = (bf16[768,128]{1,0:T(8,128)(2,1)S(1)}, bf16[768,128]{1,0:T(8,128)(2,1)S(1)}, u32[]{:S(2)}, u32[]{:S(2)}) collective-permute-start(bf16[768,128]{1,0:T(8,128)(2,1)S(1)} %get-tuple-element.15.refs_0_), channel_id=1, source_target_pairs={{0,1},{1,0},{2,3},{3,2},{4,5},{5,4},{6,7},{7,6},{8,9},{9,8},{10,11... | collective-permute-start | bytes 589832 | tf_op jit(solution)/shard_map/ppermute | solution.py:328
  15.1 4.8 %collective-permute-start.7 = (f32[2,32,256]{2,1,0:T(8,128)S(1)}, f32[2,32,256]{2,1,0:T(8,128)S(1)}, u32[]{:S(2)}, u32[]{:S(2)}) collective-permute-start(f32[2,32,256]{2,1,0:T(8,128)S(1)} %bitcast_add_fusion), channel_id=1, source_target_pairs={{0,2},{2,0},{4,6},{6,4},{1,3},{3,1},{5,7},{7,5},{8,10},{10,8},{12,... | collective-permute-start | bytes 196616 | tf_op jit(solution)/shard_map/ppermute | solution.py:350
  18.0 2.0 %collective-permute-start.5 = (f32[2,32,256]{2,1,0:T(8,128)S(1)}, f32[2,32,256]{2,1,0:T(8,128)S(1)}, u32[]{:S(2)}, u32[]{:S(2)}) collective-permute-start(f32[2,32,256]{2,1,0:T(8,128)S(1)} %bitcast.6), channel_id=1, source_target_pairs={{0,1},{1,0},{2,3},{3,2},{4,5},{5,4},{6,7},{7,6},{8,9},{9,8},{10,11... | collective-permute-start | bytes 196616 | tf_op jit(solution)/shard_map/ppermute | solution.py:328
  20.0 5.6 %collective-permute-start.8 = (f32[1,32,256]{2,1,0:T(8,128)S(1)}, f32[1,32,256]{2,1,0:T(8,128)S(1)}, u32[]{:S(2)}, u32[]{:S(2)}) collective-permute-start(f32[1,32,256]{2,1,0:T(8,128)S(1)} %get-tuple-element.21), channel_id=1, source_target_pairs={{0,4},{2,6},{4,0},{6,2},{1,5},{3,7},{5,1},{7,3},{8,12},{10,14},{12... | collective-permute-start | bytes 98312 | tf_op jit(solution)/shard_map/ppermute | solution.py:378
